TPU v7x, 512 devices: a whole 4x4x16 slice. The times are simulated.
512 devices in a mesh: role: 4 (over z_lo), tp: 4 (over x), dp: 32 (over y, z_hi, core).
Axes of the slice: x: 4, y: 4, z: 16 (z_hi: 4, z_lo: 4; z = z_hi * 4 + z_lo), core: 2. Of those that a mesh axis runs over, the one named last changes fastest.
Arguments:
- master: float32 [1024, 8192], P('tp', ('role', 'dp')), may hold values from -0.0625 to 0.0625
- key_bias: float32 [1024], P('tp'), may hold values from -3 to 3
- probe_tokens: bfloat16 [32768, 8192], P(('role', 'dp')), may hold values from -6 to 6
Outputs:
- weight: bfloat16 [8192, 1024], P(None, 'tp')
- probe_keys: bfloat16 [32768, 1024], P(('role', 'dp'), 'tp')
- checksum: float32 [8192], replicated
All inputs are finite; a program needn't handle non-finite values.
Results may differ from a plain program's by a relative error of at most 0.005.
Values may be sent and summed in bfloat16 or wider, within the bound.
No kernel may reach another device: no remote copies, remote signals or barrier semaphores. Data moves between devices by JAX's collectives and lax.ppermute only.
A program may use at most 64 MiB of HBM per device.

v0:
```python
import jax
import jax.numpy as jnp
from jax import lax
from jax.sharding import PartitionSpec as P


def copy_for_each(value, axis):
    copies = jnp.broadcast_to(value, (lax.axis_size(axis), *value.shape))
    return lax.all_to_all(copies, axis, split_axis=0, concat_axis=0, tiled=True)


def over_copies(value, axis):
    return copy_for_each(value, axis).sum(axis=0)


def body(master, key_bias, probe_tokens):
    own_rows = jnp.transpose(master).astype(jnp.bfloat16)
    replica_block = lax.all_gather(own_rows, "dp", axis=0, tiled=True)
    incoming = lax.all_gather(replica_block, "role", axis=0, tiled=True)
    totals = jnp.dot(probe_tokens, incoming, preferred_element_type=jnp.float32)
    probe_keys = (totals + key_bias[None, :]).astype(jnp.bfloat16)
    checksum = over_copies(jnp.sum(incoming.astype(jnp.float32), axis=1), "tp")
    return (incoming, probe_keys, checksum)


def solution(mesh):
    placed = (P("tp", ("role", "dp")), P("tp"), P(("role", "dp"), None))
    return jax.shard_map(
        body,
        mesh=mesh,
        in_specs=placed,
        out_specs=(P(None, "tp"), P(("role", "dp"), "tp"), P()),
        check_vma=False,
    )
```

profile of v0, /device:TPU:6, one launch (start us, length us, event | category | flops | bytes accessed | tf_op | source)
XLA Modules:
  0.0 199.0 jit_solution(13851942847966646415)
XLA Ops:
  7.2 0.0 copy-start
  7.2 0.0 all-gather.3.cloned.1.call-start
  7.2 1.5 convert_bitcast_fusion
  8.7 0.0 all-gather.3.cloned.1.call-update
  8.7 0.0 all-gather.5.cloned.1.call-start
  8.8 79.1 %all-gather.3.cloned.1.call-done = bf16[2048,256]{1,0:T(8,128)(2,1)} async-done(((bf16[64,256]{1,0:T(8,128)(2,1)}), bf16[2048,256]{1,0:T(8,128)(2,1)}) %all-gather.3.cloned.1.call-update) | async-done | bytes 1048592 | tf_op jit(solution)/shard_map/all_gather | solution.py:18
  87.9 0.0 all-gather.5.cloned.1.call-update
  87.9 84.8 %all-gather.5.cloned.1.call-done = bf16[8192,256]{1,0:T(8,128)(2,1)} async-done(((bf16[2048,256]{1,0:T(8,128)(2,1)}), bf16[8192,256]{1,0:T(8,128)(2,1)}) %all-gather.5.cloned.1.call-update) | async-done | bytes 4194320 | tf_op jit(solution)/shard_map/all_gather | solution.py:19
  172.7 3.3 %convert_reduce_fusion = f32[8192]{0:T(1024)S(1)} fusion(bf16[8192,256]{1,0:T(8,128)(2,1)} %all-gather.5.cloned.1.call-done), kind=kLoop, calls=%fused_computation | loop fusion | flops 4186112 | bytes 4227072 | tf_op jit(solution)/shard_map/reduce_sum | solution.py:22
  176.0 0.7 broadcast_in_dim.4
  176.7 4.8 %all-to-all-start = ((f32[4,1,8192]{2,1,0:T(1,128)}), f32[4,1,8192]{2,1,0:T(1,128)S(1)}, u32[]{:S(2)}, u32[]{:S(2)}) async-start(f32[4,1,8192]{2,1,0:T(1,128)} %broadcast_in_dim.4), calls=%async_computation | async-start | bytes 262144 | tf_op jit(solution)/shard_map/all_to_all | solution.py:9
  181.5 0.0 copy-done
  181.5 5.4 %fusion = bf16[256,256]{1,0:T(8,128)(2,1)} fusion(bf16[256,8192]{1,0:T(8,128)(2,1)} %param.5, bf16[8192,256]{1,0:T(8,128)(2,1)} %all-gather.5.cloned.1.call-done, f32[256]{0:T(256)S(1)} %copy-done), kind=kOutput, calls=%fused_computation.2 | convolution fusion | flops 1073872896 | bytes 8520704 | tf_op jit(solution)/shard_map/dot_general | solution.py:20
  186.9 0.0 all-to-all-done
  186.9 0.7 reduce_sum.19
  187.7 4.5 %copy.9 = bf16[8192,256]{1,0:T(8,128)(2,1)} copy(bf16[8192,256]{1,0:T(8,128)(2,1)} %all-gather.5.cloned.1.call-done) | data formatting | bytes 8388608
Async XLA Ops:
  7.2 174.4 %copy-start = (f32[256]{0:T(256)S(1)}, f32[256]{0:T(256)}, u32[]{:S(2)}) copy-start(f32[256]{0:T(256)} %param.4) | copy-start | bytes 3076
  7.2 80.7 %all-gather.3.cloned.1.call-start = ((), (), s32[]{:S(2)}) async-start(), calls=%async_computation.1 | async-start | bytes 1081344 | tf_op jit(solution)/shard_map/all_gather | solution.py:18
  8.7 164.0 %all-gather.5.cloned.1.call-start = ((), (), s32[]{:S(2)}) async-start(), calls=%async_computation.2 | async-start | bytes 5242880 | tf_op jit(solution)/shard_map/all_gather | solution.py:19
  176.7 10.2 %all-to-all-start = ((f32[4,1,8192]{2,1,0:T(1,128)}), f32[4,1,8192]{2,1,0:T(1,128)S(1)}, u32[]{:S(2)}, u32[]{:S(2)}) async-start(f32[4,1,8192]{2,1,0:T(1,128)} %broadcast_in_dim.4), calls=%async_computation | async-start | bytes 262144 | tf_op jit(solution)/shard_map/all_to_all | solution.py:9
Sparse Core Ops, SparseCore 0:
  11.7 76.1 all-gather.2
  90.0 82.6 all-gather.4
where the time goes:
time: 199 us
  waiting for transfers between devices  164 us (82%)
  between operations  14.1 us (7%)
  other arithmetic  5.54 us (3%)
  matrix products  5.37 us (3%)
  local copies, waits for them, and re-layouts  5.2 us (3%)
  starting transfers between devices  4.87 us (2%)
    all_gather x1, waiting for transfers between devices, body(): incoming = lax.all_gather(replica_block, 'role', axis=0, tiled=True)  84.8 us
    all_gather x1, waiting for transfers between devices, body(): replica_block = lax.all_gather(own_rows, 'dp', axis=0, tiled=True)  79.1 us
    dot_general x1, matrix products, body(): totals = jnp.dot(probe_tokens, incoming, preferred_element_type=jnp.float32)  5.37 us
    all_to_all x1, starting transfers between devices, copy_for_each(): return lax.all_to_all(copies, axis, split_axis=0, concat_axis=0, tiled=True)  4.79 us
    unnamed x3, local copies, waits for them, and re-layouts  4.47 us
  transfers between devices with their start and end apart: 3, of which 2 were waited for; matrix products, arithmetic and copies ran while one was open for 3% of the time, Pallas kernels for 0%

commit v1 on v0

v1 whole, which is shorter than its diff:
```python
import itertools

import jax
import jax.numpy as jnp
from jax import lax
from jax.sharding import PartitionSpec as P

SIZES = {"y": 4, "z": 16, "core": 2}


def index_of(x, y, z, core):
    return ((z % 4) * 4 + x) * 32 + (y * 4 + z // 4) * 2 + core


PLANES = [
    [index_of(x, y, z, core) for y, z, core in itertools.product(range(4), range(16), range(2))]
    for x in range(4)
]


def over_copies(value, axis):
    copies = jnp.broadcast_to(value, (lax.axis_size(axis), *value.shape))
    return lax.all_to_all(copies, axis, split_axis=0, concat_axis=0, tiled=True).sum(axis=0)


def body(master, key_bias, probe_tokens):
    own_rows = jnp.transpose(master).astype(jnp.bfloat16)
    rows, heads = own_rows.shape
    plane = lax.all_gather(
        own_rows, ("role", "tp", "dp"), axis=0, tiled=True, axis_index_groups=PLANES
    )
    incoming = plane.reshape(4, 4, 4, 2 * rows, heads).transpose(2, 0, 1, 3, 4).reshape(-1, heads)
    totals = jnp.dot(probe_tokens, incoming, preferred_element_type=jnp.float32)
    probe_keys = (totals + key_bias[None, :]).astype(jnp.bfloat16)
    checksum = over_copies(jnp.sum(incoming.astype(jnp.float32), axis=1), "tp")
    return (incoming, probe_keys, checksum)


def solution(mesh):
    placed = (P("tp", ("role", "dp")), P("tp"), P(("role", "dp"), None))
    return jax.shard_map(
        body,
        mesh=mesh,
        in_specs=placed,
        out_specs=(P(None, "tp"), P(("role", "dp"), "tp"), P()),
        check_vma=False,
    )
```

time: 199 us -> 183 us (0.920)
  waiting for transfers between devices: 164 us -> 150 us
  local copies, waits for them, and re-layouts: 5.2 us -> 3 us
    all_gather x2 -> x1, waiting for transfers between devices: 164 us -> 150 us  [body(): lax.all_gather(own_rows, ('role', 'tp', 'dp'), axis=0, tiled=True, axis_i...]
    unnamed x3 -> x4, local copies, waits for them, and re-layouts: 4.47 us -> 0.01 us
    reshape x0 -> x1, local copies, waits for them, and re-layouts: none -> 2.29 us  [body(): plane.reshape(4, 4, 4, 2 * rows, heads).transpose(2, 0, 1, 3, 4)]
  transfers between devices with their start and end apart: 3 -> 2, of which waited for: 2 -> 1; matrix products, arithmetic and copies ran while one was open for 3% -> 3% of each run, Pallas kernels for 0% -> 0%
where the time goes in v1:
time: 183 us
  waiting for transfers between devices  150 us (82%)
  between operations  14.1 us (8%)
  other arithmetic  5.7 us (3%)
  matrix products  5.37 us (3%)
  starting transfers between devices  4.83 us (3%)
  local copies, waits for them, and re-layouts  3 us (2%)
    all_gather x1, waiting for transfers between devices, body(): lax.all_gather(own_rows, ('role', 'tp', 'dp'), axis=0, tiled=True, axis_i...  150 us
    dot_general x1, matrix products, body(): totals = jnp.dot(probe_tokens, incoming, preferred_element_type=jnp.float32)  5.37 us
    all_to_all x1, starting transfers between devices, over_copies(): lax.all_to_all(copies, axis, split_axis=0, concat_axis=0, tiled=True)  4.79 us
  transfers between devices with their start and end apart: 2, of which 1 were waited for; matrix products, arithmetic and copies ran while one was open for 3% of the time, Pallas kernels for 0%

profile of v1, /device:TPU:6, one launch (start us, length us, event | category | flops | bytes accessed | tf_op | source)
XLA Modules:
  0.0 182.5 jit_solution(14234205316903624458)
XLA Ops:
  7.2 0.0 all-gather.2.cloned.1.call-start
  7.2 1.5 convert_bitcast_fusion
  8.7 0.0 all-gather.2.cloned.1.call-update
  8.7 149.6 %all-gather.2.cloned.1.call-done = bf16[8192,256]{1,0:T(8,128)(2,1)} async-done(((bf16[64,256]{1,0:T(8,128)(2,1)}), bf16[8192,256]{1,0:T(8,128)(2,1)}) %all-gather.2.cloned.1.call-update) | async-done | bytes 4194320 | tf_op jit(solution)/shard_map/all_gather | solution.py:29
  158.3 0.0 copy-start
  158.3 3.5 %convert_reduce_fusion = f32[4,4,4,128]{3,2,1,0:T(4,128)S(1)} fusion(bf16[4,4,4,128,256]{4,3,2,1,0:T(8,128)(2,1)} %bitcast.10), kind=kLoop, calls=%fused_computation | loop fusion | flops 4186112 | bytes 4227072 | tf_op jit(solution)/shard_map/reduce_sum | solution.py:35
  161.8 0.0 copy-done
  161.8 0.0 copy-start.1
  161.8 2.3 %copy.8 = bf16[4,4,4,128,256]{4,3,1,0,2:T(8,128)(2,1)} copy(bf16[4,4,4,128,256]{4,3,2,1,0:T(8,128)(2,1)S(1)} %bitcast.11) | data formatting | bytes 8388608 | tf_op jit(solution)/shard_map/reshape | solution.py:32
  164.1 0.7 broadcast_in_dim.7
  164.8 4.8 %all-to-all-start = ((f32[4,1,8192]{2,1,0:T(1,128)}), f32[4,1,8192]{2,1,0:T(1,128)S(1)}, u32[]{:S(2)}, u32[]{:S(2)}) async-start(f32[4,1,8192]{2,1,0:T(1,128)} %broadcast_in_dim.7), calls=%async_computation | async-start | bytes 262144 | tf_op jit(solution)/shard_map/all_to_all | solution.py:23
  169.6 0.0 copy-done.1
  169.6 5.4 %fusion = bf16[256,256]{1,0:T(8,128)(2,1)} fusion(bf16[256,8192]{1,0:T(8,128)(2,1)} %param.5, bf16[8192,256]{1,0:T(8,128)(2,1)} %bitcast.12, f32[256]{0:T(256)S(1)} %copy-done.1), kind=kOutput, calls=%fused_computation.2 | convolution fusion | flops 1073872896 | bytes 8520704 | tf_op jit(solution)/shard_map/dot_general | solution.py:33
  175.0 0.0 all-to-all-done
  175.0 0.7 reduce_sum.19
Async XLA Ops:
  7.2 151.1 %all-gather.2.cloned.1.call-start = ((), (), s32[]{:S(2)}) async-start(), calls=%async_computation.1 | async-start | bytes 4227072 | tf_op jit(solution)/shard_map/all_gather | solution.py:29
  158.3 3.5 %copy-start = (bf16[8192,256]{1,0:T(8,128)(2,1)S(1)}, bf16[8192,256]{1,0:T(8,128)(2,1)}, u32[]{:S(2)}) copy-start(bf16[8192,256]{1,0:T(8,128)(2,1)} %all-gather.2.cloned.1.call-done) | copy-start | bytes 12582916
  161.8 7.8 %copy-start.1 = (f32[256]{0:T(256)S(1)}, f32[256]{0:T(256)}, u32[]{:S(2)}) copy-start(f32[256]{0:T(256)} %param.4) | copy-start | bytes 3076
  164.8 10.2 %all-to-all-start = ((f32[4,1,8192]{2,1,0:T(1,128)}), f32[4,1,8192]{2,1,0:T(1,128)S(1)}, u32[]{:S(2)}, u32[]{:S(2)}) async-start(f32[4,1,8192]{2,1,0:T(1,128)} %broadcast_in_dim.7), calls=%async_computation | async-start | bytes 262144 | tf_op jit(solution)/shard_map/all_to_all | solution.py:23
Sparse Core Ops, SparseCore 0:
  11.7 146.5 all-gather.1

commit v2 on v0

v2 whole, which is shorter than its diff:
```python
import functools
import itertools

import jax
import jax.numpy as jnp
from jax import lax
from jax.experimental import pallas as pl
from jax.experimental.pallas import tpu as pltpu
from jax.sharding import PartitionSpec as P


AXES = ("role", "tp", "dp")
NX, NY, NZ, NC, LO = 4, 4, 16, 2, 4
HI = NZ // LO
LANES = 128
SAME, BACK, AHEAD, FAR = range(4)
CORE = 4


def index_of(x, y, z, core):
    y, z, core = y % NY, z % NZ, core % NC
    return ((z % LO) * NX + x) * (NY * HI * NC) + (y * HI + z // LO) * NC + core


CHIPS = list(itertools.product(range(NX), range(NY), range(NZ), range(NC)))
Z_RINGS = [
    [index_of(x, y, z, c) for z in range(NZ)]
    for x, y, c in itertools.product(range(NX), range(NY), range(NC))
]


ONWARD = [(index_of(x, y, z, c), index_of(x, y + 2 * c - 1, z, c)) for x, y, z, c in CHIPS]
SWAP = [(index_of(x, y, z, c), index_of(x, y, z, c + 1)) for x, y, z, c in CHIPS]


def onward(value):
    return lax.ppermute(value, AXES, ONWARD)


def swap(value):
    return lax.ppermute(value, AXES, SWAP)


def row_of(place, which, lo, span):
    return pl.multiple_of((lo * NY + place[which]) * span, span)


def fetch(place, which, probes, cols, sem):
    span = cols.shape[-1]
    gets = []
    for lo in range(LO):
        get = pltpu.make_async_copy(
            probes.at[:, pl.ds(row_of(place, which, lo, span), span)], cols.at[lo], sem.at[lo]
        )
        get.start()
        gets.append(get)
    return gets


def assemble(place, own, other, block, rows):
    for side, piece in enumerate((own, other)):
        core = place[CORE] if side == 0 else 1 - place[CORE]
        for z in range(NZ):
            into = pl.multiple_of(((z // LO) * NC + core) * rows, rows)
            block[z % LO, pl.ds(into, rows), :] = piece[pl.ds(z * rows, rows), :]


def row_sums(block):
    ones = jnp.ones((8, block.shape[-1]), block.dtype)
    return [
        lax.dot_general(
            ones, block[lo], (((1,), (1,)), ((), ())), preferred_element_type=jnp.float32
        )
        for lo in range(LO)
    ]


def step_kernel(which, rows, first, place, own, other, probes, *refs):
    if first:
        weight, total, sums, block, cols, put_sem, get_sem = refs
    else:
        total_in, _, weight, total, sums, block, cols, put_sem, get_sem = refs
    span = HI * NC * rows
    gets = fetch(place, which, probes, cols, get_sem)
    puts = []
    for side, piece in enumerate((own, other)):
        core = place[CORE] if side == 0 else 1 - place[CORE]
        for z in range(NZ):
            at = row_of(place, which, z % LO, span) + ((z // LO) * NC + core) * rows
            put = pltpu.make_async_copy(
                piece.at[pl.ds(z * rows, rows)],
                weight.at[pl.ds(pl.multiple_of(at, rows), rows)],
                put_sem,
            )
            put.start()
            puts.append(put)
    assemble(place, own, other, block, rows)
    for lo, s in enumerate(row_sums(block)):
        for j in range(span // LANES):
            sums[lo * (span // LANES) + j, :] = s[0, j * LANES : (j + 1) * LANES]
    acc = jnp.zeros(total.shape, total.dtype) if first else total_in[...]
    for lo in range(LO):
        gets[lo].wait()
        acc += jnp.dot(cols[lo], block[lo], preferred_element_type=jnp.float32)
    total[...] = acc
    for put in puts:
        put.wait()


def sums_kernel(rows, place, own, other, same, back, ahead, block, sums):
    span = HI * NC * rows
    lines = span // LANES
    assemble(place, own, other, block, rows)
    for which, ref in ((SAME, same), (BACK, back), (AHEAD, ahead)):
        for lo in range(LO):
            at = (lo * NY + place[which]) * lines
            for x in range(NX):
                sums[x, pl.ds(at, lines), :] = ref[lo * lines : (lo + 1) * lines, :]
    for lo, s in enumerate(row_sums(block)):
        at = (lo * NY + place[FAR]) * lines
        for x in range(NX):
            for j in range(lines):
                sums[x, pl.ds(at + j, 1), :] = s[0:1, j * LANES : (j + 1) * LANES]


def last_kernel(place, block, probes, total_in, bias, _, weight, keys, cols, put_sem, get_sem):
    span = block.shape[1]
    gets = fetch(place, FAR, probes, cols, get_sem)
    puts = []
    for lo in range(LO):
        put = pltpu.make_async_copy(
            block.at[lo], weight.at[pl.ds(row_of(place, FAR, lo, span), span)], put_sem.at[lo]
        )
        put.start()
        puts.append(put)
    acc = total_in[...] + bias[...]
    for lo in range(LO):
        gets[lo].wait()
        acc += jnp.dot(cols[lo], block[lo], preferred_element_type=jnp.float32)
    keys[...] = acc.astype(keys.dtype)
    for put in puts:
        put.wait()


VMEM = pl.BlockSpec(memory_space=pltpu.VMEM)
SMEM = pl.BlockSpec(memory_space=pltpu.SMEM)
HBM = pl.BlockSpec(memory_space=pltpu.HBM)
LIMIT = pltpu.CompilerParams(vmem_limit_bytes=50 << 20)


def sizes(piece, probes):
    rows = piece.shape[0] // NZ
    return rows, HI * NC * rows, piece.shape[1], probes.shape[0], probes.shape[1]


def cost(flops, moved):
    return pl.CostEstimate(flops=flops, bytes_accessed=moved, transcendentals=0)


def step(place, which, own, other, probes, carried=None):
    rows, span, heads, tokens, width = sizes(own, probes)
    first = carried is None
    return pl.pallas_call(
        functools.partial(step_kernel, which, rows, first),
        out_shape=(
            jax.ShapeDtypeStruct((width, heads), jnp.bfloat16),
            jax.ShapeDtypeStruct((tokens, heads), jnp.float32),
            jax.ShapeDtypeStruct((LO * span // LANES, LANES), jnp.float32),
        ),
        in_specs=[SMEM, VMEM, VMEM, HBM] + ([] if first else [VMEM, HBM]),
        out_specs=(HBM, VMEM, VMEM),
        scratch_shapes=[
            pltpu.VMEM((LO, span, heads), jnp.bfloat16),
            pltpu.VMEM((LO, tokens, span), jnp.bfloat16),
            pltpu.SemaphoreType.DMA,
            pltpu.SemaphoreType.DMA((LO,)),
        ],
        input_output_aliases={} if first else {5: 0},
        compiler_params=LIMIT,
        cost_estimate=cost(2 * LO * span * heads * tokens, 2 * LO * span * (heads + tokens)),
    )(place, own, other, probes, *(() if first else (carried[1], carried[0])))


def all_sums(place, own, other, probes, before):
    rows, span, heads, _, width = sizes(own, probes)
    return pl.pallas_call(
        functools.partial(sums_kernel, rows),
        out_shape=(
            jax.ShapeDtypeStruct((LO, span, heads), jnp.bfloat16),
            jax.ShapeDtypeStruct((NX, width // LANES, LANES), jnp.float32),
        ),
        in_specs=[SMEM] + [VMEM] * 5,
        out_specs=(VMEM, VMEM),
        compiler_params=LIMIT,
        cost_estimate=cost(2 * LO * span * heads * 8, 4 * LO * span * heads),
    )(place, own, other, *before)


def last(place, block, probes, carried, bias):
    _, span, heads = block.shape
    tokens, width = probes.shape
    return pl.pallas_call(
        last_kernel,
        out_shape=(
            jax.ShapeDtypeStruct((width, heads), jnp.bfloat16),
            jax.ShapeDtypeStruct((tokens, heads), jnp.bfloat16),
        ),
        in_specs=[SMEM, VMEM, HBM, VMEM, VMEM, HBM],
        out_specs=(HBM, VMEM),
        scratch_shapes=[
            pltpu.VMEM((LO, tokens, span), jnp.bfloat16),
            pltpu.SemaphoreType.DMA((LO,)),
            pltpu.SemaphoreType.DMA((LO,)),
        ],
        input_output_aliases={5: 0},
        compiler_params=LIMIT,
        cost_estimate=cost(2 * LO * span * heads * tokens, 2 * LO * span * (heads + tokens)),
    )(place, block, probes, carried[1], bias.reshape(1, -1), carried[0])


def body(master, key_bias, probe_tokens):
    dp = lax.axis_index("dp")
    core = lax.rem(dp, NC)
    y = lax.div(dp, HI * NC)
    back = lax.rem(y + 1 + 2 * core, NY)
    place = jnp.stack([y, back, lax.rem(back + 2, NY), lax.rem(y + 2, NY), core])

    own_rows = jnp.transpose(master).astype(jnp.bfloat16)
    mine = lax.all_gather(own_rows, AXES, axis=0, tiled=True, axis_index_groups=Z_RINGS)
    back_same = onward(mine)
    mine_other = swap(mine)
    back_other = onward(mine_other)
    far_same = onward(back_same)
    ahead_other = swap(back_same)
    ahead_same = swap(back_other)
    far_other = swap(far_same)

    s0 = step(place, SAME, mine, mine_other, probe_tokens)
    s1 = step(place, BACK, back_same, back_other, probe_tokens, s0)
    s2 = step(place, AHEAD, ahead_same, ahead_other, probe_tokens, s1)
    block, sums = all_sums(
        place, far_same, far_other, probe_tokens, (s0[2], s1[2], s2[2])
    )
    gathered = lax.all_to_all(sums, "tp", split_axis=0, concat_axis=0, tiled=True)
    weight, probe_keys = last(place, block, probe_tokens, s2, key_bias)
    checksum = gathered.sum(axis=0).reshape(-1)
    return (weight, probe_keys, checksum)


def solution(mesh):
    placed = (P("tp", ("role", "dp")), P("tp"), P(("role", "dp"), None))
    return jax.shard_map(
        body,
        mesh=mesh,
        in_specs=placed,
        out_specs=(P(None, "tp"), P(("role", "dp"), "tp"), P()),
        check_vma=False,
    )
```

time: 199 us -> 91.7 us (0.46)
  the two profiles are of different devices: /device:TPU:6 before, /device:TPU:24 now
where the time goes in v2:
time: 91.7 us; the launch traced here: 91 us
  blocking collectives  38.5 us (42%)
  starting transfers between devices  18.9 us (21%)
  waiting for transfers between devices  15.5 us (17%)
  Pallas kernels  13.9 us (15%)
  local copies, waits for them, and re-layouts  1.92 us (2%)
  other arithmetic  1.47 us (2%)
    all_gather x1, blocking collectives, body(): lax.all_gather(own_rows, AXES, axis=0, tiled=True, axis_index_groups=Z_RI...  38.5 us
    ppermute x3, waiting for transfers between devices, onward(): return lax.ppermute(value, AXES, ONWARD)  13 us
    pallas_call x3, Pallas kernels, step(): pl.pallas_call(functools.partial(step_kernel, which, rows, first), out_sh...  8.32 us
    ppermute x4, starting transfers between devices, swap(): return lax.ppermute(value, AXES, SWAP)  7.65 us
    ppermute x3, starting transfers between devices, onward(): return lax.ppermute(value, AXES, ONWARD)  6.92 us
    all_to_all x1, starting transfers between devices, body(): lax.all_to_all(sums, 'tp', split_axis=0, concat_axis=0, tiled=True)  4.29 us
    pallas_call x1, Pallas kernels, last(): pl.pallas_call(last_kernel, out_shape=(jax.ShapeDtypeStruct((width, heads...  3.4 us
    all_to_all x1, waiting for transfers between devices, body(): lax.all_to_all(sums, 'tp', split_axis=0, concat_axis=0, tiled=True)  2.57 us
  transfers between devices with their start and end apart: 8, of which 4 were waited for; matrix products, arithmetic and copies ran while one was open for 0% of the time, Pallas kernels for 13%

profile of v2, /device:TPU:24, one launch (start us, length us, event | category | flops | bytes accessed | tf_op | source)
XLA Modules:
  0.0 91.0 jit_solution(6179436455466581018)
XLA Ops:
  0.6 0.8 convert_bitcast_fusion
  1.5 38.5 %all_gather.3.own = bf16[1024,256]{1,0:T(8,128)(2,1)S(1)} all-gather(bf16[64,256]{1,0:T(8,128)(2,1)S(1)} %convert_bitcast_fusion), channel_id=1, replica_groups={{0,128,256,384,2,130,258,386,4,132,260,388,6,134,262,390},{1,129,257,38..., dimensions={0}, use_global_device_ids=true | all-gather | bytes 557056 | tf_op jit(solution)/shard_map/all_gather | solution.py:229
  40.0 1.9 %collective-permute-start.3 = (bf16[1024,256]{1,0:T(8,128)(2,1)S(1)}, bf16[1024,256]{1,0:T(8,128)(2,1)S(1)}, u32[]{:S(2)}, u32[]{:S(2)}) collective-permute-start(bf16[1024,256]{1,0:T(8,128)(2,1)S(1)} %all_gather.3.own), channel_id=1, source_target_pairs={{0,1},{1,0},{128,129},{129,128},{256,257},{257,256},{384,385},{385... | collective-permute-start | bytes 1572872 | tf_op jit(solution)/shard_map/ppermute | solution.py:41
  41.9 2.7 %collective-permute-start = (bf16[1024,256]{1,0:T(8,128)(2,1)S(1)}, bf16[1024,256]{1,0:T(8,128)(2,1)S(1)}, u32[]{:S(2)}, u32[]{:S(2)}) collective-permute-start(bf16[1024,256]{1,0:T(8,128)(2,1)S(1)} %all_gather.3.own), channel_id=1, source_target_pairs={{0,24},{1,9},{128,152},{129,137},{256,280},{257,265},{384,408},{38... | collective-permute-start | bytes 1572872 | tf_op jit(solution)/shard_map/ppermute | solution.py:37
  44.6 0.0 collective-permute-done.3.other
  44.6 2.4 %collective-permute-start.4 = (bf16[1024,256]{1,0:T(8,128)(2,1)S(1)}, bf16[1024,256]{1,0:T(8,128)(2,1)S(1)}, u32[]{:S(2)}, u32[]{:S(2)}) collective-permute-start(bf16[1024,256]{1,0:T(8,128)(2,1)S(1)} %collective-permute-done.3.other), channel_id=1, source_target_pairs={{0,24},{1,9},{128,152},{129,137},{256,280},{257,265},{384,408},{38... | collective-permute-start | bytes 1572872 | tf_op jit(solution)/shard_map/ppermute | solution.py:37
  46.9 0.0 copy-start
  47.0 0.8 copy-done
  47.7 6.5 %collective-permute-done.own = bf16[1024,256]{1,0:T(8,128)(2,1)S(1)} collective-permute-done((bf16[1024,256]{1,0:T(8,128)(2,1)S(1)}, bf16[1024,256]{1,0:T(8,128)(2,1)S(1)}, u32[]{:S(2)}, u32[]{:S(2)}) %collective-permute-start) | collective-permute-done | bytes 524320 | tf_op jit(solution)/shard_map/ppermute | solution.py:37
  54.2 1.9 %collective-permute-start.1 = (bf16[1024,256]{1,0:T(8,128)(2,1)S(1)}, bf16[1024,256]{1,0:T(8,128)(2,1)S(1)}, u32[]{:S(2)}, u32[]{:S(2)}) collective-permute-start(bf16[1024,256]{1,0:T(8,128)(2,1)S(1)} %collective-permute-done.own), channel_id=1, source_target_pairs={{0,24},{1,9},{128,152},{129,137},{256,280},{257,265},{384,408},{38... | collective-permute-start | bytes 1572872 | tf_op jit(solution)/shard_map/ppermute | solution.py:37
  56.1 1.9 %collective-permute-start.6 = (bf16[1024,256]{1,0:T(8,128)(2,1)S(1)}, bf16[1024,256]{1,0:T(8,128)(2,1)S(1)}, u32[]{:S(2)}, u32[]{:S(2)}) collective-permute-start(bf16[1024,256]{1,0:T(8,128)(2,1)S(1)} %collective-permute-done.own), channel_id=1, source_target_pairs={{0,1},{1,0},{128,129},{129,128},{256,257},{257,256},{384,385},{385... | collective-permute-start | bytes 1572872 | tf_op jit(solution)/shard_map/ppermute | solution.py:41
  58.0 1.8 %collective-permute-done.4.other = bf16[1024,256]{1,0:T(8,128)(2,1)S(1)} collective-permute-done((bf16[1024,256]{1,0:T(8,128)(2,1)S(1)}, bf16[1024,256]{1,0:T(8,128)(2,1)S(1)}, u32[]{:S(2)}, u32[]{:S(2)}) %collective-permute-start.4) | collective-permute-done | bytes 524320 | tf_op jit(solution)/shard_map/ppermute | solution.py:37
  59.8 1.9 %collective-permute-start.5 = (bf16[1024,256]{1,0:T(8,128)(2,1)S(1)}, bf16[1024,256]{1,0:T(8,128)(2,1)S(1)}, u32[]{:S(2)}, u32[]{:S(2)}) collective-permute-start(bf16[1024,256]{1,0:T(8,128)(2,1)S(1)} %collective-permute-done.4.other), channel_id=1, source_target_pairs={{0,1},{1,0},{128,129},{129,128},{256,257},{257,256},{384,385},{385... | collective-permute-start | bytes 1572872 | tf_op jit(solution)/shard_map/ppermute | solution.py:41
  61.7 4.7 %collective-permute-done.1.own = bf16[1024,256]{1,0:T(8,128)(2,1)S(1)} collective-permute-done((bf16[1024,256]{1,0:T(8,128)(2,1)S(1)}, bf16[1024,256]{1,0:T(8,128)(2,1)S(1)}, u32[]{:S(2)}, u32[]{:S(2)}) %collective-permute-start.1) | collective-permute-done | bytes 524320 | tf_op jit(solution)/shard_map/ppermute | solution.py:37
  66.5 1.9 %collective-permute-start.2 = (bf16[1024,256]{1,0:T(8,128)(2,1)S(1)}, bf16[1024,256]{1,0:T(8,128)(2,1)}, u32[]{:S(2)}, u32[]{:S(2)}) collective-permute-start(bf16[1024,256]{1,0:T(8,128)(2,1)S(1)} %collective-permute-done.1.own), channel_id=1, source_target_pairs={{0,1},{1,0},{128,129},{129,128},{256,257},{257,256},{384,385},{385... | collective-permute-start | bytes 1572872 | tf_op jit(solution)/shard_map/ppermute | solution.py:41
  68.4 0.1 stack.23.place
  68.5 0.0 copy-start.1
  68.5 1.0 %copy-done.1 = bf16[1024,256]{1,0:T(8,128)(2,1)S(1)} copy-done((bf16[1024,256]{1,0:T(8,128)(2,1)S(1)}, bf16[1024,256]{1,0:T(8,128)(2,1)}, u32[]{:S(2)}) %copy-start.1) | copy-done | bytes 524312
  69.5 2.8 %shard_map.58 = (bf16[8192,256]{1,0:T(8,128)(2,1)}, f32[256,256]{1,0:T(8,128)S(1)}, f32[16,128]{1,0:T(8,128)S(1)}) custom-call(s32[5]{0:T(128)S(1)} %stack.23.place, bf16[1024,256]{1,0:T(8,128)(2,1)S(1)} %all_gather.3.own, bf16[1024,256]{1,0:T(8,128)(2,1)S(1)} %copy-done.1, bf16[256,8192]{1,0:T(8,128)(2,1)} %probes.7), custom_call_target="tpu_custom_call" | custom-call | flops 268435456 | bytes 2097152 | tf_op jit(solution)/shard_map/pallas_call | solution.py:163
  72.4 2.7 %shard_map.59 = (bf16[8192,256]{1,0:T(8,128)(2,1)}, f32[256,256]{1,0:T(8,128)S(1)}, f32[16,128]{1,0:T(8,128)S(1)}) custom-call(s32[5]{0:T(128)S(1)} %stack.23.place, bf16[1024,256]{1,0:T(8,128)(2,1)S(1)} %collective-permute-done.own, bf16[1024,256]{1,0:T(8,128)(2,1)S(1)} %collective-permute-done.4.other, ...), custom_call_target="tpu_custom_call", output_to_operand_aliasing={{0}: (5, {})} | custom-call | flops 268435456 | bytes 2097152 | tf_op jit(solution)/shard_map/pallas_call | solution.py:163
  75.1 0.0 collective-permute-done.6.other
  75.2 0.0 collective-permute-done.5.own
  75.2 0.0 copy-start.2
  75.2 2.7 %shard_map.60 = (bf16[8192,256]{1,0:T(8,128)(2,1)}, f32[256,256]{1,0:T(8,128)S(1)}, f32[16,128]{1,0:T(8,128)S(1)}) custom-call(s32[5]{0:T(128)S(1)} %stack.23.place, bf16[1024,256]{1,0:T(8,128)(2,1)S(1)} %collective-permute-done.5.own, bf16[1024,256]{1,0:T(8,128)(2,1)S(1)} %collective-permute-done.6.other, ...), custom_call_target="tpu_custom_call", output_to_operand_aliasing={{0}: (5, {})} | custom-call | flops 268435456 | bytes 2097152 | tf_op jit(solution)/shard_map/pallas_call | solution.py:163
  77.9 0.0 collective-permute-done.2.other
  77.9 2.2 %shard_map.61 = (bf16[4,512,256]{2,1,0:T(8,128)(2,1)S(1)}, f32[4,64,128]{2,1,0:T(8,128)}) custom-call(s32[5]{0:T(128)S(1)} %stack.23.place, bf16[1024,256]{1,0:T(8,128)(2,1)S(1)} %collective-permute-done.1.own, bf16[1024,256]{1,0:T(8,128)(2,1)} %collective-permute-done.2.other, f32[16,128]{1,0:T(8,128)S(1)} %get-tuple-element.16.same, ...), custom_call_target="tpu_custom_call" | custom-call | flops 8388608 | bytes 2097152 | tf_op jit(solution)/shard_map/pallas_call | solution.py:186
  80.1 4.3 %all-to-all-start = ((f32[4,64,128]{2,1,0:T(8,128)}), f32[4,64,128]{2,1,0:T(8,128)S(1)}, u32[]{:S(2)}, u32[]{:S(2)}) async-start(f32[4,64,128]{2,1,0:T(8,128)} %get-tuple-element.28), calls=%async_computation | async-start | bytes 262144 | tf_op jit(solution)/shard_map/all_to_all | solution.py:244
  84.4 0.0 copy-done.2
  84.4 3.4 %shard_map.62 = (bf16[8192,256]{1,0:T(8,128)(2,1)}, bf16[256,256]{1,0:T(8,128)(2,1)}) custom-call(s32[5]{0:T(128)S(1)} %stack.23.place, bf16[4,512,256]{2,1,0:T(8,128)(2,1)S(1)} %get-tuple-element.23.block, bf16[256,8192]{1,0:T(8,128)(2,1)} %probes.7, f32[256,256]{1,0:T(8,128)S(1)} %get-tuple-element.24.total_in, ...), custom_call_target="tpu_custom_call", output_to_operand_aliasing={{0}: (5, {})} | custom-call | flops 268435456 | bytes 2097152 | tf_op jit(solution)/shard_map/pallas_call | solution.py:202
  87.8 2.6 %all-to-all-done = f32[4,64,128]{2,1,0:T(8,128)S(1)} async-done(((f32[4,64,128]{2,1,0:T(8,128)}), f32[4,64,128]{2,1,0:T(8,128)S(1)}, u32[]{:S(2)}, u32[]{:S(2)}) %all-to-all-start) | async-done | bytes 131104 | tf_op jit(solution)/shard_map/all_to_all | solution.py:244
  90.4 0.6 reduce_sum.9
Async XLA Ops:
  40.0 4.6 %collective-permute-start.3 = (bf16[1024,256]{1,0:T(8,128)(2,1)S(1)}, bf16[1024,256]{1,0:T(8,128)(2,1)S(1)}, u32[]{:S(2)}, u32[]{:S(2)}) collective-permute-start(bf16[1024,256]{1,0:T(8,128)(2,1)S(1)} %all_gather.3.own), channel_id=1, source_target_pairs={{0,1},{1,0},{128,129},{129,128},{256,257},{257,256},{384,385},{385... | collective-permute-start | bytes 1572872 | tf_op jit(solution)/shard_map/ppermute | solution.py:41
  41.9 12.3 %collective-permute-start = (bf16[1024,256]{1,0:T(8,128)(2,1)S(1)}, bf16[1024,256]{1,0:T(8,128)(2,1)S(1)}, u32[]{:S(2)}, u32[]{:S(2)}) collective-permute-start(bf16[1024,256]{1,0:T(8,128)(2,1)S(1)} %all_gather.3.own), channel_id=1, source_target_pairs={{0,24},{1,9},{128,152},{129,137},{256,280},{257,265},{384,408},{38... | collective-permute-start | bytes 1572872 | tf_op jit(solution)/shard_map/ppermute | solution.py:37
  44.6 15.2 %collective-permute-start.4 = (bf16[1024,256]{1,0:T(8,128)(2,1)S(1)}, bf16[1024,256]{1,0:T(8,128)(2,1)S(1)}, u32[]{:S(2)}, u32[]{:S(2)}) collective-permute-start(bf16[1024,256]{1,0:T(8,128)(2,1)S(1)} %collective-permute-done.3.other), channel_id=1, source_target_pairs={{0,24},{1,9},{128,152},{129,137},{256,280},{257,265},{384,408},{38... | collective-permute-start | bytes 1572872 | tf_op jit(solution)/shard_map/ppermute | solution.py:37
  46.9 0.8 copy-start
  54.2 12.3 %collective-permute-start.1 = (bf16[1024,256]{1,0:T(8,128)(2,1)S(1)}, bf16[1024,256]{1,0:T(8,128)(2,1)S(1)}, u32[]{:S(2)}, u32[]{:S(2)}) collective-permute-start(bf16[1024,256]{1,0:T(8,128)(2,1)S(1)} %collective-permute-done.own), channel_id=1, source_target_pairs={{0,24},{1,9},{128,152},{129,137},{256,280},{257,265},{384,408},{38... | collective-permute-start | bytes 1572872 | tf_op jit(solution)/shard_map/ppermute | solution.py:37
  56.1 19.0 %collective-permute-start.6 = (bf16[1024,256]{1,0:T(8,128)(2,1)S(1)}, bf16[1024,256]{1,0:T(8,128)(2,1)S(1)}, u32[]{:S(2)}, u32[]{:S(2)}) collective-permute-start(bf16[1024,256]{1,0:T(8,128)(2,1)S(1)} %collective-permute-done.own), channel_id=1, source_target_pairs={{0,1},{1,0},{128,129},{129,128},{256,257},{257,256},{384,385},{385... | collective-permute-start | bytes 1572872 | tf_op jit(solution)/shard_map/ppermute | solution.py:41
  59.8 15.3 %collective-permute-start.5 = (bf16[1024,256]{1,0:T(8,128)(2,1)S(1)}, bf16[1024,256]{1,0:T(8,128)(2,1)S(1)}, u32[]{:S(2)}, u32[]{:S(2)}) collective-permute-start(bf16[1024,256]{1,0:T(8,128)(2,1)S(1)} %collective-permute-done.4.other), channel_id=1, source_target_pairs={{0,1},{1,0},{128,129},{129,128},{256,257},{257,256},{384,385},{385... | collective-permute-start | bytes 1572872 | tf_op jit(solution)/shard_map/ppermute | solution.py:41
  66.5 11.5 %collective-permute-start.2 = (bf16[1024,256]{1,0:T(8,128)(2,1)S(1)}, bf16[1024,256]{1,0:T(8,128)(2,1)}, u32[]{:S(2)}, u32[]{:S(2)}) collective-permute-start(bf16[1024,256]{1,0:T(8,128)(2,1)S(1)} %collective-permute-done.1.own), channel_id=1, source_target_pairs={{0,1},{1,0},{128,129},{129,128},{256,257},{257,256},{384,385},{385... | collective-permute-start | bytes 1572872 | tf_op jit(solution)/shard_map/ppermute | solution.py:41
  68.5 1.0 %copy-start.1 = (bf16[1024,256]{1,0:T(8,128)(2,1)S(1)}, bf16[1024,256]{1,0:T(8,128)(2,1)}, u32[]{:S(2)}) copy-start(bf16[1024,256]{1,0:T(8,128)(2,1)} %copy-done) | copy-start | bytes 1572868
  75.2 9.2 %copy-start.2 = (f32[256]{0:T(256)S(1)}, f32[256]{0:T(256)}, u32[]{:S(2)}) copy-start(f32[256]{0:T(256)} %param.4) | copy-start | bytes 3076
  80.1 10.3 %all-to-all-start = ((f32[4,64,128]{2,1,0:T(8,128)}), f32[4,64,128]{2,1,0:T(8,128)S(1)}, u32[]{:S(2)}, u32[]{:S(2)}) async-start(f32[4,64,128]{2,1,0:T(8,128)} %get-tuple-element.28), calls=%async_computation | async-start | bytes 262144 | tf_op jit(solution)/shard_map/all_to_all | solution.py:244

commit v3 on v2

--- a/solution.py
+++ b/solution.py
@@ -43,18 +43,6 @@
 
 def row_of(place, which, lo, span):
     return pl.multiple_of((lo * NY + place[which]) * span, span)
-
-
-def fetch(place, which, probes, cols, sem):
-    span = cols.shape[-1]
-    gets = []
-    for lo in range(LO):
-        get = pltpu.make_async_copy(
-            probes.at[:, pl.ds(row_of(place, which, lo, span), span)], cols.at[lo], sem.at[lo]
-        )
-        get.start()
-        gets.append(get)
-    return gets
 
 
 def assemble(place, own, other, block, rows):
@@ -75,13 +63,8 @@
     ]
 
 
-def step_kernel(which, rows, first, place, own, other, probes, *refs):
-    if first:
-        weight, total, sums, block, cols, put_sem, get_sem = refs
-    else:
-        total_in, _, weight, total, sums, block, cols, put_sem, get_sem = refs
+def put_rows(place, which, own, other, weight, rows, sem):
     span = HI * NC * rows
-    gets = fetch(place, which, probes, cols, get_sem)
     puts = []
     for side, piece in enumerate((own, other)):
         core = place[CORE] if side == 0 else 1 - place[CORE]
@@ -90,19 +73,54 @@
             put = pltpu.make_async_copy(
                 piece.at[pl.ds(z * rows, rows)],
                 weight.at[pl.ds(pl.multiple_of(at, rows), rows)],
-                put_sem,
+                sem,
             )
             put.start()
             puts.append(put)
+    return puts
+
+
+def line_sums(block, sums):
+    lines = block.shape[1] // LANES
+    for lo, s in enumerate(row_sums(block)):
+        for j in range(lines):
+            sums[lo * lines + j, :] = s[0, j * LANES : (j + 1) * LANES]
+
+
+def first_kernel(rows, place, own, other, probes, weight, total, sums, *refs):
+    back, ahead, far, block, cols_same, put_sem, get_sem = refs
+    cols = (cols_same, back, ahead, far)
+    span = HI * NC * rows
+    gets = []
+    for which in range(NY):
+        for lo in range(LO):
+            get = pltpu.make_async_copy(
+                probes.at[:, pl.ds(row_of(place, which, lo, span), span)],
+                cols[which].at[lo],
+                get_sem.at[which, lo],
+            )
+            get.start()
+            gets.append(get)
+    puts = put_rows(place, SAME, own, other, weight, rows, put_sem)
     assemble(place, own, other, block, rows)
-    for lo, s in enumerate(row_sums(block)):
-        for j in range(span // LANES):
-            sums[lo * (span // LANES) + j, :] = s[0, j * LANES : (j + 1) * LANES]
-    acc = jnp.zeros(total.shape, total.dtype) if first else total_in[...]
+    line_sums(block, sums)
+    acc = jnp.zeros(total.shape, total.dtype)
     for lo in range(LO):
         gets[lo].wait()
+        acc += jnp.dot(cols_same[lo], block[lo], preferred_element_type=jnp.float32)
+    total[...] = acc
+    for copy in puts + gets[LO:]:
+        copy.wait()
+
+
+def step_kernel(which, rows, place, own, other, cols, total_in, _, weight, total, sums, block, put_sem):
+    puts = put_rows(place, which, own, other, weight, rows, put_sem)
+    assemble(place, own, other, block, rows)
+    acc = total_in[...]
+    for lo in range(LO):
         acc += jnp.dot(cols[lo], block[lo], preferred_element_type=jnp.float32)
     total[...] = acc
+    line_sums(block, sums)
     for put in puts:
         put.wait()
 
@@ -123,19 +141,22 @@
                 sums[x, pl.ds(at + j, 1), :] = s[0:1, j * LANES : (j + 1) * LANES]
 
 
-def last_kernel(place, block, probes, total_in, bias, _, weight, keys, cols, put_sem, get_sem):
+def last_kernel(place, block, cols, total_in, bias, _, weight, keys, put_sem):
     span = block.shape[1]
-    gets = fetch(place, FAR, probes, cols, get_sem)
+    part = span // HI
     puts = []
     for lo in range(LO):
-        put = pltpu.make_async_copy(
-            block.at[lo], weight.at[pl.ds(row_of(place, FAR, lo, span), span)], put_sem.at[lo]
-        )
-        put.start()
-        puts.append(put)
+        for hi in range(HI):
+            at = row_of(place, FAR, lo, span) + hi * part
+            put = pltpu.make_async_copy(
+                block.at[lo, pl.ds(hi * part, part)],
+                weight.at[pl.ds(pl.multiple_of(at, part), part)],
+                put_sem,
+            )
+            put.start()
+            puts.append(put)
     acc = total_in[...] + bias[...]
     for lo in range(LO):
-        gets[lo].wait()
         acc += jnp.dot(cols[lo], block[lo], preferred_element_type=jnp.float32)
     keys[...] = acc.astype(keys.dtype)
     for put in puts:
@@ -145,7 +166,7 @@
 VMEM = pl.BlockSpec(memory_space=pltpu.VMEM)
 SMEM = pl.BlockSpec(memory_space=pltpu.SMEM)
 HBM = pl.BlockSpec(memory_space=pltpu.HBM)
-LIMIT = pltpu.CompilerParams(vmem_limit_bytes=50 << 20)
+LIMIT = pltpu.CompilerParams(vmem_limit_bytes=46 << 20)
 
 
 def sizes(piece, probes):
@@ -157,28 +178,47 @@
     return pl.CostEstimate(flops=flops, bytes_accessed=moved, transcendentals=0)
 
 
-def step(place, which, own, other, probes, carried=None):
+def first_step(place, own, other, probes):
     rows, span, heads, tokens, width = sizes(own, probes)
-    first = carried is None
-    return pl.pallas_call(
-        functools.partial(step_kernel, which, rows, first),
+    return pl.pallas_call(
+        functools.partial(first_kernel, rows),
         out_shape=(
             jax.ShapeDtypeStruct((width, heads), jnp.bfloat16),
             jax.ShapeDtypeStruct((tokens, heads), jnp.float32),
             jax.ShapeDtypeStruct((LO * span // LANES, LANES), jnp.float32),
-        ),
-        in_specs=[SMEM, VMEM, VMEM, HBM] + ([] if first else [VMEM, HBM]),
-        out_specs=(HBM, VMEM, VMEM),
+            *[jax.ShapeDtypeStruct((LO, tokens, span), jnp.bfloat16)] * 3,
+        ),
+        in_specs=[SMEM, VMEM, VMEM, HBM],
+        out_specs=(HBM, *[VMEM] * 5),
         scratch_shapes=[
             pltpu.VMEM((LO, span, heads), jnp.bfloat16),
             pltpu.VMEM((LO, tokens, span), jnp.bfloat16),
             pltpu.SemaphoreType.DMA,
-            pltpu.SemaphoreType.DMA((LO,)),
+            pltpu.SemaphoreType.DMA((NY, LO)),
         ],
-        input_output_aliases={} if first else {5: 0},
-        compiler_params=LIMIT,
-        cost_estimate=cost(2 * LO * span * heads * tokens, 2 * LO * span * (heads + tokens)),
-    )(place, own, other, probes, *(() if first else (carried[1], carried[0])))
+        compiler_params=LIMIT,
+        cost_estimate=cost(2 * LO * span * heads * tokens, 2 * LO * span * (heads + NY * tokens)),
+    )(place, own, other, probes)
+
+
+def step(place, which, own, other, cols, carried):
+    _, tokens, span = cols.shape
+    width, heads = carried[0].shape
+    rows = own.shape[0] // NZ
+    return pl.pallas_call(
+        functools.partial(step_kernel, which, rows),
+        out_shape=(
+            jax.ShapeDtypeStruct((width, heads), jnp.bfloat16),
+            jax.ShapeDtypeStruct((tokens, heads), jnp.float32),
+            jax.ShapeDtypeStruct((LO * span // LANES, LANES), jnp.float32),
+        ),
+        in_specs=[SMEM, VMEM, VMEM, VMEM, VMEM, HBM],
+        out_specs=(HBM, VMEM, VMEM),
+        scratch_shapes=[pltpu.VMEM((LO, span, heads), jnp.bfloat16), pltpu.SemaphoreType.DMA],
+        input_output_aliases={5: 0},
+        compiler_params=LIMIT,
+        cost_estimate=cost(2 * LO * span * heads * tokens, 2 * LO * span * heads),
+    )(place, own, other, cols, carried[1], carried[0])
 
 
 def all_sums(place, own, other, probes, before):
@@ -196,26 +236,22 @@
     )(place, own, other, *before)
 
 
-def last(place, block, probes, carried, bias):
+def last(place, block, cols, carried, bias):
     _, span, heads = block.shape
-    tokens, width = probes.shape
+    tokens, width = carried[1].shape[0], carried[0].shape[0]
     return pl.pallas_call(
         last_kernel,
         out_shape=(
             jax.ShapeDtypeStruct((width, heads), jnp.bfloat16),
             jax.ShapeDtypeStruct((tokens, heads), jnp.bfloat16),
         ),
-        in_specs=[SMEM, VMEM, HBM, VMEM, VMEM, HBM],
+        in_specs=[SMEM, VMEM, VMEM, VMEM, VMEM, HBM],
         out_specs=(HBM, VMEM),
-        scratch_shapes=[
-            pltpu.VMEM((LO, tokens, span), jnp.bfloat16),
-            pltpu.SemaphoreType.DMA((LO,)),
-            pltpu.SemaphoreType.DMA((LO,)),
-        ],
+        scratch_shapes=[pltpu.SemaphoreType.DMA],
         input_output_aliases={5: 0},
         compiler_params=LIMIT,
-        cost_estimate=cost(2 * LO * span * heads * tokens, 2 * LO * span * (heads + tokens)),
-    )(place, block, probes, carried[1], bias.reshape(1, -1), carried[0])
+        cost_estimate=cost(2 * LO * span * heads * tokens, 2 * LO * span * heads),
+    )(place, block, cols, carried[1], bias.reshape(1, -1), carried[0])
 
 
 def body(master, key_bias, probe_tokens):
@@ -235,14 +271,14 @@
     ahead_same = swap(back_other)
     far_other = swap(far_same)
 
-    s0 = step(place, SAME, mine, mine_other, probe_tokens)
-    s1 = step(place, BACK, back_same, back_other, probe_tokens, s0)
-    s2 = step(place, AHEAD, ahead_same, ahead_other, probe_tokens, s1)
+    *s0, cols_back, cols_ahead, cols_far = first_step(place, mine, mine_other, probe_tokens)
+    s1 = step(place, BACK, back_same, back_other, cols_back, s0)
+    s2 = step(place, AHEAD, ahead_same, ahead_other, cols_ahead, s1)
     block, sums = all_sums(
         place, far_same, far_other, probe_tokens, (s0[2], s1[2], s2[2])
     )
     gathered = lax.all_to_all(sums, "tp", split_axis=0, concat_axis=0, tiled=True)
-    weight, probe_keys = last(place, block, probe_tokens, s2, key_bias)
+    weight, probe_keys = last(place, block, cols_far, s2, key_bias)
     checksum = gathered.sum(axis=0).reshape(-1)
     return (weight, probe_keys, checksum)
 

time: 91.7 us -> 93.4 us (1.019)
  local copies, waits for them, and re-layouts: 1.92 us -> 3.75 us
  waiting for transfers between devices: 15.5 us -> 16.6 us
  Pallas kernels: 13.9 us -> 12.8 us
    unnamed x6 -> x10, local copies, waits for them, and re-layouts: 1.84 us -> 3.66 us
    pallas_call x1, Pallas kernels: 3.4 us -> 2.38 us  [last(): pl.pallas_call(last_kernel, out_shape=(jax.ShapeDtypeStruct((width, heads...]
    all_to_all x1, waiting for transfers between devices: 2.57 us -> 3.58 us  [body(): lax.all_to_all(sums, 'tp', split_axis=0, concat_axis=0, tiled=True)]
  transfers between devices with their start and end apart: 8 -> 8, of which waited for: 4 -> 4; matrix products, arithmetic and copies ran while one was open for 0% -> 0% of each run, Pallas kernels for 13% -> 12%
where the time goes in v3:
time: 93.4 us; the launch traced here: 92.8 us
  blocking collectives  38.5 us (41%)
  starting transfers between devices  18.9 us (20%)
  waiting for transfers between devices  16.6 us (18%)
  Pallas kernels  12.8 us (14%)
  local copies, waits for them, and re-layouts  3.75 us (4%)
  other arithmetic  1.47 us (2%)
    all_gather x1, blocking collectives, body(): lax.all_gather(own_rows, AXES, axis=0, tiled=True, axis_index_groups=Z_RI...  38.5 us
    ppermute x3, waiting for transfers between devices, onward(): return lax.ppermute(value, AXES, ONWARD)  13 us
    ppermute x4, starting transfers between devices, swap(): return lax.ppermute(value, AXES, SWAP)  7.65 us
    ppermute x3, starting transfers between devices, onward(): return lax.ppermute(value, AXES, ONWARD)  6.92 us
    pallas_call x2, Pallas kernels, step(): pl.pallas_call(functools.partial(step_kernel, which, rows), out_shape=(ja...  5.41 us
    all_to_all x1, starting transfers between devices, body(): lax.all_to_all(sums, 'tp', split_axis=0, concat_axis=0, tiled=True)  4.29 us
    unnamed x10, local copies, waits for them, and re-layouts  3.66 us
    all_to_all x1, waiting for transfers between devices, body(): lax.all_to_all(sums, 'tp', split_axis=0, concat_axis=0, tiled=True)  3.58 us
  transfers between devices with their start and end apart: 8, of which 4 were waited for; matrix products, arithmetic and copies ran while one was open for 0% of the time, Pallas kernels for 12%

profile of v3, /device:TPU:24, one launch (start us, length us, event | category | flops | bytes accessed | tf_op | source)
XLA Modules:
  0.0 92.8 jit_solution(18064321289631963300)
XLA Ops:
  0.6 0.8 convert_bitcast_fusion
  1.5 38.5 %all_gather.3.own = bf16[1024,256]{1,0:T(8,128)(2,1)S(1)} all-gather(bf16[64,256]{1,0:T(8,128)(2,1)S(1)} %convert_bitcast_fusion), channel_id=1, replica_groups={{0,128,256,384,2,130,258,386,4,132,260,388,6,134,262,390},{1,129,257,38..., dimensions={0}, use_global_device_ids=true | all-gather | bytes 557056 | tf_op jit(solution)/shard_map/all_gather | solution.py:265
  40.0 1.9 %collective-permute-start.3 = (bf16[1024,256]{1,0:T(8,128)(2,1)S(1)}, bf16[1024,256]{1,0:T(8,128)(2,1)S(1)}, u32[]{:S(2)}, u32[]{:S(2)}) collective-permute-start(bf16[1024,256]{1,0:T(8,128)(2,1)S(1)} %all_gather.3.own), channel_id=1, source_target_pairs={{0,1},{1,0},{128,129},{129,128},{256,257},{257,256},{384,385},{385... | collective-permute-start | bytes 1572872 | tf_op jit(solution)/shard_map/ppermute | solution.py:41
  41.9 2.7 %collective-permute-start = (bf16[1024,256]{1,0:T(8,128)(2,1)S(1)}, bf16[1024,256]{1,0:T(8,128)(2,1)S(1)}, u32[]{:S(2)}, u32[]{:S(2)}) collective-permute-start(bf16[1024,256]{1,0:T(8,128)(2,1)S(1)} %all_gather.3.own), channel_id=1, source_target_pairs={{0,24},{1,9},{128,152},{129,137},{256,280},{257,265},{384,408},{38... | collective-permute-start | bytes 1572872 | tf_op jit(solution)/shard_map/ppermute | solution.py:37
  44.6 0.0 collective-permute-done.3.other
  44.6 2.4 %collective-permute-start.4 = (bf16[1024,256]{1,0:T(8,128)(2,1)S(1)}, bf16[1024,256]{1,0:T(8,128)(2,1)}, u32[]{:S(2)}, u32[]{:S(2)}) collective-permute-start(bf16[1024,256]{1,0:T(8,128)(2,1)S(1)} %collective-permute-done.3.other), channel_id=1, source_target_pairs={{0,24},{1,9},{128,152},{129,137},{256,280},{257,265},{384,408},{38... | collective-permute-start | bytes 1572872 | tf_op jit(solution)/shard_map/ppermute | solution.py:37
  46.9 0.0 copy-start.2
  47.0 0.8 copy-done.2
  47.7 6.5 %collective-permute-done.own = bf16[1024,256]{1,0:T(8,128)(2,1)S(1)} collective-permute-done((bf16[1024,256]{1,0:T(8,128)(2,1)S(1)}, bf16[1024,256]{1,0:T(8,128)(2,1)S(1)}, u32[]{:S(2)}, u32[]{:S(2)}) %collective-permute-start) | collective-permute-done | bytes 524320 | tf_op jit(solution)/shard_map/ppermute | solution.py:37
  54.2 1.9 %collective-permute-start.1 = (bf16[1024,256]{1,0:T(8,128)(2,1)S(1)}, bf16[1024,256]{1,0:T(8,128)(2,1)S(1)}, u32[]{:S(2)}, u32[]{:S(2)}) collective-permute-start(bf16[1024,256]{1,0:T(8,128)(2,1)S(1)} %collective-permute-done.own), channel_id=1, source_target_pairs={{0,24},{1,9},{128,152},{129,137},{256,280},{257,265},{384,408},{38... | collective-permute-start | bytes 1572872 | tf_op jit(solution)/shard_map/ppermute | solution.py:37
  56.1 1.9 %collective-permute-start.6 = (bf16[1024,256]{1,0:T(8,128)(2,1)S(1)}, bf16[1024,256]{1,0:T(8,128)(2,1)}, u32[]{:S(2)}, u32[]{:S(2)}) collective-permute-start(bf16[1024,256]{1,0:T(8,128)(2,1)S(1)} %collective-permute-done.own), channel_id=1, source_target_pairs={{0,1},{1,0},{128,129},{129,128},{256,257},{257,256},{384,385},{385... | collective-permute-start | bytes 1572872 | tf_op jit(solution)/shard_map/ppermute | solution.py:41
  58.0 1.9 %collective-permute-done.4.other = bf16[1024,256]{1,0:T(8,128)(2,1)} collective-permute-done((bf16[1024,256]{1,0:T(8,128)(2,1)S(1)}, bf16[1024,256]{1,0:T(8,128)(2,1)}, u32[]{:S(2)}, u32[]{:S(2)}) %collective-permute-start.4) | collective-permute-done | bytes 524320 | tf_op jit(solution)/shard_map/ppermute | solution.py:37
  59.9 1.9 %collective-permute-start.5 = (bf16[1024,256]{1,0:T(8,128)(2,1)}, bf16[1024,256]{1,0:T(8,128)(2,1)}, u32[]{:S(2)}, u32[]{:S(2)}) collective-permute-start(bf16[1024,256]{1,0:T(8,128)(2,1)} %collective-permute-done.4.other), channel_id=1, source_target_pairs={{0,1},{1,0},{128,129},{129,128},{256,257},{257,256},{384,385},{385... | collective-permute-start | bytes 1572872 | tf_op jit(solution)/shard_map/ppermute | solution.py:41
  61.8 4.6 %collective-permute-done.1.own = bf16[1024,256]{1,0:T(8,128)(2,1)S(1)} collective-permute-done((bf16[1024,256]{1,0:T(8,128)(2,1)S(1)}, bf16[1024,256]{1,0:T(8,128)(2,1)S(1)}, u32[]{:S(2)}, u32[]{:S(2)}) %collective-permute-start.1) | collective-permute-done | bytes 524320 | tf_op jit(solution)/shard_map/ppermute | solution.py:37
  66.5 1.9 %collective-permute-start.2 = (bf16[1024,256]{1,0:T(8,128)(2,1)S(1)}, bf16[1024,256]{1,0:T(8,128)(2,1)S(1)}, u32[]{:S(2)}, u32[]{:S(2)}) collective-permute-start(bf16[1024,256]{1,0:T(8,128)(2,1)S(1)} %collective-permute-done.1.own), channel_id=1, source_target_pairs={{0,1},{1,0},{128,129},{129,128},{256,257},{257,256},{384,385},{385... | collective-permute-start | bytes 1572872 | tf_op jit(solution)/shard_map/ppermute | solution.py:41
  68.4 0.1 stack.23.place
  68.5 1.0 %copy-done.3 = bf16[1024,256]{1,0:T(8,128)(2,1)S(1)} copy-done((bf16[1024,256]{1,0:T(8,128)(2,1)S(1)}, bf16[1024,256]{1,0:T(8,128)(2,1)}, u32[]{:S(2)}) %copy-start.3) | copy-done | bytes 524312
  69.5 3.4 %shard_map.58 = (bf16[8192,256]{1,0:T(8,128)(2,1)}, f32[256,256]{1,0:T(8,128)S(1)}, f32[16,128]{1,0:T(8,128)S(1)}, bf16[4,256,512]{2,1,0:T(8,128)(2,1)S(1)}, bf1...) custom-call(s32[5]{0:T(128)S(1)} %stack.23.place, bf16[1024,256]{1,0:T(8,128)(2,1)S(1)} %all_gather.3.own, ...), custom_call_target="tpu_custom_call" | custom-call | flops 268435456 | bytes 5242880 | tf_op jit(solution)/shard_map/pallas_call | solution.py:183
  72.9 2.6 %shard_map.59 = (bf16[8192,256]{1,0:T(8,128)(2,1)}, f32[256,256]{1,0:T(8,128)S(1)}, f32[16,128]{1,0:T(8,128)S(1)}) custom-call(s32[5]{0:T(128)S(1)} %stack.23.place, bf16[1024,256]{1,0:T(8,128)(2,1)S(1)} %collective-permute-done.own, bf16[1024,256]{1,0:T(8,128)(2,1)} %collective-permute-done.4.other, ...), custom_call_target="tpu_custom_call", output_to_operand_aliasing={{0}: (5, {})} | custom-call | flops 268435456 | bytes 1048576 | tf_op jit(solution)/shard_map/pallas_call | solution.py:208
  75.5 0.0 copy-start.4
  75.6 0.0 collective-permute-done.6.other
  75.6 0.0 collective-permute-done.5.own
  75.6 2.8 %shard_map.60 = (bf16[8192,256]{1,0:T(8,128)(2,1)}, f32[256,256]{1,0:T(8,128)S(1)}, f32[16,128]{1,0:T(8,128)S(1)}) custom-call(s32[5]{0:T(128)S(1)} %stack.23.place, bf16[1024,256]{1,0:T(8,128)(2,1)} %collective-permute-done.5.own, bf16[1024,256]{1,0:T(8,128)(2,1)} %collective-permute-done.6.other, ...), custom_call_target="tpu_custom_call", output_to_operand_aliasing={{0}: (5, {})} | custom-call | flops 268435456 | bytes 1048576 | tf_op jit(solution)/shard_map/pallas_call | solution.py:208
  78.4 0.0 collective-permute-done.2.other
  78.4 0.0 copy-start
  78.4 0.8 copy-done
  79.2 1.0 %copy-done.1 = bf16[1024,256]{1,0:T(8,128)(2,1)S(1)} copy-done((bf16[1024,256]{1,0:T(8,128)(2,1)S(1)}, bf16[1024,256]{1,0:T(8,128)(2,1)}, u32[]{:S(2)}) %copy-start.1) | copy-done | bytes 524312
  80.2 1.7 %shard_map.61 = (bf16[4,512,256]{2,1,0:T(8,128)(2,1)S(1)}, f32[4,64,128]{2,1,0:T(8,128)}) custom-call(s32[5]{0:T(128)S(1)} %stack.23.place, bf16[1024,256]{1,0:T(8,128)(2,1)S(1)} %collective-permute-done.1.own, bf16[1024,256]{1,0:T(8,128)(2,1)S(1)} %copy-done.1, f32[16,128]{1,0:T(8,128)S(1)} %get-tuple-element.19.same, ...), custom_call_target="tpu_custom_call" | custom-call | flops 8388608 | bytes 2097152 | tf_op jit(solution)/shard_map/pallas_call | solution.py:226
  81.9 4.3 %all-to-all-start = ((f32[4,64,128]{2,1,0:T(8,128)}), f32[4,64,128]{2,1,0:T(8,128)S(1)}, u32[]{:S(2)}, u32[]{:S(2)}) async-start(f32[4,64,128]{2,1,0:T(8,128)} %get-tuple-element.34), calls=%async_computation | async-start | bytes 262144 | tf_op jit(solution)/shard_map/all_to_all | solution.py:280
  86.2 2.4 %shard_map.62 = (bf16[8192,256]{1,0:T(8,128)(2,1)}, bf16[256,256]{1,0:T(8,128)(2,1)}) custom-call(s32[5]{0:T(128)S(1)} %stack.23.place, bf16[4,512,256]{2,1,0:T(8,128)(2,1)S(1)} %get-tuple-element.28.block, bf16[4,256,512]{2,1,0:T(8,128)(2,1)S(1)} %get-tuple-element.29.cols, ...), custom_call_target="tpu_custom_call", output_to_operand_aliasing={{0}: (5, {})} | custom-call | flops 268435456 | bytes 1048576 | tf_op jit(solution)/shard_map/pallas_call | solution.py:242
  88.6 3.6 %all-to-all-done = f32[4,64,128]{2,1,0:T(8,128)S(1)} async-done(((f32[4,64,128]{2,1,0:T(8,128)}), f32[4,64,128]{2,1,0:T(8,128)S(1)}, u32[]{:S(2)}, u32[]{:S(2)}) %all-to-all-start) | async-done | bytes 131104 | tf_op jit(solution)/shard_map/all_to_all | solution.py:280
  92.1 0.6 reduce_sum.9
  (3 shorter events, 0.0 us)
Async XLA Ops:
  40.0 4.6 %collective-permute-start.3 = (bf16[1024,256]{1,0:T(8,128)(2,1)S(1)}, bf16[1024,256]{1,0:T(8,128)(2,1)S(1)}, u32[]{:S(2)}, u32[]{:S(2)}) collective-permute-start(bf16[1024,256]{1,0:T(8,128)(2,1)S(1)} %all_gather.3.own), channel_id=1, source_target_pairs={{0,1},{1,0},{128,129},{129,128},{256,257},{257,256},{384,385},{385... | collective-permute-start | bytes 1572872 | tf_op jit(solution)/shard_map/ppermute | solution.py:41
  41.9 12.3 %collective-permute-start = (bf16[1024,256]{1,0:T(8,128)(2,1)S(1)}, bf16[1024,256]{1,0:T(8,128)(2,1)S(1)}, u32[]{:S(2)}, u32[]{:S(2)}) collective-permute-start(bf16[1024,256]{1,0:T(8,128)(2,1)S(1)} %all_gather.3.own), channel_id=1, source_target_pairs={{0,24},{1,9},{128,152},{129,137},{256,280},{257,265},{384,408},{38... | collective-permute-start | bytes 1572872 | tf_op jit(solution)/shard_map/ppermute | solution.py:37
  44.6 15.3 %collective-permute-start.4 = (bf16[1024,256]{1,0:T(8,128)(2,1)S(1)}, bf16[1024,256]{1,0:T(8,128)(2,1)}, u32[]{:S(2)}, u32[]{:S(2)}) collective-permute-start(bf16[1024,256]{1,0:T(8,128)(2,1)S(1)} %collective-permute-done.3.other), channel_id=1, source_target_pairs={{0,24},{1,9},{128,152},{129,137},{256,280},{257,265},{384,408},{38... | collective-permute-start | bytes 1572872 | tf_op jit(solution)/shard_map/ppermute | solution.py:37
  46.9 0.8 copy-start.2
  54.2 12.3 %collective-permute-start.1 = (bf16[1024,256]{1,0:T(8,128)(2,1)S(1)}, bf16[1024,256]{1,0:T(8,128)(2,1)S(1)}, u32[]{:S(2)}, u32[]{:S(2)}) collective-permute-start(bf16[1024,256]{1,0:T(8,128)(2,1)S(1)} %collective-permute-done.own), channel_id=1, source_target_pairs={{0,24},{1,9},{128,152},{129,137},{256,280},{257,265},{384,408},{38... | collective-permute-start | bytes 1572872 | tf_op jit(solution)/shard_map/ppermute | solution.py:37
  56.1 19.4 %collective-permute-start.6 = (bf16[1024,256]{1,0:T(8,128)(2,1)S(1)}, bf16[1024,256]{1,0:T(8,128)(2,1)}, u32[]{:S(2)}, u32[]{:S(2)}) collective-permute-start(bf16[1024,256]{1,0:T(8,128)(2,1)S(1)} %collective-permute-done.own), channel_id=1, source_target_pairs={{0,1},{1,0},{128,129},{129,128},{256,257},{257,256},{384,385},{385... | collective-permute-start | bytes 1572872 | tf_op jit(solution)/shard_map/ppermute | solution.py:41
  59.9 15.7 %collective-permute-start.5 = (bf16[1024,256]{1,0:T(8,128)(2,1)}, bf16[1024,256]{1,0:T(8,128)(2,1)}, u32[]{:S(2)}, u32[]{:S(2)}) collective-permute-start(bf16[1024,256]{1,0:T(8,128)(2,1)} %collective-permute-done.4.other), channel_id=1, source_target_pairs={{0,1},{1,0},{128,129},{129,128},{256,257},{257,256},{384,385},{385... | collective-permute-start | bytes 1572872 | tf_op jit(solution)/shard_map/ppermute | solution.py:41
  66.5 11.9 %collective-permute-start.2 = (bf16[1024,256]{1,0:T(8,128)(2,1)S(1)}, bf16[1024,256]{1,0:T(8,128)(2,1)S(1)}, u32[]{:S(2)}, u32[]{:S(2)}) collective-permute-start(bf16[1024,256]{1,0:T(8,128)(2,1)S(1)} %collective-permute-done.1.own), channel_id=1, source_target_pairs={{0,1},{1,0},{128,129},{129,128},{256,257},{257,256},{384,385},{385... | collective-permute-start | bytes 1572872 | tf_op jit(solution)/shard_map/ppermute | solution.py:41
  68.5 1.0 %copy-start.3 = (bf16[1024,256]{1,0:T(8,128)(2,1)S(1)}, bf16[1024,256]{1,0:T(8,128)(2,1)}, u32[]{:S(2)}) copy-start(bf16[1024,256]{1,0:T(8,128)(2,1)} %copy-done.2) | copy-start | bytes 1572868
  75.5 10.6 %copy-start.4 = (f32[256]{0:T(256)S(1)}, f32[256]{0:T(256)}, u32[]{:S(2)}) copy-start(f32[256]{0:T(256)} %param.4) | copy-start | bytes 3076
  78.4 0.8 copy-start
  79.2 1.0 %copy-start.1 = (bf16[1024,256]{1,0:T(8,128)(2,1)S(1)}, bf16[1024,256]{1,0:T(8,128)(2,1)}, u32[]{:S(2)}) copy-start(bf16[1024,256]{1,0:T(8,128)(2,1)} %copy-done) | copy-start | bytes 1572868
  81.9 10.3 %all-to-all-start = ((f32[4,64,128]{2,1,0:T(8,128)}), f32[4,64,128]{2,1,0:T(8,128)S(1)}, u32[]{:S(2)}, u32[]{:S(2)}) async-start(f32[4,64,128]{2,1,0:T(8,128)} %get-tuple-element.34), calls=%async_computation | async-start | bytes 262144 | tf_op jit(solution)/shard_map/all_to_all | solution.py:280

commit v4 on v3

v4 whole, which is shorter than its diff:
```python
import functools
import itertools

import jax
import jax.numpy as jnp
from jax import lax
from jax.experimental import pallas as pl
from jax.experimental.pallas import tpu as pltpu
from jax.sharding import PartitionSpec as P


AXES = ("role", "tp", "dp")
NX, NY, NZ, NC, LO = 4, 4, 16, 2, 4
HI = NZ // LO
LANES = 128
SAME, BACK, AHEAD, FAR = range(4)
CORE = 4


def index_of(x, y, z, core):
    y, z, core = y % NY, z % NZ, core % NC
    return ((z % LO) * NX + x) * (NY * HI * NC) + (y * HI + z // LO) * NC + core


CHIPS = list(itertools.product(range(NX), range(NY), range(NZ), range(NC)))
Z_RINGS = [
    [index_of(x, y, z, c) for z in range(NZ)]
    for x, y, c in itertools.product(range(NX), range(NY), range(NC))
]


ONWARD = [(index_of(x, y, z, c), index_of(x, y + 2 * c - 1, z, c)) for x, y, z, c in CHIPS]
TEAMS = [
    [index_of(x, y, z, c) for x, c in itertools.product(range(NX), range(NC))]
    for y, z in itertools.product(range(NY), range(NZ))
]
SWAP = [(index_of(x, y, z, c), index_of(x, y, z, c + 1)) for x, y, z, c in CHIPS]


def onward(value):
    return lax.ppermute(value, AXES, ONWARD)


def swap(value):
    return lax.ppermute(value, AXES, SWAP)


def row_of(place, which, lo, span):
    return pl.multiple_of((lo * NY + place[which]) * span, span)


def assemble(core, piece, block, rows):
    span = HI * NC * rows
    for z in range(NZ):
        at = (z % LO) * span + ((z // LO) * NC + core) * rows
        block[pl.ds(pl.multiple_of(at, rows), rows), :] = piece[pl.ds(z * rows, rows), :]


def row_sums(block):
    ones = jnp.ones((8, block.shape[-1]), block.dtype)
    return lax.dot_general(
        ones, block[...], (((1,), (1,)), ((), ())), preferred_element_type=jnp.float32
    )


def fetch(place, which, probes, cols, sem):
    span = cols.shape[1] // LO
    gets = []
    for lo in range(LO):
        get = pltpu.make_async_copy(
            probes.at[:, pl.ds(row_of(place, which, lo, span), span)],
            cols.at[:, pl.ds(lo * span, span)],
            sem,
        )
        get.start()
        gets.append(get)
    return gets


def put_rows(place, which, own, other, weight, rows, sem):
    span = HI * NC * rows
    puts = []
    for side, piece in enumerate((own, other)):
        core = place[CORE] if side == 0 else 1 - place[CORE]
        for z in range(NZ):
            at = row_of(place, which, z % LO, span) + ((z // LO) * NC + core) * rows
            put = pltpu.make_async_copy(
                piece.at[pl.ds(z * rows, rows)],
                weight.at[pl.ds(pl.multiple_of(at, rows), rows)],
                sem,
            )
            put.start()
            puts.append(put)
    return puts


def put_block(place, which, block, weight, rows, sem):
    span = HI * NC * rows
    part = NC * rows
    puts = []
    for lo in range(LO):
        for hi in range(HI):
            at = row_of(place, which, lo, span) + hi * part
            put = pltpu.make_async_copy(
                block.at[pl.ds(lo * span + hi * part, part)],
                weight.at[pl.ds(pl.multiple_of(at, part), part)],
                sem,
            )
            put.start()
            puts.append(put)
    return puts


def line_sums(block, sums):
    s = row_sums(block)
    for j in range(s.shape[1] // LANES):
        sums[j, :] = s[0, j * LANES : (j + 1) * LANES]


def first_kernel(rows, place, own, other, probes, weight, total, sums, *refs):
    cols_back, block, cols_same, put_sem, get_sem = refs
    gets = fetch(place, SAME, probes, cols_same, get_sem.at[0])
    gets += fetch(place, BACK, probes, cols_back, get_sem.at[1])
    puts = put_rows(place, SAME, own, other, weight, rows, put_sem)
    assemble(place[CORE], own, block, rows)
    assemble(1 - place[CORE], other, block, rows)
    line_sums(block, sums)
    for get in gets[:LO]:
        get.wait()
    total[...] = jnp.dot(cols_same[...], block[...], preferred_element_type=jnp.float32)
    for copy in puts + gets[LO:]:
        copy.wait()


def back_kernel(rows, place, own, other, cols, total_in, _, weight, total, sums, block, put_sem):
    puts = put_rows(place, BACK, own, other, weight, rows, put_sem)
    assemble(place[CORE], own, block, rows)
    assemble(1 - place[CORE], other, block, rows)
    line_sums(block, sums)
    total[...] = total_in[...] + jnp.dot(
        cols[...], block[...], preferred_element_type=jnp.float32
    )
    for put in puts:
        put.wait()


def ahead_kernel(rows, place, block, probes, total_in, _, weight, total, cols_far, cols, put_sem, get_sem):
    gets = fetch(place, AHEAD, probes, cols, get_sem.at[0])
    later = fetch(place, FAR, probes, cols_far, get_sem.at[1])
    puts = put_block(place, AHEAD, block, weight, rows, put_sem)
    for get in gets:
        get.wait()
    total[...] = total_in[...] + jnp.dot(
        cols[...], block[...], preferred_element_type=jnp.float32
    )
    for copy in puts + later:
        copy.wait()


def sums_kernel(rows, place, own, same, back, sums, block):
    lines = HI * NC * rows // LANES
    core = place[CORE]
    block[...] = jnp.zeros_like(block)
    assemble(core, own, block, rows)
    far = row_sums(block)
    own_part = same[...] * (core == 0).astype(jnp.float32)
    nothing = jnp.zeros((lines, LANES), jnp.float32)
    for copy in range(sums.shape[0]):
        for lo in range(LO):
            def put(which, value):
                sums[copy, pl.ds((lo * NY + place[which]) * lines, lines), :] = value

            put(SAME, own_part[lo * lines : (lo + 1) * lines, :])
            put(BACK, back[lo * lines : (lo + 1) * lines, :])
            put(AHEAD, nothing)
            for j in range(lines):
                at = (lo * lines + j) * LANES
                sums[copy, pl.ds((lo * NY + place[FAR]) * lines + j, 1), :] = far[0:1, at : at + LANES]


def last_kernel(rows, place, own, other, cols, total_in, bias, _, weight, keys, block, put_sem):
    puts = put_rows(place, FAR, own, other, weight, rows, put_sem)
    assemble(place[CORE], own, block, rows)
    assemble(1 - place[CORE], other, block, rows)
    total = total_in[...] + jnp.dot(cols[...], block[...], preferred_element_type=jnp.float32)
    keys[...] = (total + bias[...]).astype(keys.dtype)
    for put in puts:
        put.wait()


VMEM = pl.BlockSpec(memory_space=pltpu.VMEM)
SMEM = pl.BlockSpec(memory_space=pltpu.SMEM)
HBM = pl.BlockSpec(memory_space=pltpu.HBM)
LIMIT = pltpu.CompilerParams(vmem_limit_bytes=48 << 20)


def sizes(piece, probes):
    rows = piece.shape[0] // NZ
    return rows, HI * NC * rows, piece.shape[1], probes.shape[0], probes.shape[1]


def cost(flops, moved):
    return pl.CostEstimate(flops=flops, bytes_accessed=moved, transcendentals=0)


def first_step(place, own, other, probes):
    rows, span, heads, tokens, width = sizes(own, probes)
    depth = LO * span
    return pl.pallas_call(
        functools.partial(first_kernel, rows),
        out_shape=(
            jax.ShapeDtypeStruct((width, heads), jnp.bfloat16),
            jax.ShapeDtypeStruct((tokens, heads), jnp.float32),
            jax.ShapeDtypeStruct((depth // LANES, LANES), jnp.float32),
            jax.ShapeDtypeStruct((tokens, depth), jnp.bfloat16),
        ),
        in_specs=[SMEM, VMEM, VMEM, HBM],
        out_specs=(HBM, *[VMEM] * 3),
        scratch_shapes=[
            pltpu.VMEM((depth, heads), jnp.bfloat16),
            pltpu.VMEM((tokens, depth), jnp.bfloat16),
            pltpu.SemaphoreType.DMA,
            pltpu.SemaphoreType.DMA((2,)),
        ],
        compiler_params=LIMIT,
        cost_estimate=cost(2 * depth * heads * tokens, 2 * depth * (heads + 2 * tokens)),
    )(place, own, other, probes)


def back_step(place, own, other, cols, carried):
    tokens, depth = cols.shape
    width, heads = carried[0].shape
    return pl.pallas_call(
        functools.partial(back_kernel, own.shape[0] // NZ),
        out_shape=(
            jax.ShapeDtypeStruct((width, heads), jnp.bfloat16),
            jax.ShapeDtypeStruct((tokens, heads), jnp.float32),
            jax.ShapeDtypeStruct((depth // LANES, LANES), jnp.float32),
            jax.ShapeDtypeStruct((depth, heads), jnp.bfloat16),
        ),
        in_specs=[SMEM, VMEM, VMEM, VMEM, VMEM, HBM],
        out_specs=(HBM, VMEM, VMEM, VMEM),
        scratch_shapes=[pltpu.SemaphoreType.DMA],
        input_output_aliases={5: 0},
        compiler_params=LIMIT,
        cost_estimate=cost(2 * depth * heads * tokens, 2 * depth * heads),
    )(place, own, other, cols, carried[1], carried[0])


def ahead_step(place, block, probes, carried):
    depth, heads = block.shape
    tokens, width = probes.shape
    return pl.pallas_call(
        functools.partial(ahead_kernel, depth // (NZ * NC)),
        out_shape=(
            jax.ShapeDtypeStruct((width, heads), jnp.bfloat16),
            jax.ShapeDtypeStruct((tokens, heads), jnp.float32),
            jax.ShapeDtypeStruct((tokens, depth), jnp.bfloat16),
        ),
        in_specs=[SMEM, VMEM, HBM, VMEM, HBM],
        out_specs=(HBM, VMEM, VMEM),
        scratch_shapes=[
            pltpu.VMEM((tokens, depth), jnp.bfloat16),
            pltpu.SemaphoreType.DMA,
            pltpu.SemaphoreType.DMA((2,)),
        ],
        input_output_aliases={4: 0},
        compiler_params=LIMIT,
        cost_estimate=cost(2 * depth * heads * tokens, 2 * depth * (heads + 2 * tokens)),
    )(place, block, probes, carried[1], carried[0])


def team_sums(place, own, same, back, width):
    rows = own.shape[0] // NZ
    return pl.pallas_call(
        functools.partial(sums_kernel, rows),
        out_shape=jax.ShapeDtypeStruct((NX * NC, width // LANES, LANES), jnp.float32),
        in_specs=[SMEM] + [VMEM] * 3,
        out_specs=VMEM,
        scratch_shapes=[pltpu.VMEM((NC * own.shape[0], own.shape[1]), jnp.bfloat16)],
        compiler_params=LIMIT,
        cost_estimate=cost(16 * own.size * NC, 4 * own.size),
    )(place, own, same, back)


def last_step(place, own, other, cols, carried, bias):
    tokens, depth = cols.shape
    width, heads = carried[0].shape
    return pl.pallas_call(
        functools.partial(last_kernel, own.shape[0] // NZ),
        out_shape=(
            jax.ShapeDtypeStruct((width, heads), jnp.bfloat16),
            jax.ShapeDtypeStruct((tokens, heads), jnp.bfloat16),
        ),
        in_specs=[SMEM, VMEM, VMEM, VMEM, VMEM, VMEM, HBM],
        out_specs=(HBM, VMEM),
        scratch_shapes=[pltpu.VMEM((depth, heads), jnp.bfloat16), pltpu.SemaphoreType.DMA],
        input_output_aliases={6: 0},
        compiler_params=LIMIT,
        cost_estimate=cost(2 * depth * heads * tokens, 2 * depth * heads),
    )(place, own, other, cols, carried[1], bias.reshape(1, -1), carried[0])


def body(master, key_bias, probe_tokens):
    dp = lax.axis_index("dp")
    core = lax.rem(dp, NC)
    y = lax.div(dp, HI * NC)
    back = lax.rem(y + 1 + 2 * core, NY)
    place = jnp.stack([y, back, lax.rem(back + 2, NY), lax.rem(y + 2, NY), core])

    own_rows = jnp.transpose(master).astype(jnp.bfloat16)
    own_rows, place = lax.optimization_barrier((own_rows, place))
    mine = lax.all_gather(own_rows, AXES, axis=0, tiled=True, axis_index_groups=Z_RINGS)
    back_same = onward(mine)
    mine_other = swap(mine)
    back_other = onward(mine_other)
    far_same = onward(back_same)
    *s0, cols_back = first_step(place, mine, mine_other, probe_tokens)
    *s1, block = back_step(place, back_same, back_other, cols_back, s0)
    ahead = swap(block)
    sums = team_sums(place, far_same, s0[2], s1[2], probe_tokens.shape[1])
    gathered = lax.all_to_all(
        sums, AXES, split_axis=0, concat_axis=0, tiled=True, axis_index_groups=TEAMS
    )
    far_other = swap(far_same)
    *s2, cols_far = ahead_step(place, ahead, probe_tokens, s1)
    weight, probe_keys = last_step(place, far_same, far_other, cols_far, s2, key_bias)
    checksum = gathered.sum(axis=0).reshape(-1)
    return (weight, probe_keys, checksum)


def solution(mesh):
    placed = (P("tp", ("role", "dp")), P("tp"), P(("role", "dp"), None))
    return jax.shard_map(
        body,
        mesh=mesh,
        in_specs=placed,
        out_specs=(P(None, "tp"), P(("role", "dp"), "tp"), P()),
        check_vma=False,
    )
```

time: 93.4 us -> 98.3 us (1.052)
  blocking collectives: 38.5 us -> 50.3 us
  starting transfers between devices: 18.9 us -> 12.7 us
  waiting for transfers between devices: 16.6 us -> 20.3 us
  local copies, waits for them, and re-layouts: 3.75 us -> 0.09 us
  Pallas kernels: 12.8 us -> 11.2 us
    all_to_all x0 -> x1, blocking collectives: none -> 11.8 us  [body(): lax.all_to_all(sums, AXES, split_axis=0, concat_axis=0, tiled=True, axis_...]
    ppermute x3, waiting for transfers between devices: 13 us -> 20.3 us  [onward(): return lax.ppermute(value, AXES, ONWARD)]
    all_to_all x1 -> x0, starting transfers between devices: 4.29 us -> none  [body(): lax.all_to_all(sums, 'tp', split_axis=0, concat_axis=0, tiled=True)]
    unnamed x10 -> x2, local copies, waits for them, and re-layouts: 3.66 us -> 0.01 us
    all_to_all x1 -> x0, waiting for transfers between devices: 3.58 us -> none  [body(): lax.all_to_all(sums, 'tp', split_axis=0, concat_axis=0, tiled=True)]
    ppermute x4 -> x3, starting transfers between devices: 7.65 us -> 5.74 us  [swap(): return lax.ppermute(value, AXES, SWAP)]
    pallas_call x4, Pallas kernels: 9.45 us -> 8.3 us  [the longest x1 2.61 us: ahead_step(): pl.pallas_call(functools.partial(ahead_kernel, depth // (NZ * NC)), out_s...]
  transfers between devices with their start and end apart: 8 -> 6, of which waited for: 4 -> 3; matrix products, arithmetic and copies ran while one was open for 0% -> 2% of each run, Pallas kernels for 12% -> 7%
where the time goes in v4:
time: 98.3 us; the launch traced here: 97.8 us
  blocking collectives  50.3 us (51%)
  waiting for transfers between devices  20.3 us (21%)
  starting transfers between devices  12.7 us (13%)
  Pallas kernels  11.2 us (11%)
  other arithmetic  2.43 us (2%)
    all_gather x1, blocking collectives, body(): lax.all_gather(own_rows, AXES, axis=0, tiled=True, axis_index_groups=Z_RI...  38.5 us
    ppermute x3, waiting for transfers between devices, onward(): return lax.ppermute(value, AXES, ONWARD)  20.3 us
    all_to_all x1, blocking collectives, body(): lax.all_to_all(sums, AXES, split_axis=0, concat_axis=0, tiled=True, axis_...  11.8 us
    ppermute x3, starting transfers between devices, onward(): return lax.ppermute(value, AXES, ONWARD)  6.93 us
    ppermute x3, starting transfers between devices, swap(): return lax.ppermute(value, AXES, SWAP)  5.74 us
    pallas_call x1, Pallas kernels, first_step(): pl.pallas_call(functools.partial(first_kernel, rows), out_shape=(jax.Shap...  2.91 us
    pallas_call x1, Pallas kernels, ahead_step(): pl.pallas_call(functools.partial(ahead_kernel, depth // (NZ * NC)), out_s...  2.61 us
    pallas_call x1, Pallas kernels, last_step(): pl.pallas_call(functools.partial(last_kernel, own.shape[0] // NZ), out_sh...  2.48 us
  transfers between devices with their start and end apart: 6, of which 3 were waited for; matrix products, arithmetic and copies ran while one was open for 2% of the time, Pallas kernels for 7%

profile of v4, /device:TPU:24, one launch (start us, length us, event | category | flops | bytes accessed | tf_op | source)
XLA Modules:
  0.0 97.8 jit_solution(17100849123918869448)
XLA Ops:
  0.7 0.8 convert_bitcast_fusion
  1.5 0.1 stack.23.place
  1.6 38.5 %all_gather.3.own = bf16[1024,256]{1,0:T(8,128)(2,1)S(1)} all-gather(bf16[64,256]{1,0:T(8,128)(2,1)S(1)} %convert_bitcast_fusion), channel_id=1, replica_groups={{0,128,256,384,2,130,258,386,4,132,260,388,6,134,262,390},{1,129,257,38..., dimensions={0}, use_global_device_ids=true | all-gather | bytes 557056 | tf_op jit(solution)/shard_map/all_gather | solution.py:313
  40.1 1.9 %collective-permute-start.3 = (bf16[1024,256]{1,0:T(8,128)(2,1)S(1)}, bf16[1024,256]{1,0:T(8,128)(2,1)S(1)}, u32[]{:S(2)}, u32[]{:S(2)}) collective-permute-start(bf16[1024,256]{1,0:T(8,128)(2,1)S(1)} %all_gather.3.own), channel_id=1, source_target_pairs={{0,1},{1,0},{128,129},{129,128},{256,257},{257,256},{384,385},{385... | collective-permute-start | bytes 1572872 | tf_op jit(solution)/shard_map/ppermute | solution.py:45
  42.0 2.7 %collective-permute-start = (bf16[1024,256]{1,0:T(8,128)(2,1)S(1)}, bf16[1024,256]{1,0:T(8,128)(2,1)S(1)}, u32[]{:S(2)}, u32[]{:S(2)}) collective-permute-start(bf16[1024,256]{1,0:T(8,128)(2,1)S(1)} %all_gather.3.own), channel_id=1, source_target_pairs={{0,24},{1,9},{128,152},{129,137},{256,280},{257,265},{384,408},{38... | collective-permute-start | bytes 1572872 | tf_op jit(solution)/shard_map/ppermute | solution.py:41
  44.7 0.0 collective-permute-done.3.other
  44.7 2.4 %collective-permute-start.4 = (bf16[1024,256]{1,0:T(8,128)(2,1)S(1)}, bf16[1024,256]{1,0:T(8,128)(2,1)S(1)}, u32[]{:S(2)}, u32[]{:S(2)}) collective-permute-start(bf16[1024,256]{1,0:T(8,128)(2,1)S(1)} %collective-permute-done.3.other), channel_id=1, source_target_pairs={{0,24},{1,9},{128,152},{129,137},{256,280},{257,265},{384,408},{38... | collective-permute-start | bytes 1572872 | tf_op jit(solution)/shard_map/ppermute | solution.py:41
  47.1 2.9 %shard_map.58 = (bf16[8192,256]{1,0:T(8,128)(2,1)}, f32[256,256]{1,0:T(8,128)S(1)}, f32[16,128]{1,0:T(8,128)S(1)}, bf16[256,2048]{1,0:T(8,128)(2,1)S(1)}) custom-call(s32[5]{0:T(128)S(1)} %stack.23.place, bf16[1024,256]{1,0:T(8,128)(2,1)S(1)} %all_gather.3.own, bf16[1024,256]{1,0:T(8,128)(2,1)S(1)} %collective-permute-done.3.other, bf16[256,8192]{1,0:T(8,128)(2,1)} %probes.3), custom_call_target="tpu_custom_call" | custom-call | flops 268435456 | bytes 3145728 | tf_op jit(solution)/shard_map/pallas_call | solution.py:209
  50.0 4.3 %collective-permute-done.own = bf16[1024,256]{1,0:T(8,128)(2,1)S(1)} collective-permute-done((bf16[1024,256]{1,0:T(8,128)(2,1)S(1)}, bf16[1024,256]{1,0:T(8,128)(2,1)S(1)}, u32[]{:S(2)}, u32[]{:S(2)}) %collective-permute-start) | collective-permute-done | bytes 524320 | tf_op jit(solution)/shard_map/ppermute | solution.py:41
  54.3 5.6 %collective-permute-done.4.other = bf16[1024,256]{1,0:T(8,128)(2,1)S(1)} collective-permute-done((bf16[1024,256]{1,0:T(8,128)(2,1)S(1)}, bf16[1024,256]{1,0:T(8,128)(2,1)S(1)}, u32[]{:S(2)}, u32[]{:S(2)}) %collective-permute-start.4) | collective-permute-done | bytes 524320 | tf_op jit(solution)/shard_map/ppermute | solution.py:41
  59.9 2.1 %shard_map.59 = (bf16[8192,256]{1,0:T(8,128)(2,1)}, f32[256,256]{1,0:T(8,128)S(1)}, f32[16,128]{1,0:T(8,128)S(1)}, bf16[2048,256]{1,0:T(8,128)(2,1)S(1)}) custom-call(s32[5]{0:T(128)S(1)} %stack.23.place, bf16[1024,256]{1,0:T(8,128)(2,1)S(1)} %collective-permute-done.own, ...), custom_call_target="tpu_custom_call", output_to_operand_aliasing={{0}: (5, {})} | custom-call | flops 268435456 | bytes 1048576 | tf_op jit(solution)/shard_map/pallas_call | solution.py:233
  62.1 1.9 %collective-permute-start.5 = (bf16[2048,256]{1,0:T(8,128)(2,1)S(1)}, bf16[2048,256]{1,0:T(8,128)(2,1)S(1)}, u32[]{:S(2)}, u32[]{:S(2)}) collective-permute-start(bf16[2048,256]{1,0:T(8,128)(2,1)S(1)} %get-tuple-element.23), channel_id=1, source_target_pairs={{0,1},{1,0},{128,129},{129,128},{256,257},{257,256},{384,385},{385... | collective-permute-start | bytes 3145736 | tf_op jit(solution)/shard_map/ppermute | solution.py:45
  64.0 1.9 %collective-permute-start.1 = (bf16[1024,256]{1,0:T(8,128)(2,1)S(1)}, bf16[1024,256]{1,0:T(8,128)(2,1)S(1)}, u32[]{:S(2)}, u32[]{:S(2)}) collective-permute-start(bf16[1024,256]{1,0:T(8,128)(2,1)S(1)} %collective-permute-done.own), channel_id=1, source_target_pairs={{0,24},{1,9},{128,152},{129,137},{256,280},{257,265},{384,408},{38... | collective-permute-start | bytes 1572872 | tf_op jit(solution)/shard_map/ppermute | solution.py:41
  65.9 10.4 %collective-permute-done.1.own = bf16[1024,256]{1,0:T(8,128)(2,1)S(1)} collective-permute-done((bf16[1024,256]{1,0:T(8,128)(2,1)S(1)}, bf16[1024,256]{1,0:T(8,128)(2,1)S(1)}, u32[]{:S(2)}, u32[]{:S(2)}) %collective-permute-start.1) | collective-permute-done | bytes 524320 | tf_op jit(solution)/shard_map/ppermute | solution.py:41
  76.3 1.9 %collective-permute-start.2 = (bf16[1024,256]{1,0:T(8,128)(2,1)S(1)}, bf16[1024,256]{1,0:T(8,128)(2,1)S(1)}, u32[]{:S(2)}, u32[]{:S(2)}) collective-permute-start(bf16[1024,256]{1,0:T(8,128)(2,1)S(1)} %collective-permute-done.1.own), channel_id=1, source_target_pairs={{0,1},{1,0},{128,129},{129,128},{256,257},{257,256},{384,385},{385... | collective-permute-start | bytes 1572872 | tf_op jit(solution)/shard_map/ppermute | solution.py:45
  78.2 1.1 %shard_map.62 = f32[8,64,128]{2,1,0:T(8,128)S(1)} custom-call(s32[5]{0:T(128)S(1)} %stack.23.place, bf16[1024,256]{1,0:T(8,128)(2,1)S(1)} %collective-permute-done.1.own, f32[16,128]{1,0:T(8,128)S(1)} %get-tuple-element.31.same, f32[16,128]{1,0:T(8,128)S(1)} %get-tuple-element.32.back), custom_call_target="tpu_custom_call" | custom-call | flops 8388608 | bytes 1048576 | tf_op jit(solution)/shard_map/pallas_call | solution.py:275
  79.3 11.8 %all_to_all.5 = f32[8,64,128]{2,1,0:T(8,128)} all-to-all(f32[8,64,128]{2,1,0:T(8,128)S(1)} %shard_map.62), channel_id=1, replica_groups={{0,1,32,33,64,65,96,97},{128,129,160,161,192,193,224,225},{256,257,288,..., dimensions={0} | all-to-all | bytes 524288 | tf_op jit(solution)/shard_map/all_to_all | solution.py:322
  91.1 1.6 %reduce_sum.9 = f32[64,128]{1,0:T(8,128)} reduce(f32[8,64,128]{2,1,0:T(8,128)} %all_to_all.5, f32[]{:T(128)} %constant.23.clone.1), dimensions={0}, to_apply=%region_0.0 | reduce | flops 57344 | bytes 294916 | tf_op jit(solution)/shard_map/reduce_sum | solution.py:328
  92.7 0.0 collective-permute-done.5.block
  92.7 0.0 copy-start
  92.7 2.6 %shard_map.60 = (bf16[8192,256]{1,0:T(8,128)(2,1)}, f32[256,256]{1,0:T(8,128)S(1)}, bf16[256,2048]{1,0:T(8,128)(2,1)S(1)}) custom-call(s32[5]{0:T(128)S(1)} %stack.23.place, bf16[2048,256]{1,0:T(8,128)(2,1)S(1)} %collective-permute-done.5.block, bf16[256,8192]{1,0:T(8,128)(2,1)} %probes.3, ...), custom_call_target="tpu_custom_call", output_to_operand_aliasing={{0}: (4, {})} | custom-call | flops 268435456 | bytes 3145728 | tf_op jit(solution)/shard_map/pallas_call | solution.py:253
  95.3 0.0 collective-permute-done.2.other
  95.3 0.0 copy-done
  95.3 2.5 %shard_map.61 = (bf16[8192,256]{1,0:T(8,128)(2,1)}, bf16[256,256]{1,0:T(8,128)(2,1)}) custom-call(s32[5]{0:T(128)S(1)} %stack.23.place, bf16[1024,256]{1,0:T(8,128)(2,1)S(1)} %collective-permute-done.1.own, bf16[1024,256]{1,0:T(8,128)(2,1)S(1)} %collective-permute-done.2.other, ...), custom_call_target="tpu_custom_call", output_to_operand_aliasing={{0}: (6, {})} | custom-call | flops 268435456 | bytes 1048576 | tf_op jit(solution)/shard_map/pallas_call | solution.py:289
Async XLA Ops:
  40.1 4.6 %collective-permute-start.3 = (bf16[1024,256]{1,0:T(8,128)(2,1)S(1)}, bf16[1024,256]{1,0:T(8,128)(2,1)S(1)}, u32[]{:S(2)}, u32[]{:S(2)}) collective-permute-start(bf16[1024,256]{1,0:T(8,128)(2,1)S(1)} %all_gather.3.own), channel_id=1, source_target_pairs={{0,1},{1,0},{128,129},{129,128},{256,257},{257,256},{384,385},{385... | collective-permute-start | bytes 1572872 | tf_op jit(solution)/shard_map/ppermute | solution.py:45
  42.0 12.3 %collective-permute-start = (bf16[1024,256]{1,0:T(8,128)(2,1)S(1)}, bf16[1024,256]{1,0:T(8,128)(2,1)S(1)}, u32[]{:S(2)}, u32[]{:S(2)}) collective-permute-start(bf16[1024,256]{1,0:T(8,128)(2,1)S(1)} %all_gather.3.own), channel_id=1, source_target_pairs={{0,24},{1,9},{128,152},{129,137},{256,280},{257,265},{384,408},{38... | collective-permute-start | bytes 1572872 | tf_op jit(solution)/shard_map/ppermute | solution.py:41
  44.7 15.2 %collective-permute-start.4 = (bf16[1024,256]{1,0:T(8,128)(2,1)S(1)}, bf16[1024,256]{1,0:T(8,128)(2,1)S(1)}, u32[]{:S(2)}, u32[]{:S(2)}) collective-permute-start(bf16[1024,256]{1,0:T(8,128)(2,1)S(1)} %collective-permute-done.3.other), channel_id=1, source_target_pairs={{0,24},{1,9},{128,152},{129,137},{256,280},{257,265},{384,408},{38... | collective-permute-start | bytes 1572872 | tf_op jit(solution)/shard_map/ppermute | solution.py:41
  62.1 30.6 %collective-permute-start.5 = (bf16[2048,256]{1,0:T(8,128)(2,1)S(1)}, bf16[2048,256]{1,0:T(8,128)(2,1)S(1)}, u32[]{:S(2)}, u32[]{:S(2)}) collective-permute-start(bf16[2048,256]{1,0:T(8,128)(2,1)S(1)} %get-tuple-element.23), channel_id=1, source_target_pairs={{0,1},{1,0},{128,129},{129,128},{256,257},{257,256},{384,385},{385... | collective-permute-start | bytes 3145736 | tf_op jit(solution)/shard_map/ppermute | solution.py:45
  64.0 12.3 %collective-permute-start.1 = (bf16[1024,256]{1,0:T(8,128)(2,1)S(1)}, bf16[1024,256]{1,0:T(8,128)(2,1)S(1)}, u32[]{:S(2)}, u32[]{:S(2)}) collective-permute-start(bf16[1024,256]{1,0:T(8,128)(2,1)S(1)} %collective-permute-done.own), channel_id=1, source_target_pairs={{0,24},{1,9},{128,152},{129,137},{256,280},{257,265},{384,408},{38... | collective-permute-start | bytes 1572872 | tf_op jit(solution)/shard_map/ppermute | solution.py:41
  76.3 19.0 %collective-permute-start.2 = (bf16[1024,256]{1,0:T(8,128)(2,1)S(1)}, bf16[1024,256]{1,0:T(8,128)(2,1)S(1)}, u32[]{:S(2)}, u32[]{:S(2)}) collective-permute-start(bf16[1024,256]{1,0:T(8,128)(2,1)S(1)} %collective-permute-done.1.own), channel_id=1, source_target_pairs={{0,1},{1,0},{128,129},{129,128},{256,257},{257,256},{384,385},{385... | collective-permute-start | bytes 1572872 | tf_op jit(solution)/shard_map/ppermute | solution.py:45
  92.7 2.6 %copy-start = (f32[256]{0:T(256)S(1)}, f32[256]{0:T(256)}, u32[]{:S(2)}) copy-start(f32[256]{0:T(256)} %param.4) | copy-start | bytes 3076

commit v5 on v0

v5 whole, which is shorter than its diff:
```python
import functools
import itertools

import jax
import jax.numpy as jnp
from jax import lax
from jax.experimental import pallas as pl
from jax.experimental.pallas import tpu as pltpu
from jax.sharding import PartitionSpec as P


AXES = ("role", "tp", "dp")
NX, NY, NZ, NC, LO = 4, 4, 16, 2, 4
HI = NZ // LO
LANES = 128
SAME, BACK, AHEAD, FAR = range(4)
CORE = 4


def index_of(x, y, z, core):
    y, z, core = y % NY, z % NZ, core % NC
    return ((z % LO) * NX + x) * (NY * HI * NC) + (y * HI + z // LO) * NC + core


CHIPS = list(itertools.product(range(NX), range(NY), range(NZ), range(NC)))
Z_RINGS = [
    [index_of(x, y, z, c) for z in range(NZ)]
    for x, y, c in itertools.product(range(NX), range(NY), range(NC))
]


ONWARD = [(index_of(x, y, z, c), index_of(x, y + 2 * c - 1, z, c)) for x, y, z, c in CHIPS]
CONTRARY = [(index_of(x, y, z, c), index_of(x, y + 1 - 2 * c, z, c)) for x, y, z, c in CHIPS]
TEAMS = [
    [index_of(x, y, z, c) for x, c in itertools.product(range(NX), range(NC))]
    for y, z in itertools.product(range(NY), range(NZ))
]
SWAP = [(index_of(x, y, z, c), index_of(x, y, z, c + 1)) for x, y, z, c in CHIPS]


def onward(value):
    return lax.ppermute(value, AXES, ONWARD)


def contrary(value):
    return lax.ppermute(value, AXES, CONTRARY)


def swap(value):
    return lax.ppermute(value, AXES, SWAP)


def row_of(place, which, lo, span):
    return pl.multiple_of((lo * NY + place[which]) * span, span)


def assemble(core, piece, block, rows):
    span = HI * NC * rows
    for z in range(NZ):
        at = (z % LO) * span + ((z // LO) * NC + core) * rows
        block[pl.ds(pl.multiple_of(at, rows), rows), :] = piece[pl.ds(z * rows, rows), :]


def row_sums(block):
    ones = jnp.ones((8, block.shape[-1]), block.dtype)
    return lax.dot_general(
        ones, block[...], (((1,), (1,)), ((), ())), preferred_element_type=jnp.float32
    )


def fetch(place, which, probes, cols, sem):
    span = cols.shape[1] // LO
    gets = []
    for lo in range(LO):
        get = pltpu.make_async_copy(
            probes.at[:, pl.ds(row_of(place, which, lo, span), span)],
            cols.at[:, pl.ds(lo * span, span)],
            sem,
        )
        get.start()
        gets.append(get)
    return gets


def put_rows(place, which, own, other, weight, rows, sem):
    span = HI * NC * rows
    puts = []
    for side, piece in enumerate((own, other)):
        core = place[CORE] if side == 0 else 1 - place[CORE]
        for z in range(NZ):
            at = row_of(place, which, z % LO, span) + ((z // LO) * NC + core) * rows
            put = pltpu.make_async_copy(
                piece.at[pl.ds(z * rows, rows)],
                weight.at[pl.ds(pl.multiple_of(at, rows), rows)],
                sem,
            )
            put.start()
            puts.append(put)
    return puts


def line_sums(block, sums, first):
    s = row_sums(block)
    for j in range(s.shape[1] // LANES):
        sums[first + j, :] = s[0, j * LANES : (j + 1) * LANES]


def near_kernel(rows, place, own, other, own_b, other_b, probes, weight, total, sums, *refs):
    blocks, cols, put_sem, get_sem = refs
    gets = [fetch(place, which, probes, cols.at[i], get_sem.at[i]) for i, which in enumerate((SAME, BACK))]
    puts = put_rows(place, SAME, own, other, weight, rows, put_sem)
    puts += put_rows(place, BACK, own_b, other_b, weight, rows, put_sem)
    core = place[CORE]
    for i, (mine, partner) in enumerate(((own, other), (own_b, other_b))):
        block = blocks.at[i]
        assemble(core, mine, block, rows)
        assemble(1 - core, partner, block, rows)
        line_sums(block, sums, i * (block.shape[0] // LANES))
    for i in range(2):
        for get in gets[i]:
            get.wait()
        part = jnp.dot(cols[i], blocks[i], preferred_element_type=jnp.float32)
        total[...] = part if i == 0 else total[...] + part
    for put in puts:
        put.wait()


def sums_kernel(rows, place, own, near, sums):
    lines = HI * NC * rows // LANES
    core = place[CORE]
    ones = jnp.ones((8, own.shape[1]), own.dtype)
    s = lax.dot_general(
        ones, own[...], (((1,), (1,)), ((), ())), preferred_element_type=jnp.float32
    )
    lane = lax.broadcasted_iota(jnp.int32, (1, LANES), 1)
    my_half = (lane // rows) == core
    own_part = near[: LO * lines, :] * (core == 0).astype(jnp.float32)
    nothing = jnp.zeros((lines, LANES), jnp.float32)
    for lo in range(LO):
        sums[0, pl.ds((lo * NY + place[SAME]) * lines, lines), :] = own_part[
            lo * lines : (lo + 1) * lines, :
        ]
        sums[0, pl.ds((lo * NY + place[BACK]) * lines, lines), :] = near[
            (LO + lo) * lines : (LO + lo + 1) * lines, :
        ]
        sums[0, pl.ds((lo * NY + place[AHEAD]) * lines, lines), :] = nothing
    for pair in range(NZ // 2):
        both = s[0:1, pair * LANES : (pair + 1) * LANES]
        turned = pltpu.roll(both, rows, 1)
        for odd in range(2):
            z = 2 * pair + odd
            line = jnp.where(core == odd, both, turned)
            at = (z % LO * NY + place[FAR]) * lines + z // LO
            sums[0, pl.ds(at, 1), :] = jnp.where(my_half, line, 0.0)
    whole = sums[0]
    for copy in range(1, sums.shape[0]):
        sums[copy] = whole


def last_kernel(rows, place, own, other, own_f, other_f, probes, total_in, bias, _, weight, keys, *refs):
    blocks, cols, put_sem, get_sem = refs
    gets = [fetch(place, which, probes, cols.at[i], get_sem.at[i]) for i, which in enumerate((AHEAD, FAR))]
    puts = put_rows(place, AHEAD, own, other, weight, rows, put_sem)
    puts += put_rows(place, FAR, own_f, other_f, weight, rows, put_sem)
    core = place[CORE]
    for i, (mine, partner) in enumerate(((own, other), (own_f, other_f))):
        assemble(core, mine, blocks.at[i], rows)
        assemble(1 - core, partner, blocks.at[i], rows)
    total = total_in[...] + bias[...]
    for i in range(2):
        for get in gets[i]:
            get.wait()
        total += jnp.dot(cols[i], blocks[i], preferred_element_type=jnp.float32)
    keys[...] = total.astype(keys.dtype)
    for put in puts:
        put.wait()


VMEM = pl.BlockSpec(memory_space=pltpu.VMEM)
SMEM = pl.BlockSpec(memory_space=pltpu.SMEM)
HBM = pl.BlockSpec(memory_space=pltpu.HBM)
LIMIT = pltpu.CompilerParams(vmem_limit_bytes=48 << 20)


def sizes(piece, probes):
    rows = piece.shape[0] // NZ
    return rows, HI * NC * rows, piece.shape[1], probes.shape[0], probes.shape[1]


def cost(flops, moved):
    return pl.CostEstimate(flops=flops, bytes_accessed=moved, transcendentals=0)


def scratch(tokens, depth, heads):
    return [
        pltpu.VMEM((2, depth, heads), jnp.bfloat16),
        pltpu.VMEM((2, tokens, depth), jnp.bfloat16),
        pltpu.SemaphoreType.DMA,
        pltpu.SemaphoreType.DMA((2,)),
    ]


def near_step(place, pieces, probes):
    rows, span, heads, tokens, width = sizes(pieces[0], probes)
    depth = LO * span
    return pl.pallas_call(
        functools.partial(near_kernel, rows),
        out_shape=(
            jax.ShapeDtypeStruct((width, heads), jnp.bfloat16),
            jax.ShapeDtypeStruct((tokens, heads), jnp.float32),
            jax.ShapeDtypeStruct((2 * depth // LANES, LANES), jnp.float32),
        ),
        in_specs=[SMEM, VMEM, VMEM, VMEM, VMEM, HBM],
        out_specs=(HBM, VMEM, VMEM),
        scratch_shapes=scratch(tokens, depth, heads),
        compiler_params=LIMIT,
        cost_estimate=cost(4 * depth * heads * tokens, 4 * depth * (heads + tokens)),
    )(place, *pieces, probes)


def team_sums(place, own, near, width):
    return pl.pallas_call(
        functools.partial(sums_kernel, own.shape[0] // NZ),
        out_shape=jax.ShapeDtypeStruct((NX * NC, width // LANES, LANES), jnp.float32),
        in_specs=[SMEM, VMEM, VMEM],
        out_specs=VMEM,
        compiler_params=LIMIT,
        cost_estimate=cost(16 * own.size, 2 * own.size),
    )(place, own, near)


def last_step(place, pieces, probes, carried, bias):
    rows, span, heads, tokens, width = sizes(pieces[0], probes)
    depth = LO * span
    return pl.pallas_call(
        functools.partial(last_kernel, rows),
        out_shape=(
            jax.ShapeDtypeStruct((width, heads), jnp.bfloat16),
            jax.ShapeDtypeStruct((tokens, heads), jnp.bfloat16),
        ),
        in_specs=[SMEM, VMEM, VMEM, VMEM, VMEM, HBM, VMEM, VMEM, HBM],
        out_specs=(HBM, VMEM),
        scratch_shapes=scratch(tokens, depth, heads),
        input_output_aliases={8: 0},
        compiler_params=LIMIT,
        cost_estimate=cost(4 * depth * heads * tokens, 4 * depth * (heads + tokens)),
    )(place, *pieces, probes, carried[1], bias.reshape(1, -1), carried[0])


def body(master, key_bias, probe_tokens):
    dp = lax.axis_index("dp")
    core = lax.rem(dp, NC)
    y = lax.div(dp, HI * NC)
    back = lax.rem(y + 1 + 2 * core, NY)
    place = jnp.stack([y, back, lax.rem(back + 2, NY), lax.rem(y + 2, NY), core])

    own_rows = jnp.transpose(master).astype(jnp.bfloat16)
    own_rows, place = lax.optimization_barrier((own_rows, place))
    mine = lax.all_gather(own_rows, AXES, axis=0, tiled=True, axis_index_groups=Z_RINGS)
    back = onward(mine)
    ahead = contrary(mine)
    far = onward(back)
    mine_other = swap(mine)
    ahead_other = swap(back)
    back_other = swap(ahead)
    far_other = swap(far)

    near = near_step(place, (mine, mine_other, back, back_other), probe_tokens)
    sums = team_sums(place, far, near[2], probe_tokens.shape[1])
    gathered = lax.all_to_all(
        sums, AXES, split_axis=0, concat_axis=0, tiled=True, axis_index_groups=TEAMS
    )
    weight, probe_keys = last_step(
        place, (ahead, ahead_other, far, far_other), probe_tokens, near, key_bias
    )
    checksum = gathered.sum(axis=0).reshape(-1)
    return (weight, probe_keys, checksum)


def solution(mesh):
    placed = (P("tp", ("role", "dp")), P("tp"), P(("role", "dp"), None))
    return jax.shard_map(
        body,
        mesh=mesh,
        in_specs=placed,
        out_specs=(P(None, "tp"), P(("role", "dp"), "tp"), P()),
        check_vma=False,
    )
```

time: 199 us -> 90.1 us (0.45)
  the two profiles are of different devices: /device:TPU:6 before, /device:TPU:1 now
where the time goes in v5:
time: 90.1 us; the launch traced here: 89.6 us
  blocking collectives  42.6 us (47%)
  starting transfers between devices  30.2 us (34%)
  Pallas kernels  9.88 us (11%)
  waiting for transfers between devices  4.64 us (5%)
  other arithmetic  1.48 us (2%)
    all_gather x1, blocking collectives, body(): lax.all_gather(own_rows, AXES, axis=0, tiled=True, axis_index_groups=Z_RI...  31.9 us
    ppermute x4, starting transfers between devices, swap(): return lax.ppermute(value, AXES, SWAP)  21.7 us
    all_to_all x1, blocking collectives, body(): lax.all_to_all(sums, AXES, split_axis=0, concat_axis=0, tiled=True, axis_...  10.7 us
    ppermute x2, starting transfers between devices, onward(): return lax.ppermute(value, AXES, ONWARD)  5.11 us
    ppermute x2, waiting for transfers between devices, onward(): return lax.ppermute(value, AXES, ONWARD)  4.63 us
    pallas_call x1, Pallas kernels, last_step(): pl.pallas_call(functools.partial(last_kernel, rows), out_shape=(jax.Shape...  4.56 us
    pallas_call x1, Pallas kernels, near_step(): pl.pallas_call(functools.partial(near_kernel, rows), out_shape=(jax.Shape...  4.44 us
    ppermute x1, starting transfers between devices, contrary(): return lax.ppermute(value, AXES, CONTRARY)  3.36 us
  transfers between devices with their start and end apart: 7, of which 1 were waited for; matrix products, arithmetic and copies ran while one was open for 1% of the time, Pallas kernels for 6%

profile of v5, /device:TPU:1, one launch (start us, length us, event | category | flops | bytes accessed | tf_op | source)
XLA Modules:
  0.0 89.6 jit_solution(8871285537001416173)
XLA Ops:
  0.7 0.8 convert_bitcast_fusion
  1.5 0.1 stack.23.place
  1.6 0.0 copy-start
  1.6 31.9 %all_gather.3.own = bf16[1024,256]{1,0:T(8,128)(2,1)S(1)} all-gather(bf16[64,256]{1,0:T(8,128)(2,1)S(1)} %convert_bitcast_fusion), channel_id=1, replica_groups={{0,128,256,384,2,130,258,386,4,132,260,388,6,134,262,390},{1,129,257,38..., dimensions={0}, use_global_device_ids=true | all-gather | bytes 557056 | tf_op jit(solution)/shard_map/all_gather | solution.py:259
  33.5 3.2 %collective-permute-start.1 = (bf16[1024,256]{1,0:T(8,128)(2,1)S(1)}, bf16[1024,256]{1,0:T(8,128)(2,1)S(1)}, u32[]{:S(2)}, u32[]{:S(2)}) collective-permute-start(bf16[1024,256]{1,0:T(8,128)(2,1)S(1)} %all_gather.3.own), channel_id=1, source_target_pairs={{0,24},{1,9},{128,152},{129,137},{256,280},{257,265},{384,408},{38... | collective-permute-start | bytes 1572872 | tf_op jit(solution)/shard_map/ppermute | solution.py:42
  36.7 3.4 %collective-permute-start = (bf16[1024,256]{1,0:T(8,128)(2,1)S(1)}, bf16[1024,256]{1,0:T(8,128)(2,1)S(1)}, u32[]{:S(2)}, u32[]{:S(2)}) collective-permute-start(bf16[1024,256]{1,0:T(8,128)(2,1)S(1)} %all_gather.3.own), channel_id=1, source_target_pairs={{0,8},{1,25},{128,136},{129,153},{256,264},{257,281},{384,392},{38... | collective-permute-start | bytes 1572872 | tf_op jit(solution)/shard_map/ppermute | solution.py:46
  40.1 4.6 %collective-permute-done.1.own_b = bf16[1024,256]{1,0:T(8,128)(2,1)S(1)} collective-permute-done((bf16[1024,256]{1,0:T(8,128)(2,1)S(1)}, bf16[1024,256]{1,0:T(8,128)(2,1)S(1)}, u32[]{:S(2)}, u32[]{:S(2)}) %collective-permute-start.1) | collective-permute-done | bytes 524320 | tf_op jit(solution)/shard_map/ppermute | solution.py:42
  44.7 1.9 %collective-permute-start.3 = (bf16[1024,256]{1,0:T(8,128)(2,1)S(1)}, bf16[1024,256]{1,0:T(8,128)(2,1)S(1)}, u32[]{:S(2)}, u32[]{:S(2)}) collective-permute-start(bf16[1024,256]{1,0:T(8,128)(2,1)S(1)} %collective-permute-done.1.own_b), channel_id=1, source_target_pairs={{0,24},{1,9},{128,152},{129,137},{256,280},{257,265},{384,408},{38... | collective-permute-start | bytes 1572872 | tf_op jit(solution)/shard_map/ppermute | solution.py:42
  46.6 14.2 %collective-permute-start.5 = (bf16[1024,256]{1,0:T(8,128)(2,1)S(1)}, bf16[1024,256]{1,0:T(8,128)(2,1)S(1)}, u32[]{:S(2)}, u32[]{:S(2)}) collective-permute-start(bf16[1024,256]{1,0:T(8,128)(2,1)S(1)} %all_gather.3.own), channel_id=1, source_target_pairs={{0,1},{1,0},{128,129},{129,128},{256,257},{257,256},{384,385},{385... | collective-permute-start | bytes 1572872 | tf_op jit(solution)/shard_map/ppermute | solution.py:50
  60.8 0.0 collective-permute-done.own
  60.9 3.2 %collective-permute-start.6 = (bf16[1024,256]{1,0:T(8,128)(2,1)S(1)}, bf16[1024,256]{1,0:T(8,128)(2,1)S(1)}, u32[]{:S(2)}, u32[]{:S(2)}) collective-permute-start(bf16[1024,256]{1,0:T(8,128)(2,1)S(1)} %collective-permute-done.own), channel_id=1, source_target_pairs={{0,1},{1,0},{128,129},{129,128},{256,257},{257,256},{384,385},{385... | collective-permute-start | bytes 1572872 | tf_op jit(solution)/shard_map/ppermute | solution.py:50
  64.0 1.9 %collective-permute-start.2 = (bf16[1024,256]{1,0:T(8,128)(2,1)S(1)}, bf16[1024,256]{1,0:T(8,128)(2,1)S(1)}, u32[]{:S(2)}, u32[]{:S(2)}) collective-permute-start(bf16[1024,256]{1,0:T(8,128)(2,1)S(1)} %collective-permute-done.1.own_b), channel_id=1, source_target_pairs={{0,1},{1,0},{128,129},{129,128},{256,257},{257,256},{384,385},{385... | collective-permute-start | bytes 1572872 | tf_op jit(solution)/shard_map/ppermute | solution.py:50
  66.0 0.0 collective-permute-done.3.own_f.own
  66.0 2.4 %collective-permute-start.4 = (bf16[1024,256]{1,0:T(8,128)(2,1)S(1)}, bf16[1024,256]{1,0:T(8,128)(2,1)S(1)}, u32[]{:S(2)}, u32[]{:S(2)}) collective-permute-start(bf16[1024,256]{1,0:T(8,128)(2,1)S(1)} %collective-permute-done.3.own_f.own), channel_id=1, source_target_pairs={{0,1},{1,0},{128,129},{129,128},{256,257},{257,256},{384,385},{385... | collective-permute-start | bytes 1572872 | tf_op jit(solution)/shard_map/ppermute | solution.py:50
  68.4 0.0 collective-permute-done.5.other
  68.4 0.0 collective-permute-done.6.other_b
  68.4 4.4 %shard_map.58 = (bf16[8192,256]{1,0:T(8,128)(2,1)}, f32[256,256]{1,0:T(8,128)S(1)}, f32[32,128]{1,0:T(8,128)S(1)}) custom-call(s32[5]{0:T(128)S(1)} %stack.23.place, bf16[1024,256]{1,0:T(8,128)(2,1)S(1)} %all_gather.3.own, bf16[1024,256]{1,0:T(8,128)(2,1)S(1)} %collective-permute-done.5.other, bf16[1024,256]{1,0:T(8,128)(2,1)S(1)} %collective-permute-done.1.own_b, ...), custom_call_target="tpu_custom_call" | custom-call | flops 536870912 | bytes 4194304 | tf_op jit(solution)/shard_map/pallas_call | solution.py:206
  72.9 0.9 shard_map.60
  73.7 10.7 %all_to_all.5 = f32[8,64,128]{2,1,0:T(8,128)S(1)} all-to-all(f32[8,64,128]{2,1,0:T(8,128)S(1)} %shard_map.60), channel_id=1, replica_groups={{0,1,32,33,64,65,96,97},{128,129,160,161,192,193,224,225},{256,257,288,..., dimensions={0} | all-to-all | bytes 524288 | tf_op jit(solution)/shard_map/all_to_all | solution.py:270
  84.4 0.6 reduce_sum.9
  85.1 0.0 collective-permute-done.2.other
  85.1 0.0 collective-permute-done.4.other_f
  85.1 0.0 copy-done
  85.1 4.6 %shard_map.59 = (bf16[8192,256]{1,0:T(8,128)(2,1)}, bf16[256,256]{1,0:T(8,128)(2,1)}) custom-call(s32[5]{0:T(128)S(1)} %stack.23.place, bf16[1024,256]{1,0:T(8,128)(2,1)S(1)} %collective-permute-done.own, bf16[1024,256]{1,0:T(8,128)(2,1)S(1)} %collective-permute-done.2.other, ...), custom_call_target="tpu_custom_call", output_to_operand_aliasing={{0}: (8, {})} | custom-call | flops 536870912 | bytes 4194304 | tf_op jit(solution)/shard_map/pallas_call | solution.py:235
Async XLA Ops:
  1.6 83.5 %copy-start = (f32[256]{0:T(256)S(1)}, f32[256]{0:T(256)}, u32[]{:S(2)}) copy-start(f32[256]{0:T(256)} %param.4) | copy-start | bytes 3076
  33.5 11.2 %collective-permute-start.1 = (bf16[1024,256]{1,0:T(8,128)(2,1)S(1)}, bf16[1024,256]{1,0:T(8,128)(2,1)S(1)}, u32[]{:S(2)}, u32[]{:S(2)}) collective-permute-start(bf16[1024,256]{1,0:T(8,128)(2,1)S(1)} %all_gather.3.own), channel_id=1, source_target_pairs={{0,24},{1,9},{128,152},{129,137},{256,280},{257,265},{384,408},{38... | collective-permute-start | bytes 1572872 | tf_op jit(solution)/shard_map/ppermute | solution.py:42
  36.7 24.1 %collective-permute-start = (bf16[1024,256]{1,0:T(8,128)(2,1)S(1)}, bf16[1024,256]{1,0:T(8,128)(2,1)S(1)}, u32[]{:S(2)}, u32[]{:S(2)}) collective-permute-start(bf16[1024,256]{1,0:T(8,128)(2,1)S(1)} %all_gather.3.own), channel_id=1, source_target_pairs={{0,8},{1,25},{128,136},{129,153},{256,264},{257,281},{384,392},{38... | collective-permute-start | bytes 1572872 | tf_op jit(solution)/shard_map/ppermute | solution.py:46
  44.7 21.3 %collective-permute-start.3 = (bf16[1024,256]{1,0:T(8,128)(2,1)S(1)}, bf16[1024,256]{1,0:T(8,128)(2,1)S(1)}, u32[]{:S(2)}, u32[]{:S(2)}) collective-permute-start(bf16[1024,256]{1,0:T(8,128)(2,1)S(1)} %collective-permute-done.1.own_b), channel_id=1, source_target_pairs={{0,24},{1,9},{128,152},{129,137},{256,280},{257,265},{384,408},{38... | collective-permute-start | bytes 1572872 | tf_op jit(solution)/shard_map/ppermute | solution.py:42
  46.6 21.8 %collective-permute-start.5 = (bf16[1024,256]{1,0:T(8,128)(2,1)S(1)}, bf16[1024,256]{1,0:T(8,128)(2,1)S(1)}, u32[]{:S(2)}, u32[]{:S(2)}) collective-permute-start(bf16[1024,256]{1,0:T(8,128)(2,1)S(1)} %all_gather.3.own), channel_id=1, source_target_pairs={{0,1},{1,0},{128,129},{129,128},{256,257},{257,256},{384,385},{385... | collective-permute-start | bytes 1572872 | tf_op jit(solution)/shard_map/ppermute | solution.py:50
  60.9 7.5 %collective-permute-start.6 = (bf16[1024,256]{1,0:T(8,128)(2,1)S(1)}, bf16[1024,256]{1,0:T(8,128)(2,1)S(1)}, u32[]{:S(2)}, u32[]{:S(2)}) collective-permute-start(bf16[1024,256]{1,0:T(8,128)(2,1)S(1)} %collective-permute-done.own), channel_id=1, source_target_pairs={{0,1},{1,0},{128,129},{129,128},{256,257},{257,256},{384,385},{385... | collective-permute-start | bytes 1572872 | tf_op jit(solution)/shard_map/ppermute | solution.py:50
  64.0 21.0 %collective-permute-start.2 = (bf16[1024,256]{1,0:T(8,128)(2,1)S(1)}, bf16[1024,256]{1,0:T(8,128)(2,1)S(1)}, u32[]{:S(2)}, u32[]{:S(2)}) collective-permute-start(bf16[1024,256]{1,0:T(8,128)(2,1)S(1)} %collective-permute-done.1.own_b), channel_id=1, source_target_pairs={{0,1},{1,0},{128,129},{129,128},{256,257},{257,256},{384,385},{385... | collective-permute-start | bytes 1572872 | tf_op jit(solution)/shard_map/ppermute | solution.py:50
  66.0 19.1 %collective-permute-start.4 = (bf16[1024,256]{1,0:T(8,128)(2,1)S(1)}, bf16[1024,256]{1,0:T(8,128)(2,1)S(1)}, u32[]{:S(2)}, u32[]{:S(2)}) collective-permute-start(bf16[1024,256]{1,0:T(8,128)(2,1)S(1)} %collective-permute-done.3.own_f.own), channel_id=1, source_target_pairs={{0,1},{1,0},{128,129},{129,128},{256,257},{257,256},{384,385},{385... | collective-permute-start | bytes 1572872 | tf_op jit(solution)/shard_map/ppermute | solution.py:50

commit v6 on v5

--- a/solution.py
+++ b/solution.py
@@ -99,33 +99,37 @@
     return puts
 
 
-def line_sums(block, sums, first):
+def line_sums(block, sums):
     s = row_sums(block)
     for j in range(s.shape[1] // LANES):
-        sums[first + j, :] = s[0, j * LANES : (j + 1) * LANES]
-
-
-def near_kernel(rows, place, own, other, own_b, other_b, probes, weight, total, sums, *refs):
-    blocks, cols, put_sem, get_sem = refs
-    gets = [fetch(place, which, probes, cols.at[i], get_sem.at[i]) for i, which in enumerate((SAME, BACK))]
-    puts = put_rows(place, SAME, own, other, weight, rows, put_sem)
-    puts += put_rows(place, BACK, own_b, other_b, weight, rows, put_sem)
-    core = place[CORE]
-    for i, (mine, partner) in enumerate(((own, other), (own_b, other_b))):
-        block = blocks.at[i]
-        assemble(core, mine, block, rows)
-        assemble(1 - core, partner, block, rows)
-        line_sums(block, sums, i * (block.shape[0] // LANES))
-    for i in range(2):
-        for get in gets[i]:
-            get.wait()
-        part = jnp.dot(cols[i], blocks[i], preferred_element_type=jnp.float32)
-        total[...] = part if i == 0 else total[...] + part
+        sums[j, :] = s[0, j * LANES : (j + 1) * LANES]
+
+
+def fetch_kernel(place, probes, same, back, sem):
+    gets = []
+    for which, cols in ((SAME, same), (BACK, back)):
+        gets += fetch(place, which, probes, cols, sem)
+    for get in gets:
+        get.wait()
+
+
+def near_kernel(which, rows, place, own, other, cols, *refs):
+    total_in = None
+    if which == SAME:
+        weight, total, sums, block, put_sem = refs
+    else:
+        total_in, _, weight, total, sums, block, put_sem = refs
+    puts = put_rows(place, which, own, other, weight, rows, put_sem)
+    assemble(place[CORE], own, block, rows)
+    assemble(1 - place[CORE], other, block, rows)
+    line_sums(block, sums)
+    part = jnp.dot(cols[...], block[...], preferred_element_type=jnp.float32)
+    total[...] = part if total_in is None else total_in[...] + part
     for put in puts:
         put.wait()
 
 
-def sums_kernel(rows, place, own, near, sums):
+def sums_kernel(rows, place, own, same, back, sums):
     lines = HI * NC * rows // LANES
     core = place[CORE]
     ones = jnp.ones((8, own.shape[1]), own.dtype)
@@ -134,14 +138,14 @@
     )
     lane = lax.broadcasted_iota(jnp.int32, (1, LANES), 1)
     my_half = (lane // rows) == core
-    own_part = near[: LO * lines, :] * (core == 0).astype(jnp.float32)
+    own_part = same[...] * (core == 0).astype(jnp.float32)
     nothing = jnp.zeros((lines, LANES), jnp.float32)
     for lo in range(LO):
         sums[0, pl.ds((lo * NY + place[SAME]) * lines, lines), :] = own_part[
             lo * lines : (lo + 1) * lines, :
         ]
-        sums[0, pl.ds((lo * NY + place[BACK]) * lines, lines), :] = near[
-            (LO + lo) * lines : (LO + lo + 1) * lines, :
+        sums[0, pl.ds((lo * NY + place[BACK]) * lines, lines), :] = back[
+            lo * lines : (lo + 1) * lines, :
         ]
         sums[0, pl.ds((lo * NY + place[AHEAD]) * lines, lines), :] = nothing
     for pair in range(NZ // 2):
@@ -179,7 +183,8 @@
 VMEM = pl.BlockSpec(memory_space=pltpu.VMEM)
 SMEM = pl.BlockSpec(memory_space=pltpu.SMEM)
 HBM = pl.BlockSpec(memory_space=pltpu.HBM)
-LIMIT = pltpu.CompilerParams(vmem_limit_bytes=48 << 20)
+LIMIT = pltpu.CompilerParams(vmem_limit_bytes=49 << 20)
+SMALL = pltpu.CompilerParams(vmem_limit_bytes=16 << 20)
 
 
 def sizes(piece, probes):
@@ -191,42 +196,48 @@
     return pl.CostEstimate(flops=flops, bytes_accessed=moved, transcendentals=0)
 
 
-def scratch(tokens, depth, heads):
-    return [
-        pltpu.VMEM((2, depth, heads), jnp.bfloat16),
-        pltpu.VMEM((2, tokens, depth), jnp.bfloat16),
-        pltpu.SemaphoreType.DMA,
-        pltpu.SemaphoreType.DMA((2,)),
-    ]
-
-
-def near_step(place, pieces, probes):
-    rows, span, heads, tokens, width = sizes(pieces[0], probes)
-    depth = LO * span
+def fetch_step(place, probes, depth):
+    tokens = probes.shape[0]
     return pl.pallas_call(
-        functools.partial(near_kernel, rows),
+        fetch_kernel,
+        out_shape=[jax.ShapeDtypeStruct((tokens, depth), jnp.bfloat16)] * 2,
+        in_specs=[SMEM, HBM],
+        out_specs=[VMEM] * 2,
+        scratch_shapes=[pltpu.SemaphoreType.DMA],
+        compiler_params=LIMIT,
+        cost_estimate=cost(tokens * depth * 1000, 8 * tokens * depth),
+    )(place, probes)
+
+
+def near_step(place, which, own, other, cols, width, carried=None):
+    tokens, depth = cols.shape
+    heads = own.shape[1]
+    first = carried is None
+    return pl.pallas_call(
+        functools.partial(near_kernel, which, own.shape[0] // NZ),
         out_shape=(
             jax.ShapeDtypeStruct((width, heads), jnp.bfloat16),
             jax.ShapeDtypeStruct((tokens, heads), jnp.float32),
-            jax.ShapeDtypeStruct((2 * depth // LANES, LANES), jnp.float32),
+            jax.ShapeDtypeStruct((depth // LANES, LANES), jnp.float32),
         ),
-        in_specs=[SMEM, VMEM, VMEM, VMEM, VMEM, HBM],
+        in_specs=[SMEM, VMEM, VMEM, VMEM] + ([] if first else [VMEM, HBM]),
         out_specs=(HBM, VMEM, VMEM),
-        scratch_shapes=scratch(tokens, depth, heads),
-        compiler_params=LIMIT,
-        cost_estimate=cost(4 * depth * heads * tokens, 4 * depth * (heads + tokens)),
-    )(place, *pieces, probes)
-
-
-def team_sums(place, own, near, width):
+        scratch_shapes=[pltpu.VMEM((depth, heads), jnp.bfloat16), pltpu.SemaphoreType.DMA],
+        input_output_aliases={} if first else {5: 0},
+        compiler_params=SMALL,
+        cost_estimate=cost(2 * depth * heads * tokens, 2 * depth * (heads + tokens)),
+    )(place, own, other, cols, *(() if first else (carried[1], carried[0])))
+
+
+def team_sums(place, own, same, back, width):
     return pl.pallas_call(
         functools.partial(sums_kernel, own.shape[0] // NZ),
         out_shape=jax.ShapeDtypeStruct((NX * NC, width // LANES, LANES), jnp.float32),
-        in_specs=[SMEM, VMEM, VMEM],
+        in_specs=[SMEM, VMEM, VMEM, VMEM],
         out_specs=VMEM,
-        compiler_params=LIMIT,
+        compiler_params=SMALL,
         cost_estimate=cost(16 * own.size, 2 * own.size),
-    )(place, own, near)
+    )(place, own, same, back)
 
 
 def last_step(place, pieces, probes, carried, bias):
@@ -240,7 +251,12 @@
         ),
         in_specs=[SMEM, VMEM, VMEM, VMEM, VMEM, HBM, VMEM, VMEM, HBM],
         out_specs=(HBM, VMEM),
-        scratch_shapes=scratch(tokens, depth, heads),
+        scratch_shapes=[
+            pltpu.VMEM((2, depth, heads), jnp.bfloat16),
+            pltpu.VMEM((2, tokens, depth), jnp.bfloat16),
+            pltpu.SemaphoreType.DMA,
+            pltpu.SemaphoreType.DMA((2,)),
+        ],
         input_output_aliases={8: 0},
         compiler_params=LIMIT,
         cost_estimate=cost(4 * depth * heads * tokens, 4 * depth * (heads + tokens)),
@@ -265,13 +281,16 @@
     back_other = swap(ahead)
     far_other = swap(far)
 
-    near = near_step(place, (mine, mine_other, back, back_other), probe_tokens)
-    sums = team_sums(place, far, near[2], probe_tokens.shape[1])
+    width = probe_tokens.shape[1]
+    cols = fetch_step(place, probe_tokens, 2 * mine.shape[0])
+    s0 = near_step(place, SAME, mine, mine_other, cols[0], width)
+    s1 = near_step(place, BACK, back, back_other, cols[1], width, s0)
+    sums = team_sums(place, far, s0[2], s1[2], width)
     gathered = lax.all_to_all(
         sums, AXES, split_axis=0, concat_axis=0, tiled=True, axis_index_groups=TEAMS
     )
     weight, probe_keys = last_step(
-        place, (ahead, ahead_other, far, far_other), probe_tokens, near, key_bias
+        place, (ahead, ahead_other, far, far_other), probe_tokens, s1, key_bias
     )
     checksum = gathered.sum(axis=0).reshape(-1)
     return (weight, probe_keys, checksum)

time: 90.1 us -> 91.8 us (1.019)
  Pallas kernels: 9.88 us -> 11.7 us
    pallas_call x1 -> x3, Pallas kernels: 4.44 us -> 6.3 us  [the longest x2 4.23 us: near_step(): pl.pallas_call(functools.partial(near_kernel, which, own.shape[0] // NZ),...]
  transfers between devices with their start and end apart: 7 -> 7, of which waited for: 1 -> 1; matrix products, arithmetic and copies ran while one was open for 1% -> 1% of each run, Pallas kernels for 6% -> 8%
where the time goes in v6:
time: 91.8 us; the launch traced here: 91.4 us
  blocking collectives  42.5 us (46%)
  starting transfers between devices  30.2 us (33%)
  Pallas kernels  11.7 us (13%)
  waiting for transfers between devices  4.64 us (5%)
  other arithmetic  1.48 us (2%)
    all_gather x1, blocking collectives, body(): lax.all_gather(own_rows, AXES, axis=0, tiled=True, axis_index_groups=Z_RI...  31.8 us
    ppermute x4, starting transfers between devices, swap(): return lax.ppermute(value, AXES, SWAP)  21.7 us
    all_to_all x1, blocking collectives, body(): lax.all_to_all(sums, AXES, split_axis=0, concat_axis=0, tiled=True, axis_...  10.7 us
    ppermute x2, starting transfers between devices, onward(): return lax.ppermute(value, AXES, ONWARD)  5.11 us
    ppermute x2, waiting for transfers between devices, onward(): return lax.ppermute(value, AXES, ONWARD)  4.63 us
    pallas_call x1, Pallas kernels, last_step(): pl.pallas_call(functools.partial(last_kernel, rows), out_shape=(jax.Shape...  4.57 us
    pallas_call x2, Pallas kernels, near_step(): pl.pallas_call(functools.partial(near_kernel, which, own.shape[0] // NZ),...  4.23 us
    ppermute x1, starting transfers between devices, contrary(): return lax.ppermute(value, AXES, CONTRARY)  3.36 us
  transfers between devices with their start and end apart: 7, of which 1 were waited for; matrix products, arithmetic and copies ran while one was open for 1% of the time, Pallas kernels for 8%

profile of v6, /device:TPU:1, one launch (start us, length us, event | category | flops | bytes accessed | tf_op | source)
XLA Modules:
  0.0 91.4 jit_solution(1026663861902516973)
XLA Ops:
  0.7 0.8 convert_bitcast_fusion
  1.5 0.1 stack.23.place
  1.6 31.8 %all_gather.3.own = bf16[1024,256]{1,0:T(8,128)(2,1)S(1)} all-gather(bf16[64,256]{1,0:T(8,128)(2,1)S(1)} %convert_bitcast_fusion), channel_id=1, replica_groups={{0,128,256,384,2,130,258,386,4,132,260,388,6,134,262,390},{1,129,257,38..., dimensions={0}, use_global_device_ids=true | all-gather | bytes 557056 | tf_op jit(solution)/shard_map/all_gather | solution.py:275
  33.4 3.2 %collective-permute-start.1 = (bf16[1024,256]{1,0:T(8,128)(2,1)S(1)}, bf16[1024,256]{1,0:T(8,128)(2,1)S(1)}, u32[]{:S(2)}, u32[]{:S(2)}) collective-permute-start(bf16[1024,256]{1,0:T(8,128)(2,1)S(1)} %all_gather.3.own), channel_id=1, source_target_pairs={{0,24},{1,9},{128,152},{129,137},{256,280},{257,265},{384,408},{38... | collective-permute-start | bytes 1572872 | tf_op jit(solution)/shard_map/ppermute | solution.py:42
  36.6 3.4 %collective-permute-start = (bf16[1024,256]{1,0:T(8,128)(2,1)S(1)}, bf16[1024,256]{1,0:T(8,128)(2,1)S(1)}, u32[]{:S(2)}, u32[]{:S(2)}) collective-permute-start(bf16[1024,256]{1,0:T(8,128)(2,1)S(1)} %all_gather.3.own), channel_id=1, source_target_pairs={{0,8},{1,25},{128,136},{129,153},{256,264},{257,281},{384,392},{38... | collective-permute-start | bytes 1572872 | tf_op jit(solution)/shard_map/ppermute | solution.py:46
  39.9 4.6 %collective-permute-done.1.own = bf16[1024,256]{1,0:T(8,128)(2,1)S(1)} collective-permute-done((bf16[1024,256]{1,0:T(8,128)(2,1)S(1)}, bf16[1024,256]{1,0:T(8,128)(2,1)S(1)}, u32[]{:S(2)}, u32[]{:S(2)}) %collective-permute-start.1) | collective-permute-done | bytes 524320 | tf_op jit(solution)/shard_map/ppermute | solution.py:42
  44.6 1.9 %collective-permute-start.3 = (bf16[1024,256]{1,0:T(8,128)(2,1)S(1)}, bf16[1024,256]{1,0:T(8,128)(2,1)S(1)}, u32[]{:S(2)}, u32[]{:S(2)}) collective-permute-start(bf16[1024,256]{1,0:T(8,128)(2,1)S(1)} %collective-permute-done.1.own), channel_id=1, source_target_pairs={{0,24},{1,9},{128,152},{129,137},{256,280},{257,265},{384,408},{38... | collective-permute-start | bytes 1572872 | tf_op jit(solution)/shard_map/ppermute | solution.py:42
  46.5 14.2 %collective-permute-start.6 = (bf16[1024,256]{1,0:T(8,128)(2,1)S(1)}, bf16[1024,256]{1,0:T(8,128)(2,1)S(1)}, u32[]{:S(2)}, u32[]{:S(2)}) collective-permute-start(bf16[1024,256]{1,0:T(8,128)(2,1)S(1)} %all_gather.3.own), channel_id=1, source_target_pairs={{0,1},{1,0},{128,129},{129,128},{256,257},{257,256},{384,385},{385... | collective-permute-start | bytes 1572872 | tf_op jit(solution)/shard_map/ppermute | solution.py:50
  60.7 0.0 collective-permute-done.own
  60.7 3.2 %collective-permute-start.5 = (bf16[1024,256]{1,0:T(8,128)(2,1)S(1)}, bf16[1024,256]{1,0:T(8,128)(2,1)S(1)}, u32[]{:S(2)}, u32[]{:S(2)}) collective-permute-start(bf16[1024,256]{1,0:T(8,128)(2,1)S(1)} %collective-permute-done.own), channel_id=1, source_target_pairs={{0,1},{1,0},{128,129},{129,128},{256,257},{257,256},{384,385},{385... | collective-permute-start | bytes 1572872 | tf_op jit(solution)/shard_map/ppermute | solution.py:50
  63.9 1.9 %collective-permute-start.2 = (bf16[1024,256]{1,0:T(8,128)(2,1)S(1)}, bf16[1024,256]{1,0:T(8,128)(2,1)S(1)}, u32[]{:S(2)}, u32[]{:S(2)}) collective-permute-start(bf16[1024,256]{1,0:T(8,128)(2,1)S(1)} %collective-permute-done.1.own), channel_id=1, source_target_pairs={{0,1},{1,0},{128,129},{129,128},{256,257},{257,256},{384,385},{385... | collective-permute-start | bytes 1572872 | tf_op jit(solution)/shard_map/ppermute | solution.py:50
  65.8 0.0 collective-permute-done.3.own_f.own
  65.8 2.4 %collective-permute-start.4 = (bf16[1024,256]{1,0:T(8,128)(2,1)S(1)}, bf16[1024,256]{1,0:T(8,128)(2,1)S(1)}, u32[]{:S(2)}, u32[]{:S(2)}) collective-permute-start(bf16[1024,256]{1,0:T(8,128)(2,1)S(1)} %collective-permute-done.3.own_f.own), channel_id=1, source_target_pairs={{0,1},{1,0},{128,129},{129,128},{256,257},{257,256},{384,385},{385... | collective-permute-start | bytes 1572872 | tf_op jit(solution)/shard_map/ppermute | solution.py:50
  68.3 2.1 %shard_map.58 = (bf16[256,2048]{1,0:T(8,128)(2,1)S(1)}, bf16[256,2048]{1,0:T(8,128)(2,1)S(1)}) custom-call(s32[5]{0:T(128)S(1)} %stack.23.place, bf16[256,8192]{1,0:T(8,128)(2,1)} %probes.3), custom_call_target="tpu_custom_call" | custom-call | flops 524288000 | bytes 4194304 | tf_op jit(solution)/shard_map/pallas_call | solution.py:201
  70.3 0.0 collective-permute-done.6.other
  70.3 2.1 %shard_map.59 = (bf16[8192,256]{1,0:T(8,128)(2,1)}, f32[256,256]{1,0:T(8,128)S(1)}, f32[16,128]{1,0:T(8,128)S(1)}) custom-call(s32[5]{0:T(128)S(1)} %stack.23.place, bf16[1024,256]{1,0:T(8,128)(2,1)S(1)} %all_gather.3.own, bf16[1024,256]{1,0:T(8,128)(2,1)S(1)} %collective-permute-done.6.other, bf16[256,2048]{1,0:T(8,128)(2,1)S(1)} %get-tuple-element.18.cols), custom_call_target="tpu_custom_call" | custom-call | flops 268435456 | bytes 2097152 | tf_op jit(solution)/shard_map/pallas_call | solution.py:216
  72.5 0.0 copy-start
  72.5 0.0 collective-permute-done.5.other
  72.5 2.1 %shard_map.60 = (bf16[8192,256]{1,0:T(8,128)(2,1)}, f32[256,256]{1,0:T(8,128)S(1)}, f32[16,128]{1,0:T(8,128)S(1)}) custom-call(s32[5]{0:T(128)S(1)} %stack.23.place, bf16[1024,256]{1,0:T(8,128)(2,1)S(1)} %collective-permute-done.1.own, bf16[1024,256]{1,0:T(8,128)(2,1)S(1)} %collective-permute-done.5.other, ...), custom_call_target="tpu_custom_call", output_to_operand_aliasing={{0}: (5, {})} | custom-call | flops 268435456 | bytes 2097152 | tf_op jit(solution)/shard_map/pallas_call | solution.py:216
  74.6 0.9 shard_map.62
  75.5 10.7 %all_to_all.5 = f32[8,64,128]{2,1,0:T(8,128)S(1)} all-to-all(f32[8,64,128]{2,1,0:T(8,128)S(1)} %shard_map.62), channel_id=1, replica_groups={{0,1,32,33,64,65,96,97},{128,129,160,161,192,193,224,225},{256,257,288,..., dimensions={0} | all-to-all | bytes 524288 | tf_op jit(solution)/shard_map/all_to_all | solution.py:289
  86.2 0.6 reduce_sum.9
  86.8 0.0 collective-permute-done.2.other
  86.8 0.0 collective-permute-done.4.other_f
  86.8 0.0 copy-done
  86.8 4.6 %shard_map.61 = (bf16[8192,256]{1,0:T(8,128)(2,1)}, bf16[256,256]{1,0:T(8,128)(2,1)}) custom-call(s32[5]{0:T(128)S(1)} %stack.23.place, bf16[1024,256]{1,0:T(8,128)(2,1)S(1)} %collective-permute-done.own, bf16[1024,256]{1,0:T(8,128)(2,1)S(1)} %collective-permute-done.2.other, ...), custom_call_target="tpu_custom_call", output_to_operand_aliasing={{0}: (8, {})} | custom-call | flops 536870912 | bytes 4194304 | tf_op jit(solution)/shard_map/pallas_call | solution.py:246
Async XLA Ops:
  33.4 11.2 %collective-permute-start.1 = (bf16[1024,256]{1,0:T(8,128)(2,1)S(1)}, bf16[1024,256]{1,0:T(8,128)(2,1)S(1)}, u32[]{:S(2)}, u32[]{:S(2)}) collective-permute-start(bf16[1024,256]{1,0:T(8,128)(2,1)S(1)} %all_gather.3.own), channel_id=1, source_target_pairs={{0,24},{1,9},{128,152},{129,137},{256,280},{257,265},{384,408},{38... | collective-permute-start | bytes 1572872 | tf_op jit(solution)/shard_map/ppermute | solution.py:42
  36.6 24.1 %collective-permute-start = (bf16[1024,256]{1,0:T(8,128)(2,1)S(1)}, bf16[1024,256]{1,0:T(8,128)(2,1)S(1)}, u32[]{:S(2)}, u32[]{:S(2)}) collective-permute-start(bf16[1024,256]{1,0:T(8,128)(2,1)S(1)} %all_gather.3.own), channel_id=1, source_target_pairs={{0,8},{1,25},{128,136},{129,153},{256,264},{257,281},{384,392},{38... | collective-permute-start | bytes 1572872 | tf_op jit(solution)/shard_map/ppermute | solution.py:46
  44.6 21.3 %collective-permute-start.3 = (bf16[1024,256]{1,0:T(8,128)(2,1)S(1)}, bf16[1024,256]{1,0:T(8,128)(2,1)S(1)}, u32[]{:S(2)}, u32[]{:S(2)}) collective-permute-start(bf16[1024,256]{1,0:T(8,128)(2,1)S(1)} %collective-permute-done.1.own), channel_id=1, source_target_pairs={{0,24},{1,9},{128,152},{129,137},{256,280},{257,265},{384,408},{38... | collective-permute-start | bytes 1572872 | tf_op jit(solution)/shard_map/ppermute | solution.py:42
  46.5 23.9 %collective-permute-start.6 = (bf16[1024,256]{1,0:T(8,128)(2,1)S(1)}, bf16[1024,256]{1,0:T(8,128)(2,1)S(1)}, u32[]{:S(2)}, u32[]{:S(2)}) collective-permute-start(bf16[1024,256]{1,0:T(8,128)(2,1)S(1)} %all_gather.3.own), channel_id=1, source_target_pairs={{0,1},{1,0},{128,129},{129,128},{256,257},{257,256},{384,385},{385... | collective-permute-start | bytes 1572872 | tf_op jit(solution)/shard_map/ppermute | solution.py:50
  60.7 11.8 %collective-permute-start.5 = (bf16[1024,256]{1,0:T(8,128)(2,1)S(1)}, bf16[1024,256]{1,0:T(8,128)(2,1)S(1)}, u32[]{:S(2)}, u32[]{:S(2)}) collective-permute-start(bf16[1024,256]{1,0:T(8,128)(2,1)S(1)} %collective-permute-done.own), channel_id=1, source_target_pairs={{0,1},{1,0},{128,129},{129,128},{256,257},{257,256},{384,385},{385... | collective-permute-start | bytes 1572872 | tf_op jit(solution)/shard_map/ppermute | solution.py:50
  63.9 22.9 %collective-permute-start.2 = (bf16[1024,256]{1,0:T(8,128)(2,1)S(1)}, bf16[1024,256]{1,0:T(8,128)(2,1)S(1)}, u32[]{:S(2)}, u32[]{:S(2)}) collective-permute-start(bf16[1024,256]{1,0:T(8,128)(2,1)S(1)} %collective-permute-done.1.own), channel_id=1, source_target_pairs={{0,1},{1,0},{128,129},{129,128},{256,257},{257,256},{384,385},{385... | collective-permute-start | bytes 1572872 | tf_op jit(solution)/shard_map/ppermute | solution.py:50
  65.8 21.0 %collective-permute-start.4 = (bf16[1024,256]{1,0:T(8,128)(2,1)S(1)}, bf16[1024,256]{1,0:T(8,128)(2,1)S(1)}, u32[]{:S(2)}, u32[]{:S(2)}) collective-permute-start(bf16[1024,256]{1,0:T(8,128)(2,1)S(1)} %collective-permute-done.3.own_f.own), channel_id=1, source_target_pairs={{0,1},{1,0},{128,129},{129,128},{256,257},{257,256},{384,385},{385... | collective-permute-start | bytes 1572872 | tf_op jit(solution)/shard_map/ppermute | solution.py:50
  72.5 14.4 %copy-start = (f32[256]{0:T(256)S(1)}, f32[256]{0:T(256)}, u32[]{:S(2)}) copy-start(f32[256]{0:T(256)} %param.4) | copy-start | bytes 3076

commit v7 on v4

v7 whole, which is shorter than its diff:
```python
import functools
import itertools

import jax
import jax.numpy as jnp
from jax import lax
from jax.experimental import pallas as pl
from jax.experimental.pallas import tpu as pltpu
from jax.sharding import PartitionSpec as P


AXES = ("role", "tp", "dp")
NX, NY, NZ, NC, LO = 4, 4, 16, 2, 4
HI = NZ // LO
LANES = 128
SAME, BACK, AHEAD, FAR = range(4)
CORE = 4


def index_of(x, y, z, core):
    y, z, core = y % NY, z % NZ, core % NC
    return ((z % LO) * NX + x) * (NY * HI * NC) + (y * HI + z // LO) * NC + core


CHIPS = list(itertools.product(range(NX), range(NY), range(NZ), range(NC)))
Z_RINGS = [
    [index_of(x, y, z, c) for z in range(NZ)]
    for x, y, c in itertools.product(range(NX), range(NY), range(NC))
]


ONWARD = [(index_of(x, y, z, c), index_of(x, y + 2 * c - 1, z, c)) for x, y, z, c in CHIPS]
TEAMS = [
    [index_of(x, y, z, c) for y, c in itertools.product(range(NY), range(NC))]
    for x, z in itertools.product(range(NX), range(NZ))
]
SWAP = [(index_of(x, y, z, c), index_of(x, y, z, c + 1)) for x, y, z, c in CHIPS]


def onward(value):
    return lax.ppermute(value, AXES, ONWARD)


def swap(value):
    return lax.ppermute(value, AXES, SWAP)


def row_of(place, which, lo, span):
    return pl.multiple_of((lo * NY + place[which]) * span, span)


def assemble(core, piece, block, rows):
    span = HI * NC * rows
    for z in range(NZ):
        at = (z % LO) * span + ((z // LO) * NC + core) * rows
        block[pl.ds(pl.multiple_of(at, rows), rows), :] = piece[pl.ds(z * rows, rows), :]


def fetch(place, which, probes, cols, sem):
    span = cols.shape[1] // LO
    gets = []
    for lo in range(LO):
        get = pltpu.make_async_copy(
            probes.at[:, pl.ds(row_of(place, which, lo, span), span)],
            cols.at[:, pl.ds(lo * span, span)],
            sem,
        )
        get.start()
        gets.append(get)
    return gets


def put_rows(place, which, own, other, weight, rows, sem):
    span = HI * NC * rows
    puts = []
    for side, piece in enumerate((own, other)):
        core = place[CORE] if side == 0 else 1 - place[CORE]
        for z in range(NZ):
            at = row_of(place, which, z % LO, span) + ((z // LO) * NC + core) * rows
            put = pltpu.make_async_copy(
                piece.at[pl.ds(z * rows, rows)],
                weight.at[pl.ds(pl.multiple_of(at, rows), rows)],
                sem,
            )
            put.start()
            puts.append(put)
    return puts


def put_block(place, which, block, weight, rows, sem):
    span = HI * NC * rows
    part = NC * rows
    puts = []
    for lo in range(LO):
        for hi in range(HI):
            at = row_of(place, which, lo, span) + hi * part
            put = pltpu.make_async_copy(
                block.at[pl.ds(lo * span + hi * part, part)],
                weight.at[pl.ds(pl.multiple_of(at, part), part)],
                sem,
            )
            put.start()
            puts.append(put)
    return puts


def sums_kernel(own, sums):
    ones = jnp.ones((8, own.shape[1]), own.dtype)
    s = lax.dot_general(
        ones, own[...], (((1,), (1,)), ((), ())), preferred_element_type=jnp.float32
    )
    for copy in range(NX):
        for j in range(s.shape[1] // LANES):
            sums[copy, j : j + 1, :] = s[0:1, j * LANES : (j + 1) * LANES]


def first_kernel(rows, place, own, other, probes, weight, total, cols, block, put_sem, get_sem):
    gets = fetch(place, SAME, probes, cols, get_sem)
    puts = put_rows(place, SAME, own, other, weight, rows, put_sem)
    assemble(place[CORE], own, block, rows)
    assemble(1 - place[CORE], other, block, rows)
    for get in gets:
        get.wait()
    total[...] = jnp.dot(cols[...], block[...], preferred_element_type=jnp.float32)
    for put in puts:
        put.wait()


def back_kernel(rows, place, own, other, probes, parts, total_in, _, weight, total, sums, block, *refs):
    cols, put_sem, get_sem = refs
    gets = fetch(place, BACK, probes, cols, get_sem)
    puts = put_rows(place, BACK, own, other, weight, rows, put_sem)
    assemble(place[CORE], own, block, rows)
    assemble(1 - place[CORE], other, block, rows)
    whole = parts[0]
    for x in range(1, NX):
        whole += parts[x]
    for copy in range(sums.shape[0]):
        sums[copy] = whole
    for get in gets:
        get.wait()
    total[...] = total_in[...] + jnp.dot(
        cols[...], block[...], preferred_element_type=jnp.float32
    )
    for put in puts:
        put.wait()


def ahead_kernel(rows, place, block, probes, total_in, _, weight, total, cols_far, cols, put_sem, get_sem):
    gets = fetch(place, AHEAD, probes, cols, get_sem.at[0])
    later = fetch(place, FAR, probes, cols_far, get_sem.at[1])
    puts = put_block(place, AHEAD, block, weight, rows, put_sem)
    for get in gets:
        get.wait()
    total[...] = total_in[...] + jnp.dot(
        cols[...], block[...], preferred_element_type=jnp.float32
    )
    for copy in puts + later:
        copy.wait()


def order_sums(sums, checksum, rows):
    first_half = lax.broadcasted_iota(jnp.int32, sums.shape[1:], 1) < rows
    for y in range(NY):
        zero, one = sums[y * NC], sums[y * NC + 1]
        lines = (
            jnp.where(first_half, zero, pltpu.roll(one, rows, 1)),
            jnp.where(first_half, pltpu.roll(zero, rows, 1), one),
        )
        for z in range(NZ):
            at = (z % LO * NY + y) * HI + z // LO
            checksum[at : at + 1, :] = lines[z % 2][z // 2 : z // 2 + 1, :]


def last_kernel(rows, place, own, other, cols, sums, total_in, bias, _, weight, keys, checksum, *refs):
    block, put_sem = refs
    puts = put_rows(place, FAR, own, other, weight, rows, put_sem)
    assemble(place[CORE], own, block, rows)
    assemble(1 - place[CORE], other, block, rows)
    total = total_in[...] + jnp.dot(cols[...], block[...], preferred_element_type=jnp.float32)
    keys[...] = (total + bias[...]).astype(keys.dtype)
    order_sums(sums, checksum, rows)
    for put in puts:
        put.wait()


VMEM = pl.BlockSpec(memory_space=pltpu.VMEM)
SMEM = pl.BlockSpec(memory_space=pltpu.SMEM)
HBM = pl.BlockSpec(memory_space=pltpu.HBM)
LIMIT = pltpu.CompilerParams(vmem_limit_bytes=50 << 20)
SMALL = pltpu.CompilerParams(vmem_limit_bytes=16 << 20)


def sizes(piece, probes):
    rows = piece.shape[0] // NZ
    return rows, HI * NC * rows, piece.shape[1], probes.shape[0], probes.shape[1]


def cost(flops, moved):
    return pl.CostEstimate(flops=flops, bytes_accessed=moved, transcendentals=0)


def own_sums(own):
    return pl.pallas_call(
        sums_kernel,
        out_shape=jax.ShapeDtypeStruct((NX, own.shape[0] // LANES, LANES), jnp.float32),
        in_specs=[VMEM],
        out_specs=VMEM,
        compiler_params=SMALL,
        cost_estimate=cost(16 * own.size, 2 * own.size),
    )(own)


def near_scratch(tokens, depth):
    return [
        pltpu.VMEM((tokens, depth), jnp.bfloat16),
        pltpu.SemaphoreType.DMA,
        pltpu.SemaphoreType.DMA,
    ]


def first_step(place, own, other, probes):
    rows, span, heads, tokens, width = sizes(own, probes)
    depth = LO * span
    cols, put_sem, get_sem = near_scratch(tokens, depth)
    return pl.pallas_call(
        functools.partial(first_kernel, rows),
        out_shape=(
            jax.ShapeDtypeStruct((width, heads), jnp.bfloat16),
            jax.ShapeDtypeStruct((tokens, heads), jnp.float32),
        ),
        in_specs=[SMEM, VMEM, VMEM, HBM],
        out_specs=(HBM, VMEM),
        scratch_shapes=[cols, pltpu.VMEM((depth, heads), jnp.bfloat16), put_sem, get_sem],
        compiler_params=LIMIT,
        cost_estimate=cost(2 * depth * heads * tokens, 2 * depth * (heads + tokens)),
    )(place, own, other, probes)


def back_step(place, own, other, probes, parts, carried):
    rows, span, heads, tokens, width = sizes(own, probes)
    depth = LO * span
    return pl.pallas_call(
        functools.partial(back_kernel, rows),
        out_shape=(
            jax.ShapeDtypeStruct((width, heads), jnp.bfloat16),
            jax.ShapeDtypeStruct((tokens, heads), jnp.float32),
            jax.ShapeDtypeStruct((NY * NC, *parts.shape[1:]), jnp.float32),
            jax.ShapeDtypeStruct((depth, heads), jnp.bfloat16),
        ),
        in_specs=[SMEM, VMEM, VMEM, HBM, VMEM, VMEM, HBM],
        out_specs=(HBM, VMEM, VMEM, VMEM),
        scratch_shapes=near_scratch(tokens, depth),
        input_output_aliases={6: 0},
        compiler_params=LIMIT,
        cost_estimate=cost(2 * depth * heads * tokens, 2 * depth * (heads + tokens)),
    )(place, own, other, probes, parts, carried[1], carried[0])


def ahead_step(place, block, probes, carried):
    depth, heads = block.shape
    tokens, width = probes.shape
    return pl.pallas_call(
        functools.partial(ahead_kernel, depth // (NZ * NC)),
        out_shape=(
            jax.ShapeDtypeStruct((width, heads), jnp.bfloat16),
            jax.ShapeDtypeStruct((tokens, heads), jnp.float32),
            jax.ShapeDtypeStruct((tokens, depth), jnp.bfloat16),
        ),
        in_specs=[SMEM, VMEM, HBM, VMEM, HBM],
        out_specs=(HBM, VMEM, VMEM),
        scratch_shapes=[
            pltpu.VMEM((tokens, depth), jnp.bfloat16),
            pltpu.SemaphoreType.DMA,
            pltpu.SemaphoreType.DMA((2,)),
        ],
        input_output_aliases={4: 0},
        compiler_params=LIMIT,
        cost_estimate=cost(2 * depth * heads * tokens, 2 * depth * (heads + 2 * tokens)),
    )(place, block, probes, carried[1], carried[0])


def last_step(place, own, other, cols, sums, carried, bias):
    tokens, depth = cols.shape
    width, heads = carried[0].shape
    return pl.pallas_call(
        functools.partial(last_kernel, own.shape[0] // NZ),
        out_shape=(
            jax.ShapeDtypeStruct((width, heads), jnp.bfloat16),
            jax.ShapeDtypeStruct((tokens, heads), jnp.bfloat16),
            jax.ShapeDtypeStruct((width // LANES, LANES), jnp.float32),
        ),
        in_specs=[SMEM, VMEM, VMEM, VMEM, VMEM, VMEM, VMEM, HBM],
        out_specs=(HBM, VMEM, VMEM),
        scratch_shapes=[pltpu.VMEM((depth, heads), jnp.bfloat16), pltpu.SemaphoreType.DMA],
        input_output_aliases={7: 0},
        compiler_params=SMALL,
        cost_estimate=cost(2 * depth * heads * tokens, 2 * depth * heads),
    )(place, own, other, cols, sums, carried[1], bias.reshape(1, -1), carried[0])


def body(master, key_bias, probe_tokens):
    dp = lax.axis_index("dp")
    core = lax.rem(dp, NC)
    y = lax.div(dp, HI * NC)
    back = lax.rem(y + 1 + 2 * core, NY)
    place = jnp.stack([y, back, lax.rem(back + 2, NY), lax.rem(y + 2, NY), core])

    own_rows = jnp.transpose(master).astype(jnp.bfloat16)
    own_rows, place = lax.optimization_barrier((own_rows, place))
    mine = lax.all_gather(own_rows, AXES, axis=0, tiled=True, axis_index_groups=Z_RINGS)
    back_same = onward(mine)
    mine_other = swap(mine)
    back_other = onward(mine_other)
    far_same = onward(back_same)
    own = own_sums(mine)
    parts = lax.all_to_all(own, "tp", split_axis=0, concat_axis=0, tiled=True)
    s0 = first_step(place, mine, mine_other, probe_tokens)
    *s1, totals, block = back_step(
        place, back_same, back_other, probe_tokens, parts, s0
    )
    ahead = swap(block)
    sums = lax.all_to_all(
        totals, AXES, split_axis=0, concat_axis=0, tiled=True, axis_index_groups=TEAMS
    )
    far_other = swap(far_same)
    *s2, cols_far = ahead_step(place, ahead, probe_tokens, s1)
    weight, probe_keys, checksum = last_step(
        place, far_same, far_other, cols_far, sums, s2, key_bias
    )
    checksum = checksum.reshape(-1)
    return (weight, probe_keys, checksum)


def solution(mesh):
    placed = (P("tp", ("role", "dp")), P("tp"), P(("role", "dp"), None))
    return jax.shard_map(
        body,
        mesh=mesh,
        in_specs=placed,
        out_specs=(P(None, "tp"), P(("role", "dp"), "tp"), P()),
        check_vma=False,
    )
```

time: 98.3 us -> 94.3 us (0.959)
  the two profiles are of different devices: /device:TPU:24 before, /device:TPU:6 now
where the time goes in v7:
time: 94.3 us; the launch traced here: 92.9 us
  blocking collectives  38.5 us (41%)
  starting transfers between devices  28.8 us (31%)
  Pallas kernels  12.1 us (13%)
  waiting for transfers between devices  10.2 us (11%)
  local copies, waits for them, and re-layouts  1.73 us (2%)
    all_gather x1, blocking collectives, body(): lax.all_gather(own_rows, AXES, axis=0, tiled=True, axis_index_groups=Z_RI...  38.5 us
    ppermute x3, starting transfers between devices, onward(): return lax.ppermute(value, AXES, ONWARD)  13.1 us
    ppermute x3, waiting for transfers between devices, onward(): return lax.ppermute(value, AXES, ONWARD)  7.38 us
    ppermute x3, starting transfers between devices, swap(): return lax.ppermute(value, AXES, SWAP)  5.9 us
    all_to_all x1, starting transfers between devices, body(): lax.all_to_all(totals, AXES, split_axis=0, concat_axis=0, tiled=True, axi...  5 us
    all_to_all x1, starting transfers between devices, body(): parts = lax.all_to_all(own, 'tp', split_axis=0, concat_axis=0, tiled=True)  4.77 us
    pallas_call x1, Pallas kernels, back_step(): pl.pallas_call(functools.partial(back_kernel, rows), out_shape=(jax.Shape...  3.57 us
    pallas_call x1, Pallas kernels, ahead_step(): pl.pallas_call(functools.partial(ahead_kernel, depth // (NZ * NC)), out_s...  2.6 us
  transfers between devices with their start and end apart: 8, of which 4 were waited for; matrix products, arithmetic and copies ran while one was open for 0% of the time, Pallas kernels for 6%

profile of v7, /device:TPU:6, one launch (start us, length us, event | category | flops | bytes accessed | tf_op | source)
XLA Modules:
  0.0 92.9 jit_solution(6341072707560756235)
XLA Ops:
  0.7 0.8 convert_bitcast_fusion
  1.5 0.1 stack.23.place
  1.6 38.5 %all_gather.3.own = bf16[1024,256]{1,0:T(8,128)(2,1)S(1)} all-gather(bf16[64,256]{1,0:T(8,128)(2,1)S(1)} %convert_bitcast_fusion), channel_id=1, replica_groups={{0,128,256,384,2,130,258,386,4,132,260,388,6,134,262,390},{1,129,257,38..., dimensions={0}, use_global_device_ids=true | all-gather | bytes 557056 | tf_op jit(solution)/shard_map/all_gather | solution.py:311
  40.1 1.9 %collective-permute-start.3 = (bf16[1024,256]{1,0:T(8,128)(2,1)S(1)}, bf16[1024,256]{1,0:T(8,128)(2,1)S(1)}, u32[]{:S(2)}, u32[]{:S(2)}) collective-permute-start(bf16[1024,256]{1,0:T(8,128)(2,1)S(1)} %all_gather.3.own), channel_id=1, source_target_pairs={{0,1},{1,0},{128,129},{129,128},{256,257},{257,256},{384,385},{385... | collective-permute-start | bytes 1572872 | tf_op jit(solution)/shard_map/ppermute | solution.py:45
  42.0 4.9 %collective-permute-start = (bf16[1024,256]{1,0:T(8,128)(2,1)S(1)}, bf16[1024,256]{1,0:T(8,128)(2,1)S(1)}, u32[]{:S(2)}, u32[]{:S(2)}) collective-permute-start(bf16[1024,256]{1,0:T(8,128)(2,1)S(1)} %all_gather.3.own), channel_id=1, source_target_pairs={{0,24},{1,9},{128,152},{129,137},{256,280},{257,265},{384,408},{38... | collective-permute-start | bytes 1572872 | tf_op jit(solution)/shard_map/ppermute | solution.py:41
  47.0 0.0 collective-permute-done.3.other
  47.0 2.7 %collective-permute-start.4 = (bf16[1024,256]{1,0:T(8,128)(2,1)S(1)}, bf16[1024,256]{1,0:T(8,128)(2,1)S(1)}, u32[]{:S(2)}, u32[]{:S(2)}) collective-permute-start(bf16[1024,256]{1,0:T(8,128)(2,1)S(1)} %collective-permute-done.3.other), channel_id=1, source_target_pairs={{0,24},{1,9},{128,152},{129,137},{256,280},{257,265},{384,408},{38... | collective-permute-start | bytes 1572872 | tf_op jit(solution)/shard_map/ppermute | solution.py:41
  49.6 0.9 shard_map.58
  50.5 4.8 %all-to-all-start = ((f32[4,8,128]{2,1,0:T(8,128)}), f32[4,8,128]{2,1,0:T(8,128)S(1)}, u32[]{:S(2)}, u32[]{:S(2)}) async-start(f32[4,8,128]{2,1,0:T(8,128)} %shard_map.58), calls=%async_computation | async-start | bytes 32768 | tf_op jit(solution)/shard_map/all_to_all | solution.py:317
  55.3 2.6 %shard_map.59 = (bf16[8192,256]{1,0:T(8,128)(2,1)}, f32[256,256]{1,0:T(8,128)S(1)}) custom-call(s32[5]{0:T(128)S(1)} %stack.23.place, bf16[1024,256]{1,0:T(8,128)(2,1)S(1)} %all_gather.3.own, bf16[1024,256]{1,0:T(8,128)(2,1)S(1)} %collective-permute-done.3.other, bf16[256,8192]{1,0:T(8,128)(2,1)} %probes.5), custom_call_target="tpu_custom_call" | custom-call | flops 268435456 | bytes 2097152 | tf_op jit(solution)/shard_map/pallas_call | solution.py:226
  57.8 0.7 all-to-all-done.parts
  58.6 0.0 collective-permute-done.own
  58.6 0.7 collective-permute-done.4.other
  59.3 3.6 %shard_map.60 = (bf16[8192,256]{1,0:T(8,128)(2,1)}, f32[256,256]{1,0:T(8,128)S(1)}, f32[8,8,128]{2,1,0:T(8,128)}, bf16[2048,256]{1,0:T(8,128)(2,1)}) custom-call(s32[5]{0:T(128)S(1)} %stack.23.place, bf16[1024,256]{1,0:T(8,128)(2,1)S(1)} %collective-permute-done.own, ...), custom_call_target="tpu_custom_call", output_to_operand_aliasing={{0}: (6, {})} | custom-call | flops 268435456 | bytes 2097152 | tf_op jit(solution)/shard_map/pallas_call | solution.py:243
  62.8 2.0 %collective-permute-start.5 = (bf16[2048,256]{1,0:T(8,128)(2,1)}, bf16[2048,256]{1,0:T(8,128)(2,1)S(1)}, u32[]{:S(2)}, u32[]{:S(2)}) collective-permute-start(bf16[2048,256]{1,0:T(8,128)(2,1)} %get-tuple-element.21), channel_id=1, source_target_pairs={{0,1},{1,0},{128,129},{129,128},{256,257},{257,256},{384,385},{385... | collective-permute-start | bytes 3145736 | tf_op jit(solution)/shard_map/ppermute | solution.py:45
  64.8 5.5 %collective-permute-start.1 = (bf16[1024,256]{1,0:T(8,128)(2,1)S(1)}, bf16[1024,256]{1,0:T(8,128)(2,1)S(1)}, u32[]{:S(2)}, u32[]{:S(2)}) collective-permute-start(bf16[1024,256]{1,0:T(8,128)(2,1)S(1)} %collective-permute-done.own), channel_id=1, source_target_pairs={{0,24},{1,9},{128,152},{129,137},{256,280},{257,265},{384,408},{38... | collective-permute-start | bytes 1572872 | tf_op jit(solution)/shard_map/ppermute | solution.py:41
  70.4 6.7 %collective-permute-done.1.own = bf16[1024,256]{1,0:T(8,128)(2,1)S(1)} collective-permute-done((bf16[1024,256]{1,0:T(8,128)(2,1)S(1)}, bf16[1024,256]{1,0:T(8,128)(2,1)S(1)}, u32[]{:S(2)}, u32[]{:S(2)}) %collective-permute-start.1) | collective-permute-done | bytes 524320 | tf_op jit(solution)/shard_map/ppermute | solution.py:41
  77.0 2.0 %collective-permute-start.2 = (bf16[1024,256]{1,0:T(8,128)(2,1)S(1)}, bf16[1024,256]{1,0:T(8,128)(2,1)S(1)}, u32[]{:S(2)}, u32[]{:S(2)}) collective-permute-start(bf16[1024,256]{1,0:T(8,128)(2,1)S(1)} %collective-permute-done.1.own), channel_id=1, source_target_pairs={{0,1},{1,0},{128,129},{129,128},{256,257},{257,256},{384,385},{385... | collective-permute-start | bytes 1572872 | tf_op jit(solution)/shard_map/ppermute | solution.py:45
  79.0 5.0 %all-to-all-start.1 = ((f32[8,8,128]{2,1,0:T(8,128)}), f32[8,8,128]{2,1,0:T(8,128)S(1)}, u32[]{:S(2)}, u32[]{:S(2)}) async-start(f32[8,8,128]{2,1,0:T(8,128)} %get-tuple-element.25), calls=%async_computation.1 | async-start | bytes 65536 | tf_op jit(solution)/shard_map/all_to_all | solution.py:323
  84.0 0.0 collective-permute-done.5.block
  84.0 0.0 copy-start.2
  84.1 2.6 %shard_map.61 = (bf16[8192,256]{1,0:T(8,128)(2,1)}, f32[256,256]{1,0:T(8,128)S(1)}, bf16[256,2048]{1,0:T(8,128)(2,1)S(1)}) custom-call(s32[5]{0:T(128)S(1)} %stack.23.place, bf16[2048,256]{1,0:T(8,128)(2,1)S(1)} %collective-permute-done.5.block, bf16[256,8192]{1,0:T(8,128)(2,1)} %probes.5, ...), custom_call_target="tpu_custom_call", output_to_operand_aliasing={{0}: (4, {})} | custom-call | flops 268435456 | bytes 3145728 | tf_op jit(solution)/shard_map/pallas_call | solution.py:263
  86.7 0.0 copy-start
  86.7 0.7 copy-done
  87.4 2.1 %all-to-all-done.1.sums = f32[8,8,128]{2,1,0:T(8,128)S(1)} async-done(((f32[8,8,128]{2,1,0:T(8,128)}), f32[8,8,128]{2,1,0:T(8,128)S(1)}, u32[]{:S(2)}, u32[]{:S(2)}) %all-to-all-start.1) | async-done | bytes 32800 | tf_op jit(solution)/shard_map/all_to_all | solution.py:323
  89.5 0.0 collective-permute-done.2.other
  89.5 0.0 copy-done.2
  89.5 0.0 copy-start.1
  89.5 0.9 %copy-done.1 = f32[256,256]{1,0:T(8,128)S(1)} copy-done((f32[256,256]{1,0:T(8,128)S(1)}, f32[256,256]{1,0:T(8,128)}, u32[]{:S(2)}) %copy-start.1) | copy-done | bytes 262168
  90.5 2.5 %shard_map.62 = (bf16[8192,256]{1,0:T(8,128)(2,1)}, bf16[256,256]{1,0:T(8,128)(2,1)}, f32[64,128]{1,0:T(8,128)}) custom-call(s32[5]{0:T(128)S(1)} %stack.23.place, bf16[1024,256]{1,0:T(8,128)(2,1)S(1)} %collective-permute-done.1.own, bf16[1024,256]{1,0:T(8,128)(2,1)S(1)} %collective-permute-done.2.other, ...), custom_call_target="tpu_custom_call", output_to_operand_aliasing={{0}: (7, {})} | custom-call | flops 268435456 | bytes 1048576 | tf_op jit(solution)/shard_map/pallas_call | solution.py:286
Async XLA Ops:
  40.1 6.8 %collective-permute-start.3 = (bf16[1024,256]{1,0:T(8,128)(2,1)S(1)}, bf16[1024,256]{1,0:T(8,128)(2,1)S(1)}, u32[]{:S(2)}, u32[]{:S(2)}) collective-permute-start(bf16[1024,256]{1,0:T(8,128)(2,1)S(1)} %all_gather.3.own), channel_id=1, source_target_pairs={{0,1},{1,0},{128,129},{129,128},{256,257},{257,256},{384,385},{385... | collective-permute-start | bytes 1572872 | tf_op jit(solution)/shard_map/ppermute | solution.py:45
  42.0 16.5 %collective-permute-start = (bf16[1024,256]{1,0:T(8,128)(2,1)S(1)}, bf16[1024,256]{1,0:T(8,128)(2,1)S(1)}, u32[]{:S(2)}, u32[]{:S(2)}) collective-permute-start(bf16[1024,256]{1,0:T(8,128)(2,1)S(1)} %all_gather.3.own), channel_id=1, source_target_pairs={{0,24},{1,9},{128,152},{129,137},{256,280},{257,265},{384,408},{38... | collective-permute-start | bytes 1572872 | tf_op jit(solution)/shard_map/ppermute | solution.py:41
  47.0 12.3 %collective-permute-start.4 = (bf16[1024,256]{1,0:T(8,128)(2,1)S(1)}, bf16[1024,256]{1,0:T(8,128)(2,1)S(1)}, u32[]{:S(2)}, u32[]{:S(2)}) collective-permute-start(bf16[1024,256]{1,0:T(8,128)(2,1)S(1)} %collective-permute-done.3.other), channel_id=1, source_target_pairs={{0,24},{1,9},{128,152},{129,137},{256,280},{257,265},{384,408},{38... | collective-permute-start | bytes 1572872 | tf_op jit(solution)/shard_map/ppermute | solution.py:41
  50.5 8.1 %all-to-all-start = ((f32[4,8,128]{2,1,0:T(8,128)}), f32[4,8,128]{2,1,0:T(8,128)S(1)}, u32[]{:S(2)}, u32[]{:S(2)}) async-start(f32[4,8,128]{2,1,0:T(8,128)} %shard_map.58), calls=%async_computation | async-start | bytes 32768 | tf_op jit(solution)/shard_map/all_to_all | solution.py:317
  62.8 21.2 %collective-permute-start.5 = (bf16[2048,256]{1,0:T(8,128)(2,1)}, bf16[2048,256]{1,0:T(8,128)(2,1)S(1)}, u32[]{:S(2)}, u32[]{:S(2)}) collective-permute-start(bf16[2048,256]{1,0:T(8,128)(2,1)} %get-tuple-element.21), channel_id=1, source_target_pairs={{0,1},{1,0},{128,129},{129,128},{256,257},{257,256},{384,385},{385... | collective-permute-start | bytes 3145736 | tf_op jit(solution)/shard_map/ppermute | solution.py:45
  64.8 12.2 %collective-permute-start.1 = (bf16[1024,256]{1,0:T(8,128)(2,1)S(1)}, bf16[1024,256]{1,0:T(8,128)(2,1)S(1)}, u32[]{:S(2)}, u32[]{:S(2)}) collective-permute-start(bf16[1024,256]{1,0:T(8,128)(2,1)S(1)} %collective-permute-done.own), channel_id=1, source_target_pairs={{0,24},{1,9},{128,152},{129,137},{256,280},{257,265},{384,408},{38... | collective-permute-start | bytes 1572872 | tf_op jit(solution)/shard_map/ppermute | solution.py:41
  77.0 12.5 %collective-permute-start.2 = (bf16[1024,256]{1,0:T(8,128)(2,1)S(1)}, bf16[1024,256]{1,0:T(8,128)(2,1)S(1)}, u32[]{:S(2)}, u32[]{:S(2)}) collective-permute-start(bf16[1024,256]{1,0:T(8,128)(2,1)S(1)} %collective-permute-done.1.own), channel_id=1, source_target_pairs={{0,1},{1,0},{128,129},{129,128},{256,257},{257,256},{384,385},{385... | collective-permute-start | bytes 1572872 | tf_op jit(solution)/shard_map/ppermute | solution.py:45
  79.0 10.4 %all-to-all-start.1 = ((f32[8,8,128]{2,1,0:T(8,128)}), f32[8,8,128]{2,1,0:T(8,128)S(1)}, u32[]{:S(2)}, u32[]{:S(2)}) async-start(f32[8,8,128]{2,1,0:T(8,128)} %get-tuple-element.25), calls=%async_computation.1 | async-start | bytes 65536 | tf_op jit(solution)/shard_map/all_to_all | solution.py:323
  84.0 5.4 %copy-start.2 = (f32[256]{0:T(256)S(1)}, f32[256]{0:T(256)}, u32[]{:S(2)}) copy-start(f32[256]{0:T(256)} %param.4) | copy-start | bytes 3076
  86.7 0.7 copy-start
  89.5 1.0 %copy-start.1 = (f32[256,256]{1,0:T(8,128)S(1)}, f32[256,256]{1,0:T(8,128)}, u32[]{:S(2)}) copy-start(f32[256,256]{1,0:T(8,128)} %copy-done) | copy-start | bytes 786436

commit v8 on v7

--- a/solution.py
+++ b/solution.py
@@ -159,7 +159,7 @@
         copy.wait()
 
 
-def order_sums(sums, checksum, rows):
+def order_kernel(rows, sums, checksum):
     first_half = lax.broadcasted_iota(jnp.int32, sums.shape[1:], 1) < rows
     for y in range(NY):
         zero, one = sums[y * NC], sums[y * NC + 1]
@@ -172,14 +172,12 @@
             checksum[at : at + 1, :] = lines[z % 2][z // 2 : z // 2 + 1, :]
 
 
-def last_kernel(rows, place, own, other, cols, sums, total_in, bias, _, weight, keys, checksum, *refs):
-    block, put_sem = refs
+def last_kernel(rows, place, own, other, cols, total_in, bias, _, weight, keys, block, put_sem):
     puts = put_rows(place, FAR, own, other, weight, rows, put_sem)
     assemble(place[CORE], own, block, rows)
     assemble(1 - place[CORE], other, block, rows)
     total = total_in[...] + jnp.dot(cols[...], block[...], preferred_element_type=jnp.float32)
     keys[...] = (total + bias[...]).astype(keys.dtype)
-    order_sums(sums, checksum, rows)
     for put in puts:
         put.wait()
 
@@ -280,7 +278,18 @@
     )(place, block, probes, carried[1], carried[0])
 
 
-def last_step(place, own, other, cols, sums, carried, bias):
+def order_sums(sums, rows):
+    return pl.pallas_call(
+        functools.partial(order_kernel, rows),
+        out_shape=jax.ShapeDtypeStruct((sums.size // LANES, LANES), jnp.float32),
+        in_specs=[VMEM],
+        out_specs=VMEM,
+        compiler_params=SMALL,
+        cost_estimate=cost(sums.size, 8 * sums.size),
+    )(sums)
+
+
+def last_step(place, own, other, cols, carried, bias):
     tokens, depth = cols.shape
     width, heads = carried[0].shape
     return pl.pallas_call(
@@ -288,15 +297,14 @@
         out_shape=(
             jax.ShapeDtypeStruct((width, heads), jnp.bfloat16),
             jax.ShapeDtypeStruct((tokens, heads), jnp.bfloat16),
-            jax.ShapeDtypeStruct((width // LANES, LANES), jnp.float32),
         ),
-        in_specs=[SMEM, VMEM, VMEM, VMEM, VMEM, VMEM, VMEM, HBM],
-        out_specs=(HBM, VMEM, VMEM),
+        in_specs=[SMEM, VMEM, VMEM, VMEM, VMEM, VMEM, HBM],
+        out_specs=(HBM, VMEM),
         scratch_shapes=[pltpu.VMEM((depth, heads), jnp.bfloat16), pltpu.SemaphoreType.DMA],
-        input_output_aliases={7: 0},
+        input_output_aliases={6: 0},
         compiler_params=SMALL,
         cost_estimate=cost(2 * depth * heads * tokens, 2 * depth * heads),
-    )(place, own, other, cols, sums, carried[1], bias.reshape(1, -1), carried[0])
+    )(place, own, other, cols, carried[1], bias.reshape(1, -1), carried[0])
 
 
 def body(master, key_bias, probe_tokens):
@@ -325,10 +333,8 @@
     )
     far_other = swap(far_same)
     *s2, cols_far = ahead_step(place, ahead, probe_tokens, s1)
-    weight, probe_keys, checksum = last_step(
-        place, far_same, far_other, cols_far, sums, s2, key_bias
-    )
-    checksum = checksum.reshape(-1)
+    weight, probe_keys = last_step(place, far_same, far_other, cols_far, s2, key_bias)
+    checksum = order_sums(sums, own_rows.shape[0]).reshape(-1)
     return (weight, probe_keys, checksum)
 
 

time: 94.3 us -> 95.4 us (1.012)
  blocking collectives: 38.5 us -> 48.7 us
  starting transfers between devices: 28.8 us -> 23.8 us
  waiting for transfers between devices: 10.2 us -> 8.09 us
  local copies, waits for them, and re-layouts: 1.73 us -> 0.09 us
    all_to_all x0 -> x1, blocking collectives: none -> 10.2 us  [body(): lax.all_to_all(totals, AXES, split_axis=0, concat_axis=0, tiled=True, axi...]
    all_to_all x1 -> x0, starting transfers between devices: 5 us -> none  [body(): lax.all_to_all(totals, AXES, split_axis=0, concat_axis=0, tiled=True, axi...]
    all_to_all x1 -> x0, waiting for transfers between devices: 2.13 us -> none  [body(): lax.all_to_all(totals, AXES, split_axis=0, concat_axis=0, tiled=True, axi...]
    unnamed x6 -> x2, local copies, waits for them, and re-layouts: 1.64 us -> 0.01 us
    pallas_call x1, Pallas kernels: 3.57 us -> 2.59 us  [back_step(): pl.pallas_call(functools.partial(back_kernel, rows), out_shape=(jax.Shape...]
  transfers between devices with their start and end apart: 8 -> 7, of which waited for: 4 -> 3; matrix products, arithmetic and copies ran while one was open for 0% -> 0% of each run, Pallas kernels for 6% -> 7%
where the time goes in v8:
time: 95.4 us; the launch traced here: 94.1 us
  blocking collectives  48.7 us (51%)
  starting transfers between devices  23.8 us (25%)
  Pallas kernels  11.8 us (12%)
  waiting for transfers between devices  8.09 us (8%)
    all_gather x1, blocking collectives, body(): lax.all_gather(own_rows, AXES, axis=0, tiled=True, axis_index_groups=Z_RI...  38.5 us
    ppermute x3, starting transfers between devices, onward(): return lax.ppermute(value, AXES, ONWARD)  13.1 us
    all_to_all x1, blocking collectives, body(): lax.all_to_all(totals, AXES, split_axis=0, concat_axis=0, tiled=True, axi...  10.2 us
    ppermute x3, waiting for transfers between devices, onward(): return lax.ppermute(value, AXES, ONWARD)  7.38 us
    ppermute x3, starting transfers between devices, swap(): return lax.ppermute(value, AXES, SWAP)  5.91 us
    all_to_all x1, starting transfers between devices, body(): parts = lax.all_to_all(own, 'tp', split_axis=0, concat_axis=0, tiled=True)  4.77 us
    pallas_call x1, Pallas kernels, ahead_step(): pl.pallas_call(functools.partial(ahead_kernel, depth // (NZ * NC)), out_s...  2.6 us
    pallas_call x1, Pallas kernels, back_step(): pl.pallas_call(functools.partial(back_kernel, rows), out_shape=(jax.Shape...  2.59 us
  transfers between devices with their start and end apart: 7, of which 3 were waited for; matrix products, arithmetic and copies ran while one was open for 0% of the time, Pallas kernels for 7%

profile of v8, /device:TPU:6, one launch (start us, length us, event | category | flops | bytes accessed | tf_op | source)
XLA Modules:
  0.0 94.1 jit_solution(4300626024596319258)
XLA Ops:
  0.7 0.8 convert_bitcast_fusion
  1.5 0.1 stack.23.place
  1.6 38.5 %all_gather.3.own = bf16[1024,256]{1,0:T(8,128)(2,1)S(1)} all-gather(bf16[64,256]{1,0:T(8,128)(2,1)S(1)} %convert_bitcast_fusion), channel_id=1, replica_groups={{0,128,256,384,2,130,258,386,4,132,260,388,6,134,262,390},{1,129,257,38..., dimensions={0}, use_global_device_ids=true | all-gather | bytes 557056 | tf_op jit(solution)/shard_map/all_gather | solution.py:319
  40.1 1.9 %collective-permute-start.3 = (bf16[1024,256]{1,0:T(8,128)(2,1)S(1)}, bf16[1024,256]{1,0:T(8,128)(2,1)S(1)}, u32[]{:S(2)}, u32[]{:S(2)}) collective-permute-start(bf16[1024,256]{1,0:T(8,128)(2,1)S(1)} %all_gather.3.own), channel_id=1, source_target_pairs={{0,1},{1,0},{128,129},{129,128},{256,257},{257,256},{384,385},{385... | collective-permute-start | bytes 1572872 | tf_op jit(solution)/shard_map/ppermute | solution.py:45
  42.0 4.9 %collective-permute-start = (bf16[1024,256]{1,0:T(8,128)(2,1)S(1)}, bf16[1024,256]{1,0:T(8,128)(2,1)S(1)}, u32[]{:S(2)}, u32[]{:S(2)}) collective-permute-start(bf16[1024,256]{1,0:T(8,128)(2,1)S(1)} %all_gather.3.own), channel_id=1, source_target_pairs={{0,24},{1,9},{128,152},{129,137},{256,280},{257,265},{384,408},{38... | collective-permute-start | bytes 1572872 | tf_op jit(solution)/shard_map/ppermute | solution.py:41
  47.0 0.0 collective-permute-done.3.other
  47.0 2.7 %collective-permute-start.4 = (bf16[1024,256]{1,0:T(8,128)(2,1)S(1)}, bf16[1024,256]{1,0:T(8,128)(2,1)S(1)}, u32[]{:S(2)}, u32[]{:S(2)}) collective-permute-start(bf16[1024,256]{1,0:T(8,128)(2,1)S(1)} %collective-permute-done.3.other), channel_id=1, source_target_pairs={{0,24},{1,9},{128,152},{129,137},{256,280},{257,265},{384,408},{38... | collective-permute-start | bytes 1572872 | tf_op jit(solution)/shard_map/ppermute | solution.py:41
  49.6 0.9 shard_map.58
  50.5 4.8 %all-to-all-start = ((f32[4,8,128]{2,1,0:T(8,128)}), f32[4,8,128]{2,1,0:T(8,128)S(1)}, u32[]{:S(2)}, u32[]{:S(2)}) async-start(f32[4,8,128]{2,1,0:T(8,128)} %shard_map.58), calls=%async_computation | async-start | bytes 32768 | tf_op jit(solution)/shard_map/all_to_all | solution.py:325
  55.3 2.6 %shard_map.59 = (bf16[8192,256]{1,0:T(8,128)(2,1)}, f32[256,256]{1,0:T(8,128)S(1)}) custom-call(s32[5]{0:T(128)S(1)} %stack.23.place, bf16[1024,256]{1,0:T(8,128)(2,1)S(1)} %all_gather.3.own, bf16[1024,256]{1,0:T(8,128)(2,1)S(1)} %collective-permute-done.3.other, bf16[256,8192]{1,0:T(8,128)(2,1)} %probes.5), custom_call_target="tpu_custom_call" | custom-call | flops 268435456 | bytes 2097152 | tf_op jit(solution)/shard_map/pallas_call | solution.py:224
  57.8 0.7 all-to-all-done.parts
  58.6 0.0 collective-permute-done.own
  58.6 0.7 collective-permute-done.4.other
  59.3 2.6 %shard_map.60 = (bf16[8192,256]{1,0:T(8,128)(2,1)}, f32[256,256]{1,0:T(8,128)S(1)}, f32[8,8,128]{2,1,0:T(8,128)S(1)}, bf16[2048,256]{1,0:T(8,128)(2,1)S(1)}) custom-call(s32[5]{0:T(128)S(1)} %stack.23.place, bf16[1024,256]{1,0:T(8,128)(2,1)S(1)} %collective-permute-done.own, ...), custom_call_target="tpu_custom_call", output_to_operand_aliasing={{0}: (6, {})} | custom-call | flops 268435456 | bytes 2097152 | tf_op jit(solution)/shard_map/pallas_call | solution.py:241
  61.9 2.0 %collective-permute-start.5 = (bf16[2048,256]{1,0:T(8,128)(2,1)S(1)}, bf16[2048,256]{1,0:T(8,128)(2,1)S(1)}, u32[]{:S(2)}, u32[]{:S(2)}) collective-permute-start(bf16[2048,256]{1,0:T(8,128)(2,1)S(1)} %get-tuple-element.20), channel_id=1, source_target_pairs={{0,1},{1,0},{128,129},{129,128},{256,257},{257,256},{384,385},{385... | collective-permute-start | bytes 3145736 | tf_op jit(solution)/shard_map/ppermute | solution.py:45
  63.9 5.5 %collective-permute-start.1 = (bf16[1024,256]{1,0:T(8,128)(2,1)S(1)}, bf16[1024,256]{1,0:T(8,128)(2,1)S(1)}, u32[]{:S(2)}, u32[]{:S(2)}) collective-permute-start(bf16[1024,256]{1,0:T(8,128)(2,1)S(1)} %collective-permute-done.own), channel_id=1, source_target_pairs={{0,24},{1,9},{128,152},{129,137},{256,280},{257,265},{384,408},{38... | collective-permute-start | bytes 1572872 | tf_op jit(solution)/shard_map/ppermute | solution.py:41
  69.4 6.7 %collective-permute-done.1.own = bf16[1024,256]{1,0:T(8,128)(2,1)S(1)} collective-permute-done((bf16[1024,256]{1,0:T(8,128)(2,1)S(1)}, bf16[1024,256]{1,0:T(8,128)(2,1)S(1)}, u32[]{:S(2)}, u32[]{:S(2)}) %collective-permute-start.1) | collective-permute-done | bytes 524320 | tf_op jit(solution)/shard_map/ppermute | solution.py:41
  76.1 2.0 %collective-permute-start.2 = (bf16[1024,256]{1,0:T(8,128)(2,1)S(1)}, bf16[1024,256]{1,0:T(8,128)(2,1)S(1)}, u32[]{:S(2)}, u32[]{:S(2)}) collective-permute-start(bf16[1024,256]{1,0:T(8,128)(2,1)S(1)} %collective-permute-done.1.own), channel_id=1, source_target_pairs={{0,1},{1,0},{128,129},{129,128},{256,257},{257,256},{384,385},{385... | collective-permute-start | bytes 1572872 | tf_op jit(solution)/shard_map/ppermute | solution.py:45
  78.1 10.2 %all_to_all.10.sums = f32[8,8,128]{2,1,0:T(8,128)S(1)} all-to-all(f32[8,8,128]{2,1,0:T(8,128)S(1)} %get-tuple-element.28), channel_id=1, replica_groups={{0,1,8,9,16,17,24,25},{128,129,136,137,144,145,152,153},{256,257,264,26..., dimensions={0} | all-to-all | bytes 65536 | tf_op jit(solution)/shard_map/all_to_all | solution.py:331
  88.3 0.7 shard_map.63
  89.0 0.0 collective-permute-done.5.block
  89.0 0.0 copy-start
  89.0 2.6 %shard_map.61 = (bf16[8192,256]{1,0:T(8,128)(2,1)}, f32[256,256]{1,0:T(8,128)S(1)}, bf16[256,2048]{1,0:T(8,128)(2,1)S(1)}) custom-call(s32[5]{0:T(128)S(1)} %stack.23.place, bf16[2048,256]{1,0:T(8,128)(2,1)S(1)} %collective-permute-done.5.block, bf16[256,8192]{1,0:T(8,128)(2,1)} %probes.5, ...), custom_call_target="tpu_custom_call", output_to_operand_aliasing={{0}: (4, {})} | custom-call | flops 268435456 | bytes 3145728 | tf_op jit(solution)/shard_map/pallas_call | solution.py:261
  91.6 0.0 collective-permute-done.2.other
  91.6 0.0 copy-done
  91.6 2.5 %shard_map.62 = (bf16[8192,256]{1,0:T(8,128)(2,1)}, bf16[256,256]{1,0:T(8,128)(2,1)}) custom-call(s32[5]{0:T(128)S(1)} %stack.23.place, bf16[1024,256]{1,0:T(8,128)(2,1)S(1)} %collective-permute-done.1.own, bf16[1024,256]{1,0:T(8,128)(2,1)S(1)} %collective-permute-done.2.other, ...), custom_call_target="tpu_custom_call", output_to_operand_aliasing={{0}: (6, {})} | custom-call | flops 268435456 | bytes 1048576 | tf_op jit(solution)/shard_map/pallas_call | solution.py:295
Async XLA Ops:
  40.1 6.8 %collective-permute-start.3 = (bf16[1024,256]{1,0:T(8,128)(2,1)S(1)}, bf16[1024,256]{1,0:T(8,128)(2,1)S(1)}, u32[]{:S(2)}, u32[]{:S(2)}) collective-permute-start(bf16[1024,256]{1,0:T(8,128)(2,1)S(1)} %all_gather.3.own), channel_id=1, source_target_pairs={{0,1},{1,0},{128,129},{129,128},{256,257},{257,256},{384,385},{385... | collective-permute-start | bytes 1572872 | tf_op jit(solution)/shard_map/ppermute | solution.py:45
  42.0 16.5 %collective-permute-start = (bf16[1024,256]{1,0:T(8,128)(2,1)S(1)}, bf16[1024,256]{1,0:T(8,128)(2,1)S(1)}, u32[]{:S(2)}, u32[]{:S(2)}) collective-permute-start(bf16[1024,256]{1,0:T(8,128)(2,1)S(1)} %all_gather.3.own), channel_id=1, source_target_pairs={{0,24},{1,9},{128,152},{129,137},{256,280},{257,265},{384,408},{38... | collective-permute-start | bytes 1572872 | tf_op jit(solution)/shard_map/ppermute | solution.py:41
  47.0 12.3 %collective-permute-start.4 = (bf16[1024,256]{1,0:T(8,128)(2,1)S(1)}, bf16[1024,256]{1,0:T(8,128)(2,1)S(1)}, u32[]{:S(2)}, u32[]{:S(2)}) collective-permute-start(bf16[1024,256]{1,0:T(8,128)(2,1)S(1)} %collective-permute-done.3.other), channel_id=1, source_target_pairs={{0,24},{1,9},{128,152},{129,137},{256,280},{257,265},{384,408},{38... | collective-permute-start | bytes 1572872 | tf_op jit(solution)/shard_map/ppermute | solution.py:41
  50.5 8.1 %all-to-all-start = ((f32[4,8,128]{2,1,0:T(8,128)}), f32[4,8,128]{2,1,0:T(8,128)S(1)}, u32[]{:S(2)}, u32[]{:S(2)}) async-start(f32[4,8,128]{2,1,0:T(8,128)} %shard_map.58), calls=%async_computation | async-start | bytes 32768 | tf_op jit(solution)/shard_map/all_to_all | solution.py:325
  61.9 27.1 %collective-permute-start.5 = (bf16[2048,256]{1,0:T(8,128)(2,1)S(1)}, bf16[2048,256]{1,0:T(8,128)(2,1)S(1)}, u32[]{:S(2)}, u32[]{:S(2)}) collective-permute-start(bf16[2048,256]{1,0:T(8,128)(2,1)S(1)} %get-tuple-element.20), channel_id=1, source_target_pairs={{0,1},{1,0},{128,129},{129,128},{256,257},{257,256},{384,385},{385... | collective-permute-start | bytes 3145736 | tf_op jit(solution)/shard_map/ppermute | solution.py:45
  63.9 12.2 %collective-permute-start.1 = (bf16[1024,256]{1,0:T(8,128)(2,1)S(1)}, bf16[1024,256]{1,0:T(8,128)(2,1)S(1)}, u32[]{:S(2)}, u32[]{:S(2)}) collective-permute-start(bf16[1024,256]{1,0:T(8,128)(2,1)S(1)} %collective-permute-done.own), channel_id=1, source_target_pairs={{0,24},{1,9},{128,152},{129,137},{256,280},{257,265},{384,408},{38... | collective-permute-start | bytes 1572872 | tf_op jit(solution)/shard_map/ppermute | solution.py:41
  76.1 15.6 %collective-permute-start.2 = (bf16[1024,256]{1,0:T(8,128)(2,1)S(1)}, bf16[1024,256]{1,0:T(8,128)(2,1)S(1)}, u32[]{:S(2)}, u32[]{:S(2)}) collective-permute-start(bf16[1024,256]{1,0:T(8,128)(2,1)S(1)} %collective-permute-done.1.own), channel_id=1, source_target_pairs={{0,1},{1,0},{128,129},{129,128},{256,257},{257,256},{384,385},{385... | collective-permute-start | bytes 1572872 | tf_op jit(solution)/shard_map/ppermute | solution.py:45
  89.0 2.6 %copy-start = (f32[256]{0:T(256)S(1)}, f32[256]{0:T(256)}, u32[]{:S(2)}) copy-start(f32[256]{0:T(256)} %param.4) | copy-start | bytes 3076

commit v9 on v8

--- a/solution.py
+++ b/solution.py
@@ -126,17 +126,22 @@
         put.wait()
 
 
-def back_kernel(rows, place, own, other, probes, parts, total_in, _, weight, total, sums, block, *refs):
-    cols, put_sem, get_sem = refs
-    gets = fetch(place, BACK, probes, cols, get_sem)
-    puts = put_rows(place, BACK, own, other, weight, rows, put_sem)
-    assemble(place[CORE], own, block, rows)
-    assemble(1 - place[CORE], other, block, rows)
+def block_kernel(rows, place, own, other, parts, totals, block, sums, sums_sem):
     whole = parts[0]
     for x in range(1, NX):
         whole += parts[x]
     for copy in range(sums.shape[0]):
         sums[copy] = whole
+    assemble(place[CORE], own, block, rows)
+    assemble(1 - place[CORE], other, block, rows)
+    out = pltpu.make_async_copy(sums, totals, sums_sem)
+    out.start()
+    out.wait()
+
+
+def back_kernel(rows, place, block, probes, total_in, _, weight, total, cols, put_sem, get_sem):
+    gets = fetch(place, BACK, probes, cols, get_sem)
+    puts = put_block(place, BACK, block, weight, rows, put_sem)
     for get in gets:
         get.wait()
     total[...] = total_in[...] + jnp.dot(
@@ -172,14 +177,18 @@
             checksum[at : at + 1, :] = lines[z % 2][z // 2 : z // 2 + 1, :]
 
 
-def last_kernel(rows, place, own, other, cols, total_in, bias, _, weight, keys, block, put_sem):
+def last_kernel(rows, place, own, other, cols, total_in, bias, _, weight, keys, block, made, put_sem, keys_sem):
     puts = put_rows(place, FAR, own, other, weight, rows, put_sem)
     assemble(place[CORE], own, block, rows)
     assemble(1 - place[CORE], other, block, rows)
     total = total_in[...] + jnp.dot(cols[...], block[...], preferred_element_type=jnp.float32)
-    keys[...] = (total + bias[...]).astype(keys.dtype)
-    for put in puts:
+    made[...] = (total + bias[...]).astype(made.dtype)
+    for put in puts[: len(puts) // 2]:
         put.wait()
+    out = pltpu.make_async_copy(made, keys, keys_sem)
+    out.start()
+    for copy in puts[len(puts) // 2 :] + [out]:
+        copy.wait()
 
 
 VMEM = pl.BlockSpec(memory_space=pltpu.VMEM)
@@ -235,24 +244,39 @@
     )(place, own, other, probes)
 
 
-def back_step(place, own, other, probes, parts, carried):
-    rows, span, heads, tokens, width = sizes(own, probes)
-    depth = LO * span
-    return pl.pallas_call(
-        functools.partial(back_kernel, rows),
+def block_step(place, own, other, parts):
+    rows, heads = own.shape[0] // NZ, own.shape[1]
+    shape = (NY * NC, *parts.shape[1:])
+    return pl.pallas_call(
+        functools.partial(block_kernel, rows),
+        out_shape=(
+            jax.ShapeDtypeStruct(shape, jnp.float32),
+            jax.ShapeDtypeStruct((NC * own.shape[0], heads), jnp.bfloat16),
+        ),
+        in_specs=[SMEM, VMEM, VMEM, VMEM],
+        out_specs=(HBM, VMEM),
+        scratch_shapes=[pltpu.VMEM(shape, jnp.float32), pltpu.SemaphoreType.DMA],
+        compiler_params=SMALL,
+        cost_estimate=cost(16 * own.size, 8 * own.size),
+    )(place, own, other, parts)
+
+
+def back_step(place, block, probes, carried):
+    depth, heads = block.shape
+    tokens, width = probes.shape
+    return pl.pallas_call(
+        functools.partial(back_kernel, depth // (NZ * NC)),
         out_shape=(
             jax.ShapeDtypeStruct((width, heads), jnp.bfloat16),
             jax.ShapeDtypeStruct((tokens, heads), jnp.float32),
-            jax.ShapeDtypeStruct((NY * NC, *parts.shape[1:]), jnp.float32),
-            jax.ShapeDtypeStruct((depth, heads), jnp.bfloat16),
-        ),
-        in_specs=[SMEM, VMEM, VMEM, HBM, VMEM, VMEM, HBM],
-        out_specs=(HBM, VMEM, VMEM, VMEM),
+        ),
+        in_specs=[SMEM, VMEM, HBM, VMEM, HBM],
+        out_specs=(HBM, VMEM),
         scratch_shapes=near_scratch(tokens, depth),
-        input_output_aliases={6: 0},
+        input_output_aliases={4: 0},
         compiler_params=LIMIT,
         cost_estimate=cost(2 * depth * heads * tokens, 2 * depth * (heads + tokens)),
-    )(place, own, other, probes, parts, carried[1], carried[0])
+    )(place, block, probes, carried[1], carried[0])
 
 
 def ahead_step(place, block, probes, carried):
@@ -299,8 +323,13 @@
             jax.ShapeDtypeStruct((tokens, heads), jnp.bfloat16),
         ),
         in_specs=[SMEM, VMEM, VMEM, VMEM, VMEM, VMEM, HBM],
-        out_specs=(HBM, VMEM),
-        scratch_shapes=[pltpu.VMEM((depth, heads), jnp.bfloat16), pltpu.SemaphoreType.DMA],
+        out_specs=(HBM, HBM),
+        scratch_shapes=[
+            pltpu.VMEM((depth, heads), jnp.bfloat16),
+            pltpu.VMEM((tokens, heads), jnp.bfloat16),
+            pltpu.SemaphoreType.DMA,
+            pltpu.SemaphoreType.DMA,
+        ],
         input_output_aliases={6: 0},
         compiler_params=SMALL,
         cost_estimate=cost(2 * depth * heads * tokens, 2 * depth * heads),
@@ -324,10 +353,9 @@
     own = own_sums(mine)
     parts = lax.all_to_all(own, "tp", split_axis=0, concat_axis=0, tiled=True)
     s0 = first_step(place, mine, mine_other, probe_tokens)
-    *s1, totals, block = back_step(
-        place, back_same, back_other, probe_tokens, parts, s0
-    )
+    totals, block = block_step(place, back_same, back_other, parts)
     ahead = swap(block)
+    s1 = back_step(place, block, probe_tokens, s0)
     sums = lax.all_to_all(
         totals, AXES, split_axis=0, concat_axis=0, tiled=True, axis_index_groups=TEAMS
     )

time: 95.4 us -> 96.3 us (level)
  the two profiles are of different devices: /device:TPU:6 before, /device:TPU:1 now
where the time goes in v9:
time: 96.3 us; the launch traced here: 95.6 us
  blocking collectives  39.8 us (41%)
  starting transfers between devices  29.2 us (30%)
  Pallas kernels  12.8 us (13%)
  waiting for transfers between devices  11.1 us (12%)
  local copies, waits for them, and re-layouts  1.13 us (1%)
    all_gather x1, blocking collectives, body(): lax.all_gather(own_rows, AXES, axis=0, tiled=True, axis_index_groups=Z_RI...  31.8 us
    ppermute x3, starting transfers between devices, swap(): return lax.ppermute(value, AXES, SWAP)  14.8 us
    ppermute x3, waiting for transfers between devices, onward(): return lax.ppermute(value, AXES, ONWARD)  11.1 us
    ppermute x3, starting transfers between devices, onward(): return lax.ppermute(value, AXES, ONWARD)  9.32 us
    all_to_all x1, blocking collectives, body(): parts = lax.all_to_all(own, 'tp', split_axis=0, concat_axis=0, tiled=True)  8.04 us
    all_to_all x1, starting transfers between devices, body(): lax.all_to_all(totals, AXES, split_axis=0, concat_axis=0, tiled=True, axi...  5.09 us
    pallas_call x1, Pallas kernels, last_step(): pl.pallas_call(functools.partial(last_kernel, own.shape[0] // NZ), out_sh...  2.84 us
    pallas_call x1, Pallas kernels, ahead_step(): pl.pallas_call(functools.partial(ahead_kernel, depth // (NZ * NC)), out_s...  2.59 us
  transfers between devices with their start and end apart: 7, of which 2 were waited for; matrix products, arithmetic and copies ran while one was open for 0% of the time, Pallas kernels for 9%

profile of v9, /device:TPU:1, one launch (start us, length us, event | category | flops | bytes accessed | tf_op | source)
XLA Modules:
  0.0 95.6 jit_solution(13966938803017056129)
XLA Ops:
  0.7 0.8 convert_bitcast_fusion
  1.5 0.1 stack.23.place
  1.6 31.8 %all_gather.3.own = bf16[1024,256]{1,0:T(8,128)(2,1)S(1)} all-gather(bf16[64,256]{1,0:T(8,128)(2,1)S(1)} %convert_bitcast_fusion), channel_id=1, replica_groups={{0,128,256,384,2,130,258,386,4,132,260,388,6,134,262,390},{1,129,257,38..., dimensions={0}, use_global_device_ids=true | all-gather | bytes 557056 | tf_op jit(solution)/shard_map/all_gather | solution.py:348
  33.4 10.1 %collective-permute-start.3 = (bf16[1024,256]{1,0:T(8,128)(2,1)S(1)}, bf16[1024,256]{1,0:T(8,128)(2,1)S(1)}, u32[]{:S(2)}, u32[]{:S(2)}) collective-permute-start(bf16[1024,256]{1,0:T(8,128)(2,1)S(1)} %all_gather.3.own), channel_id=1, source_target_pairs={{0,1},{1,0},{128,129},{129,128},{256,257},{257,256},{384,385},{385... | collective-permute-start | bytes 1572872 | tf_op jit(solution)/shard_map/ppermute | solution.py:45
  43.5 3.2 %collective-permute-start = (bf16[1024,256]{1,0:T(8,128)(2,1)S(1)}, bf16[1024,256]{1,0:T(8,128)(2,1)S(1)}, u32[]{:S(2)}, u32[]{:S(2)}) collective-permute-start(bf16[1024,256]{1,0:T(8,128)(2,1)S(1)} %all_gather.3.own), channel_id=1, source_target_pairs={{0,24},{1,9},{128,152},{129,137},{256,280},{257,265},{384,408},{38... | collective-permute-start | bytes 1572872 | tf_op jit(solution)/shard_map/ppermute | solution.py:41
  46.7 0.0 collective-permute-done.3.other
  46.7 0.0 copy-start
  46.7 3.2 %collective-permute-start.4 = (bf16[1024,256]{1,0:T(8,128)(2,1)S(1)}, bf16[1024,256]{1,0:T(8,128)(2,1)S(1)}, u32[]{:S(2)}, u32[]{:S(2)}) collective-permute-start(bf16[1024,256]{1,0:T(8,128)(2,1)S(1)} %collective-permute-done.3.other), channel_id=1, source_target_pairs={{0,24},{1,9},{128,152},{129,137},{256,280},{257,265},{384,408},{38... | collective-permute-start | bytes 1572872 | tf_op jit(solution)/shard_map/ppermute | solution.py:41
  50.0 0.2 shard_map.58
  50.2 8.0 %all_to_all.10.parts = f32[4,8,128]{2,1,0:T(8,128)S(1)} all-to-all(f32[4,8,128]{2,1,0:T(8,128)S(1)} %shard_map.58), channel_id=1, replica_groups=mesh['role'=4,'tp'=4,'dp'=32] {'tp'}, dimensions={0} | all-to-all | bytes 32768 | tf_op jit(solution)/shard_map/all_to_all | solution.py:354
  58.2 0.0 collective-permute-done.own
  58.2 0.0 copy-done
  58.2 2.2 %collective-permute-done.4.other = bf16[1024,256]{1,0:T(8,128)(2,1)S(1)} collective-permute-done((bf16[1024,256]{1,0:T(8,128)(2,1)S(1)}, bf16[1024,256]{1,0:T(8,128)(2,1)S(1)}, u32[]{:S(2)}, u32[]{:S(2)}) %collective-permute-start.4) | collective-permute-done | bytes 524320 | tf_op jit(solution)/shard_map/ppermute | solution.py:41
  60.4 1.2 %shard_map.59 = (f32[8,8,128]{2,1,0:T(8,128)}, bf16[2048,256]{1,0:T(8,128)(2,1)S(1)}) custom-call(s32[5]{0:T(128)S(1)} %stack.23.place, bf16[1024,256]{1,0:T(8,128)(2,1)S(1)} %collective-permute-done.own, bf16[1024,256]{1,0:T(8,128)(2,1)S(1)} %collective-permute-done.4.other, f32[4,8,128]{2,1,0:T(8,128)S(1)} %all_to_all.10.parts), custom_call_target="tpu_custom_call" | custom-call | flops 4194304 | bytes 2097152 | tf_op jit(solution)/shard_map/pallas_call | solution.py:250
  61.7 2.3 %collective-permute-start.5 = (bf16[2048,256]{1,0:T(8,128)(2,1)S(1)}, bf16[2048,256]{1,0:T(8,128)(2,1)S(1)}, u32[]{:S(2)}, u32[]{:S(2)}) collective-permute-start(bf16[2048,256]{1,0:T(8,128)(2,1)S(1)} %get-tuple-element.18.block), channel_id=1, source_target_pairs={{0,1},{1,0},{128,129},{129,128},{256,257},{257,256},{384,385},{385... | collective-permute-start | bytes 3145736 | tf_op jit(solution)/shard_map/ppermute | solution.py:45
  64.0 2.9 %collective-permute-start.1 = (bf16[1024,256]{1,0:T(8,128)(2,1)S(1)}, bf16[1024,256]{1,0:T(8,128)(2,1)S(1)}, u32[]{:S(2)}, u32[]{:S(2)}) collective-permute-start(bf16[1024,256]{1,0:T(8,128)(2,1)S(1)} %collective-permute-done.own), channel_id=1, source_target_pairs={{0,24},{1,9},{128,152},{129,137},{256,280},{257,265},{384,408},{38... | collective-permute-start | bytes 1572872 | tf_op jit(solution)/shard_map/ppermute | solution.py:41
  66.9 8.9 %collective-permute-done.1.own = bf16[1024,256]{1,0:T(8,128)(2,1)S(1)} collective-permute-done((bf16[1024,256]{1,0:T(8,128)(2,1)S(1)}, bf16[1024,256]{1,0:T(8,128)(2,1)S(1)}, u32[]{:S(2)}, u32[]{:S(2)}) %collective-permute-start.1) | collective-permute-done | bytes 524320 | tf_op jit(solution)/shard_map/ppermute | solution.py:41
  75.8 2.3 %collective-permute-start.2 = (bf16[1024,256]{1,0:T(8,128)(2,1)S(1)}, bf16[1024,256]{1,0:T(8,128)(2,1)}, u32[]{:S(2)}, u32[]{:S(2)}) collective-permute-start(bf16[1024,256]{1,0:T(8,128)(2,1)S(1)} %collective-permute-done.1.own), channel_id=1, source_target_pairs={{0,1},{1,0},{128,129},{129,128},{256,257},{257,256},{384,385},{385... | collective-permute-start | bytes 1572872 | tf_op jit(solution)/shard_map/ppermute | solution.py:45
  78.1 5.1 %all-to-all-start.1 = ((f32[8,8,128]{2,1,0:T(8,128)}), f32[8,8,128]{2,1,0:T(8,128)S(1)}, u32[]{:S(2)}, u32[]{:S(2)}) async-start(f32[8,8,128]{2,1,0:T(8,128)} %get-tuple-element.28), calls=%async_computation.1 | async-start | bytes 65536 | tf_op jit(solution)/shard_map/all_to_all | solution.py:359
  83.2 0.0 copy-start.1
  83.2 1.0 %copy-done.1 = bf16[1024,256]{1,0:T(8,128)(2,1)S(1)} copy-done((bf16[1024,256]{1,0:T(8,128)(2,1)S(1)}, bf16[1024,256]{1,0:T(8,128)(2,1)}, u32[]{:S(2)}) %copy-start.1) | copy-done | bytes 524312
  84.3 2.6 %shard_map.60 = (bf16[8192,256]{1,0:T(8,128)(2,1)}, f32[256,256]{1,0:T(8,128)S(1)}) custom-call(s32[5]{0:T(128)S(1)} %stack.23.place, bf16[1024,256]{1,0:T(8,128)(2,1)S(1)} %all_gather.3.own, bf16[1024,256]{1,0:T(8,128)(2,1)S(1)} %copy-done.1, bf16[256,8192]{1,0:T(8,128)(2,1)} %probes.5), custom_call_target="tpu_custom_call" | custom-call | flops 268435456 | bytes 2097152 | tf_op jit(solution)/shard_map/pallas_call | solution.py:233
  86.8 2.6 %shard_map.61 = (bf16[8192,256]{1,0:T(8,128)(2,1)}, f32[256,256]{1,0:T(8,128)S(1)}) custom-call(s32[5]{0:T(128)S(1)} %stack.23.place, bf16[2048,256]{1,0:T(8,128)(2,1)S(1)} %get-tuple-element.18.block, bf16[256,8192]{1,0:T(8,128)(2,1)} %probes.5, f32[256,256]{1,0:T(8,128)S(1)} %get-tuple-element.19.total_in, ...), custom_call_target="tpu_custom_call", output_to_operand_aliasing={{0}: (4, {})} | custom-call | flops 268435456 | bytes 2097152 | tf_op jit(solution)/shard_map/pallas_call | solution.py:267
  89.4 0.0 all-to-all-done.1.sums
  89.5 0.7 shard_map.64
  90.2 0.0 collective-permute-done.5.block
  90.2 0.0 copy-start.2
  90.2 2.6 %shard_map.62 = (bf16[8192,256]{1,0:T(8,128)(2,1)}, f32[256,256]{1,0:T(8,128)S(1)}, bf16[256,2048]{1,0:T(8,128)(2,1)S(1)}) custom-call(s32[5]{0:T(128)S(1)} %stack.23.place, bf16[2048,256]{1,0:T(8,128)(2,1)S(1)} %collective-permute-done.5.block, bf16[256,8192]{1,0:T(8,128)(2,1)} %probes.5, ...), custom_call_target="tpu_custom_call", output_to_operand_aliasing={{0}: (4, {})} | custom-call | flops 268435456 | bytes 3145728 | tf_op jit(solution)/shard_map/pallas_call | solution.py:285
  92.8 0.0 collective-permute-done.2.other
  92.8 0.0 copy-done.2
  92.8 2.8 %shard_map.63 = (bf16[8192,256]{1,0:T(8,128)(2,1)}, bf16[256,256]{1,0:T(8,128)(2,1)}) custom-call(s32[5]{0:T(128)S(1)} %stack.23.place, bf16[1024,256]{1,0:T(8,128)(2,1)S(1)} %collective-permute-done.1.own, bf16[1024,256]{1,0:T(8,128)(2,1)} %collective-permute-done.2.other, ...), custom_call_target="tpu_custom_call", output_to_operand_aliasing={{0}: (6, {})} | custom-call | flops 268435456 | bytes 1048576 | tf_op jit(solution)/shard_map/pallas_call | solution.py:319
Async XLA Ops:
  33.4 13.4 %collective-permute-start.3 = (bf16[1024,256]{1,0:T(8,128)(2,1)S(1)}, bf16[1024,256]{1,0:T(8,128)(2,1)S(1)}, u32[]{:S(2)}, u32[]{:S(2)}) collective-permute-start(bf16[1024,256]{1,0:T(8,128)(2,1)S(1)} %all_gather.3.own), channel_id=1, source_target_pairs={{0,1},{1,0},{128,129},{129,128},{256,257},{257,256},{384,385},{385... | collective-permute-start | bytes 1572872 | tf_op jit(solution)/shard_map/ppermute | solution.py:45
  43.5 14.7 %collective-permute-start = (bf16[1024,256]{1,0:T(8,128)(2,1)S(1)}, bf16[1024,256]{1,0:T(8,128)(2,1)S(1)}, u32[]{:S(2)}, u32[]{:S(2)}) collective-permute-start(bf16[1024,256]{1,0:T(8,128)(2,1)S(1)} %all_gather.3.own), channel_id=1, source_target_pairs={{0,24},{1,9},{128,152},{129,137},{256,280},{257,265},{384,408},{38... | collective-permute-start | bytes 1572872 | tf_op jit(solution)/shard_map/ppermute | solution.py:41
  46.7 11.5 %copy-start = (bf16[1024,256]{1,0:T(8,128)(2,1)}, bf16[1024,256]{1,0:T(8,128)(2,1)S(1)}, u32[]{:S(2)}) copy-start(bf16[1024,256]{1,0:T(8,128)(2,1)S(1)} %collective-permute-done.3.other) | copy-start | bytes 1572868
  46.7 13.7 %collective-permute-start.4 = (bf16[1024,256]{1,0:T(8,128)(2,1)S(1)}, bf16[1024,256]{1,0:T(8,128)(2,1)S(1)}, u32[]{:S(2)}, u32[]{:S(2)}) collective-permute-start(bf16[1024,256]{1,0:T(8,128)(2,1)S(1)} %collective-permute-done.3.other), channel_id=1, source_target_pairs={{0,24},{1,9},{128,152},{129,137},{256,280},{257,265},{384,408},{38... | collective-permute-start | bytes 1572872 | tf_op jit(solution)/shard_map/ppermute | solution.py:41
  61.7 28.5 %collective-permute-start.5 = (bf16[2048,256]{1,0:T(8,128)(2,1)S(1)}, bf16[2048,256]{1,0:T(8,128)(2,1)S(1)}, u32[]{:S(2)}, u32[]{:S(2)}) collective-permute-start(bf16[2048,256]{1,0:T(8,128)(2,1)S(1)} %get-tuple-element.18.block), channel_id=1, source_target_pairs={{0,1},{1,0},{128,129},{129,128},{256,257},{257,256},{384,385},{385... | collective-permute-start | bytes 3145736 | tf_op jit(solution)/shard_map/ppermute | solution.py:45
  64.0 11.8 %collective-permute-start.1 = (bf16[1024,256]{1,0:T(8,128)(2,1)S(1)}, bf16[1024,256]{1,0:T(8,128)(2,1)S(1)}, u32[]{:S(2)}, u32[]{:S(2)}) collective-permute-start(bf16[1024,256]{1,0:T(8,128)(2,1)S(1)} %collective-permute-done.own), channel_id=1, source_target_pairs={{0,24},{1,9},{128,152},{129,137},{256,280},{257,265},{384,408},{38... | collective-permute-start | bytes 1572872 | tf_op jit(solution)/shard_map/ppermute | solution.py:41
  75.8 17.0 %collective-permute-start.2 = (bf16[1024,256]{1,0:T(8,128)(2,1)S(1)}, bf16[1024,256]{1,0:T(8,128)(2,1)}, u32[]{:S(2)}, u32[]{:S(2)}) collective-permute-start(bf16[1024,256]{1,0:T(8,128)(2,1)S(1)} %collective-permute-done.1.own), channel_id=1, source_target_pairs={{0,1},{1,0},{128,129},{129,128},{256,257},{257,256},{384,385},{385... | collective-permute-start | bytes 1572872 | tf_op jit(solution)/shard_map/ppermute | solution.py:45
  78.1 11.3 %all-to-all-start.1 = ((f32[8,8,128]{2,1,0:T(8,128)}), f32[8,8,128]{2,1,0:T(8,128)S(1)}, u32[]{:S(2)}, u32[]{:S(2)}) async-start(f32[8,8,128]{2,1,0:T(8,128)} %get-tuple-element.28), calls=%async_computation.1 | async-start | bytes 65536 | tf_op jit(solution)/shard_map/all_to_all | solution.py:359
  83.2 1.0 %copy-start.1 = (bf16[1024,256]{1,0:T(8,128)(2,1)S(1)}, bf16[1024,256]{1,0:T(8,128)(2,1)}, u32[]{:S(2)}) copy-start(bf16[1024,256]{1,0:T(8,128)(2,1)} %copy-done) | copy-start | bytes 1572868
  90.2 2.6 %copy-start.2 = (f32[256]{0:T(256)S(1)}, f32[256]{0:T(256)}, u32[]{:S(2)}) copy-start(f32[256]{0:T(256)} %param.4) | copy-start | bytes 3076

commit v10 on v8

--- a/solution.py
+++ b/solution.py
@@ -126,9 +126,10 @@
         put.wait()
 
 
-def back_kernel(rows, place, own, other, probes, parts, total_in, _, weight, total, sums, block, *refs):
-    cols, put_sem, get_sem = refs
+def back_kernel(rows, place, own, other, probes, parts, total_in, _, weight, total, totals, block, *refs):
+    cols_ahead, cols, sums, put_sem, get_sem, sums_sem, ahead_sem = refs
     gets = fetch(place, BACK, probes, cols, get_sem)
+    later = fetch(place, AHEAD, probes, cols_ahead, ahead_sem)
     puts = put_rows(place, BACK, own, other, weight, rows, put_sem)
     assemble(place[CORE], own, block, rows)
     assemble(1 - place[CORE], other, block, rows)
@@ -142,16 +143,15 @@
     total[...] = total_in[...] + jnp.dot(
         cols[...], block[...], preferred_element_type=jnp.float32
     )
-    for put in puts:
-        put.wait()
-
-
-def ahead_kernel(rows, place, block, probes, total_in, _, weight, total, cols_far, cols, put_sem, get_sem):
-    gets = fetch(place, AHEAD, probes, cols, get_sem.at[0])
-    later = fetch(place, FAR, probes, cols_far, get_sem.at[1])
+    out = pltpu.make_async_copy(sums, totals, sums_sem)
+    out.start()
+    for copy in puts + later + [out]:
+        copy.wait()
+
+
+def ahead_kernel(rows, place, block, cols, probes, total_in, _, weight, total, cols_far, put_sem, get_sem):
+    later = fetch(place, FAR, probes, cols_far, get_sem)
     puts = put_block(place, AHEAD, block, weight, rows, put_sem)
-    for get in gets:
-        get.wait()
     total[...] = total_in[...] + jnp.dot(
         cols[...], block[...], preferred_element_type=jnp.float32
     )
@@ -172,14 +172,18 @@
             checksum[at : at + 1, :] = lines[z % 2][z // 2 : z // 2 + 1, :]
 
 
-def last_kernel(rows, place, own, other, cols, total_in, bias, _, weight, keys, block, put_sem):
+def last_kernel(rows, place, own, other, cols, total_in, bias, _, weight, keys, block, made, put_sem, keys_sem):
     puts = put_rows(place, FAR, own, other, weight, rows, put_sem)
     assemble(place[CORE], own, block, rows)
     assemble(1 - place[CORE], other, block, rows)
     total = total_in[...] + jnp.dot(cols[...], block[...], preferred_element_type=jnp.float32)
-    keys[...] = (total + bias[...]).astype(keys.dtype)
-    for put in puts:
+    made[...] = (total + bias[...]).astype(made.dtype)
+    for put in puts[: len(puts) // 2]:
         put.wait()
+    out = pltpu.make_async_copy(made, keys, keys_sem)
+    out.start()
+    for copy in puts[len(puts) // 2 :] + [out]:
+        copy.wait()
 
 
 VMEM = pl.BlockSpec(memory_space=pltpu.VMEM)
@@ -238,6 +242,7 @@
 def back_step(place, own, other, probes, parts, carried):
     rows, span, heads, tokens, width = sizes(own, probes)
     depth = LO * span
+    cols, put_sem, get_sem = near_scratch(tokens, depth)
     return pl.pallas_call(
         functools.partial(back_kernel, rows),
         out_shape=(
@@ -245,17 +250,25 @@
             jax.ShapeDtypeStruct((tokens, heads), jnp.float32),
             jax.ShapeDtypeStruct((NY * NC, *parts.shape[1:]), jnp.float32),
             jax.ShapeDtypeStruct((depth, heads), jnp.bfloat16),
+            jax.ShapeDtypeStruct((tokens, depth), jnp.bfloat16),
         ),
         in_specs=[SMEM, VMEM, VMEM, HBM, VMEM, VMEM, HBM],
-        out_specs=(HBM, VMEM, VMEM, VMEM),
-        scratch_shapes=near_scratch(tokens, depth),
+        out_specs=(HBM, VMEM, HBM, VMEM, VMEM),
+        scratch_shapes=[
+            cols,
+            pltpu.VMEM((NY * NC, *parts.shape[1:]), jnp.float32),
+            put_sem,
+            get_sem,
+            pltpu.SemaphoreType.DMA,
+            pltpu.SemaphoreType.DMA,
+        ],
         input_output_aliases={6: 0},
         compiler_params=LIMIT,
-        cost_estimate=cost(2 * depth * heads * tokens, 2 * depth * (heads + tokens)),
+        cost_estimate=cost(2 * depth * heads * tokens, 2 * depth * (heads + 2 * tokens)),
     )(place, own, other, probes, parts, carried[1], carried[0])
 
 
-def ahead_step(place, block, probes, carried):
+def ahead_step(place, block, cols, probes, carried):
     depth, heads = block.shape
     tokens, width = probes.shape
     return pl.pallas_call(
@@ -265,17 +278,16 @@
             jax.ShapeDtypeStruct((tokens, heads), jnp.float32),
             jax.ShapeDtypeStruct((tokens, depth), jnp.bfloat16),
         ),
-        in_specs=[SMEM, VMEM, HBM, VMEM, HBM],
+        in_specs=[SMEM, VMEM, VMEM, HBM, VMEM, HBM],
         out_specs=(HBM, VMEM, VMEM),
         scratch_shapes=[
-            pltpu.VMEM((tokens, depth), jnp.bfloat16),
-            pltpu.SemaphoreType.DMA,
-            pltpu.SemaphoreType.DMA((2,)),
+            pltpu.SemaphoreType.DMA,
+            pltpu.SemaphoreType.DMA,
         ],
-        input_output_aliases={4: 0},
+        input_output_aliases={5: 0},
         compiler_params=LIMIT,
-        cost_estimate=cost(2 * depth * heads * tokens, 2 * depth * (heads + 2 * tokens)),
-    )(place, block, probes, carried[1], carried[0])
+        cost_estimate=cost(2 * depth * heads * tokens, 2 * depth * (heads + tokens)),
+    )(place, block, cols, probes, carried[1], carried[0])
 
 
 def order_sums(sums, rows):
@@ -299,8 +311,13 @@
             jax.ShapeDtypeStruct((tokens, heads), jnp.bfloat16),
         ),
         in_specs=[SMEM, VMEM, VMEM, VMEM, VMEM, VMEM, HBM],
-        out_specs=(HBM, VMEM),
-        scratch_shapes=[pltpu.VMEM((depth, heads), jnp.bfloat16), pltpu.SemaphoreType.DMA],
+        out_specs=(HBM, HBM),
+        scratch_shapes=[
+            pltpu.VMEM((depth, heads), jnp.bfloat16),
+            pltpu.VMEM((tokens, heads), jnp.bfloat16),
+            pltpu.SemaphoreType.DMA,
+            pltpu.SemaphoreType.DMA,
+        ],
         input_output_aliases={6: 0},
         compiler_params=SMALL,
         cost_estimate=cost(2 * depth * heads * tokens, 2 * depth * heads),
@@ -324,7 +341,7 @@
     own = own_sums(mine)
     parts = lax.all_to_all(own, "tp", split_axis=0, concat_axis=0, tiled=True)
     s0 = first_step(place, mine, mine_other, probe_tokens)
-    *s1, totals, block = back_step(
+    *s1, totals, block, cols_ahead = back_step(
         place, back_same, back_other, probe_tokens, parts, s0
     )
     ahead = swap(block)
@@ -332,7 +349,7 @@
         totals, AXES, split_axis=0, concat_axis=0, tiled=True, axis_index_groups=TEAMS
     )
     far_other = swap(far_same)
-    *s2, cols_far = ahead_step(place, ahead, probe_tokens, s1)
+    *s2, cols_far = ahead_step(place, ahead, cols_ahead, probe_tokens, s1)
     weight, probe_keys = last_step(place, far_same, far_other, cols_far, s2, key_bias)
     checksum = order_sums(sums, own_rows.shape[0]).reshape(-1)
     return (weight, probe_keys, checksum)

time: 95.4 us -> 95.4 us (level)
  no operation moved by 1% of the time
where the time goes in v10:
time: 95.4 us; the launch traced here: 94.1 us
  blocking collectives  48.7 us (51%)
  starting transfers between devices  23.8 us (25%)
  Pallas kernels  11.8 us (12%)
  waiting for transfers between devices  8.09 us (8%)
    all_gather x1, blocking collectives, body(): lax.all_gather(own_rows, AXES, axis=0, tiled=True, axis_index_groups=Z_RI...  38.5 us
    ppermute x3, starting transfers between devices, onward(): return lax.ppermute(value, AXES, ONWARD)  13.1 us
    all_to_all x1, blocking collectives, body(): lax.all_to_all(totals, AXES, split_axis=0, concat_axis=0, tiled=True, axi...  10.2 us
    ppermute x3, waiting for transfers between devices, onward(): return lax.ppermute(value, AXES, ONWARD)  7.38 us
    ppermute x3, starting transfers between devices, swap(): return lax.ppermute(value, AXES, SWAP)  5.91 us
    all_to_all x1, starting transfers between devices, body(): parts = lax.all_to_all(own, 'tp', split_axis=0, concat_axis=0, tiled=True)  4.77 us
    pallas_call x1, Pallas kernels, back_step(): pl.pallas_call(functools.partial(back_kernel, rows), out_shape=(jax.Shape...  2.91 us
    pallas_call x1, Pallas kernels, first_step(): pl.pallas_call(functools.partial(first_kernel, rows), out_shape=(jax.Shap...  2.58 us
  transfers between devices with their start and end apart: 7, of which 3 were waited for; matrix products, arithmetic and copies ran while one was open for 0% of the time, Pallas kernels for 7%

profile of v10, /device:TPU:6, one launch (start us, length us, event | category | flops | bytes accessed | tf_op | source)
XLA Modules:
  0.0 94.1 jit_solution(12607017814073123464)
XLA Ops:
  0.7 0.8 convert_bitcast_fusion
  1.5 0.1 stack.23.place
  1.6 38.5 %all_gather.3.own = bf16[1024,256]{1,0:T(8,128)(2,1)S(1)} all-gather(bf16[64,256]{1,0:T(8,128)(2,1)S(1)} %convert_bitcast_fusion), channel_id=1, replica_groups={{0,128,256,384,2,130,258,386,4,132,260,388,6,134,262,390},{1,129,257,38..., dimensions={0}, use_global_device_ids=true | all-gather | bytes 557056 | tf_op jit(solution)/shard_map/all_gather | solution.py:336
  40.1 1.9 %collective-permute-start.3 = (bf16[1024,256]{1,0:T(8,128)(2,1)S(1)}, bf16[1024,256]{1,0:T(8,128)(2,1)S(1)}, u32[]{:S(2)}, u32[]{:S(2)}) collective-permute-start(bf16[1024,256]{1,0:T(8,128)(2,1)S(1)} %all_gather.3.own), channel_id=1, source_target_pairs={{0,1},{1,0},{128,129},{129,128},{256,257},{257,256},{384,385},{385... | collective-permute-start | bytes 1572872 | tf_op jit(solution)/shard_map/ppermute | solution.py:45
  42.0 4.9 %collective-permute-start = (bf16[1024,256]{1,0:T(8,128)(2,1)S(1)}, bf16[1024,256]{1,0:T(8,128)(2,1)S(1)}, u32[]{:S(2)}, u32[]{:S(2)}) collective-permute-start(bf16[1024,256]{1,0:T(8,128)(2,1)S(1)} %all_gather.3.own), channel_id=1, source_target_pairs={{0,24},{1,9},{128,152},{129,137},{256,280},{257,265},{384,408},{38... | collective-permute-start | bytes 1572872 | tf_op jit(solution)/shard_map/ppermute | solution.py:41
  47.0 0.0 collective-permute-done.3.other
  47.0 2.7 %collective-permute-start.4 = (bf16[1024,256]{1,0:T(8,128)(2,1)S(1)}, bf16[1024,256]{1,0:T(8,128)(2,1)S(1)}, u32[]{:S(2)}, u32[]{:S(2)}) collective-permute-start(bf16[1024,256]{1,0:T(8,128)(2,1)S(1)} %collective-permute-done.3.other), channel_id=1, source_target_pairs={{0,24},{1,9},{128,152},{129,137},{256,280},{257,265},{384,408},{38... | collective-permute-start | bytes 1572872 | tf_op jit(solution)/shard_map/ppermute | solution.py:41
  49.6 0.9 shard_map.58
  50.5 4.8 %all-to-all-start = ((f32[4,8,128]{2,1,0:T(8,128)}), f32[4,8,128]{2,1,0:T(8,128)S(1)}, u32[]{:S(2)}, u32[]{:S(2)}) async-start(f32[4,8,128]{2,1,0:T(8,128)} %shard_map.58), calls=%async_computation | async-start | bytes 32768 | tf_op jit(solution)/shard_map/all_to_all | solution.py:342
  55.3 2.6 %shard_map.59 = (bf16[8192,256]{1,0:T(8,128)(2,1)}, f32[256,256]{1,0:T(8,128)S(1)}) custom-call(s32[5]{0:T(128)S(1)} %stack.23.place, bf16[1024,256]{1,0:T(8,128)(2,1)S(1)} %all_gather.3.own, bf16[1024,256]{1,0:T(8,128)(2,1)S(1)} %collective-permute-done.3.other, bf16[256,8192]{1,0:T(8,128)(2,1)} %probes.5), custom_call_target="tpu_custom_call" | custom-call | flops 268435456 | bytes 2097152 | tf_op jit(solution)/shard_map/pallas_call | solution.py:228
  57.8 0.7 all-to-all-done.parts
  58.6 0.0 collective-permute-done.own
  58.6 0.7 collective-permute-done.4.other
  59.3 2.9 %shard_map.60 = (bf16[8192,256]{1,0:T(8,128)(2,1)}, f32[256,256]{1,0:T(8,128)S(1)}, f32[8,8,128]{2,1,0:T(8,128)S(1)}, bf16[2048,256]{1,0:T(8,128)(2,1)S(1)}, bf16[256,2048]{1,0:T(8,128)(2,1)S(1)}) custom-call(s32[5]{0:T(128)S(1)} %stack.23.place, bf16[1024,256]{1,0:T(8,128)(2,1)S(1)} %collective-permute-done.own, ...), custom_call_target="tpu_custom_call", output_to_operand_aliasing={{0}: (6, {})} | custom-call | flops 268435456 | bytes 3145728 | tf_op jit(solution)/shard_map/pallas_call | solution.py:246
  62.2 2.0 %collective-permute-start.5 = (bf16[2048,256]{1,0:T(8,128)(2,1)S(1)}, bf16[2048,256]{1,0:T(8,128)(2,1)S(1)}, u32[]{:S(2)}, u32[]{:S(2)}) collective-permute-start(bf16[2048,256]{1,0:T(8,128)(2,1)S(1)} %get-tuple-element.21), channel_id=1, source_target_pairs={{0,1},{1,0},{128,129},{129,128},{256,257},{257,256},{384,385},{385... | collective-permute-start | bytes 3145736 | tf_op jit(solution)/shard_map/ppermute | solution.py:45
  64.2 5.5 %collective-permute-start.1 = (bf16[1024,256]{1,0:T(8,128)(2,1)S(1)}, bf16[1024,256]{1,0:T(8,128)(2,1)S(1)}, u32[]{:S(2)}, u32[]{:S(2)}) collective-permute-start(bf16[1024,256]{1,0:T(8,128)(2,1)S(1)} %collective-permute-done.own), channel_id=1, source_target_pairs={{0,24},{1,9},{128,152},{129,137},{256,280},{257,265},{384,408},{38... | collective-permute-start | bytes 1572872 | tf_op jit(solution)/shard_map/ppermute | solution.py:41
  69.7 6.7 %collective-permute-done.1.own = bf16[1024,256]{1,0:T(8,128)(2,1)S(1)} collective-permute-done((bf16[1024,256]{1,0:T(8,128)(2,1)S(1)}, bf16[1024,256]{1,0:T(8,128)(2,1)S(1)}, u32[]{:S(2)}, u32[]{:S(2)}) %collective-permute-start.1) | collective-permute-done | bytes 524320 | tf_op jit(solution)/shard_map/ppermute | solution.py:41
  76.4 2.0 %collective-permute-start.2 = (bf16[1024,256]{1,0:T(8,128)(2,1)S(1)}, bf16[1024,256]{1,0:T(8,128)(2,1)S(1)}, u32[]{:S(2)}, u32[]{:S(2)}) collective-permute-start(bf16[1024,256]{1,0:T(8,128)(2,1)S(1)} %collective-permute-done.1.own), channel_id=1, source_target_pairs={{0,1},{1,0},{128,129},{129,128},{256,257},{257,256},{384,385},{385... | collective-permute-start | bytes 1572872 | tf_op jit(solution)/shard_map/ppermute | solution.py:45
  78.4 10.2 %all_to_all.10.sums = f32[8,8,128]{2,1,0:T(8,128)S(1)} all-to-all(f32[8,8,128]{2,1,0:T(8,128)S(1)} %get-tuple-element.30), channel_id=1, replica_groups={{0,1,8,9,16,17,24,25},{128,129,136,137,144,145,152,153},{256,257,264,26..., dimensions={0} | all-to-all | bytes 65536 | tf_op jit(solution)/shard_map/all_to_all | solution.py:348
  88.6 0.7 shard_map.63
  89.3 0.0 collective-permute-done.5.block
  89.3 0.0 copy-start
  89.3 2.4 %shard_map.61 = (bf16[8192,256]{1,0:T(8,128)(2,1)}, f32[256,256]{1,0:T(8,128)S(1)}, bf16[256,2048]{1,0:T(8,128)(2,1)S(1)}) custom-call(s32[5]{0:T(128)S(1)} %stack.23.place, bf16[2048,256]{1,0:T(8,128)(2,1)S(1)} %collective-permute-done.5.block, bf16[256,2048]{1,0:T(8,128)(2,1)S(1)} %get-tuple-element.22.cols, ...), custom_call_target="tpu_custom_call", output_to_operand_aliasing={{0}: (5, {})} | custom-call | flops 268435456 | bytes 2097152 | tf_op jit(solution)/shard_map/pallas_call | solution.py:274
  91.7 0.0 collective-permute-done.2.other
  91.7 0.0 copy-done
  91.7 2.3 %shard_map.62 = (bf16[8192,256]{1,0:T(8,128)(2,1)}, bf16[256,256]{1,0:T(8,128)(2,1)}) custom-call(s32[5]{0:T(128)S(1)} %stack.23.place, bf16[1024,256]{1,0:T(8,128)(2,1)S(1)} %collective-permute-done.1.own, bf16[1024,256]{1,0:T(8,128)(2,1)S(1)} %collective-permute-done.2.other, ...), custom_call_target="tpu_custom_call", output_to_operand_aliasing={{0}: (6, {})} | custom-call | flops 268435456 | bytes 1048576 | tf_op jit(solution)/shard_map/pallas_call | solution.py:307
Async XLA Ops:
  40.1 6.8 %collective-permute-start.3 = (bf16[1024,256]{1,0:T(8,128)(2,1)S(1)}, bf16[1024,256]{1,0:T(8,128)(2,1)S(1)}, u32[]{:S(2)}, u32[]{:S(2)}) collective-permute-start(bf16[1024,256]{1,0:T(8,128)(2,1)S(1)} %all_gather.3.own), channel_id=1, source_target_pairs={{0,1},{1,0},{128,129},{129,128},{256,257},{257,256},{384,385},{385... | collective-permute-start | bytes 1572872 | tf_op jit(solution)/shard_map/ppermute | solution.py:45
  42.0 16.5 %collective-permute-start = (bf16[1024,256]{1,0:T(8,128)(2,1)S(1)}, bf16[1024,256]{1,0:T(8,128)(2,1)S(1)}, u32[]{:S(2)}, u32[]{:S(2)}) collective-permute-start(bf16[1024,256]{1,0:T(8,128)(2,1)S(1)} %all_gather.3.own), channel_id=1, source_target_pairs={{0,24},{1,9},{128,152},{129,137},{256,280},{257,265},{384,408},{38... | collective-permute-start | bytes 1572872 | tf_op jit(solution)/shard_map/ppermute | solution.py:41
  47.0 12.3 %collective-permute-start.4 = (bf16[1024,256]{1,0:T(8,128)(2,1)S(1)}, bf16[1024,256]{1,0:T(8,128)(2,1)S(1)}, u32[]{:S(2)}, u32[]{:S(2)}) collective-permute-start(bf16[1024,256]{1,0:T(8,128)(2,1)S(1)} %collective-permute-done.3.other), channel_id=1, source_target_pairs={{0,24},{1,9},{128,152},{129,137},{256,280},{257,265},{384,408},{38... | collective-permute-start | bytes 1572872 | tf_op jit(solution)/shard_map/ppermute | solution.py:41
  50.5 8.1 %all-to-all-start = ((f32[4,8,128]{2,1,0:T(8,128)}), f32[4,8,128]{2,1,0:T(8,128)S(1)}, u32[]{:S(2)}, u32[]{:S(2)}) async-start(f32[4,8,128]{2,1,0:T(8,128)} %shard_map.58), calls=%async_computation | async-start | bytes 32768 | tf_op jit(solution)/shard_map/all_to_all | solution.py:342
  62.2 27.1 %collective-permute-start.5 = (bf16[2048,256]{1,0:T(8,128)(2,1)S(1)}, bf16[2048,256]{1,0:T(8,128)(2,1)S(1)}, u32[]{:S(2)}, u32[]{:S(2)}) collective-permute-start(bf16[2048,256]{1,0:T(8,128)(2,1)S(1)} %get-tuple-element.21), channel_id=1, source_target_pairs={{0,1},{1,0},{128,129},{129,128},{256,257},{257,256},{384,385},{385... | collective-permute-start | bytes 3145736 | tf_op jit(solution)/shard_map/ppermute | solution.py:45
  64.2 12.2 %collective-permute-start.1 = (bf16[1024,256]{1,0:T(8,128)(2,1)S(1)}, bf16[1024,256]{1,0:T(8,128)(2,1)S(1)}, u32[]{:S(2)}, u32[]{:S(2)}) collective-permute-start(bf16[1024,256]{1,0:T(8,128)(2,1)S(1)} %collective-permute-done.own), channel_id=1, source_target_pairs={{0,24},{1,9},{128,152},{129,137},{256,280},{257,265},{384,408},{38... | collective-permute-start | bytes 1572872 | tf_op jit(solution)/shard_map/ppermute | solution.py:41
  76.4 15.3 %collective-permute-start.2 = (bf16[1024,256]{1,0:T(8,128)(2,1)S(1)}, bf16[1024,256]{1,0:T(8,128)(2,1)S(1)}, u32[]{:S(2)}, u32[]{:S(2)}) collective-permute-start(bf16[1024,256]{1,0:T(8,128)(2,1)S(1)} %collective-permute-done.1.own), channel_id=1, source_target_pairs={{0,1},{1,0},{128,129},{129,128},{256,257},{257,256},{384,385},{385... | collective-permute-start | bytes 1572872 | tf_op jit(solution)/shard_map/ppermute | solution.py:45
  89.3 2.4 %copy-start = (f32[256]{0:T(256)S(1)}, f32[256]{0:T(256)}, u32[]{:S(2)}) copy-start(f32[256]{0:T(256)} %param.4) | copy-start | bytes 3076

commit v11 on v8

--- a/solution.py
+++ b/solution.py
@@ -126,8 +126,8 @@
         put.wait()
 
 
-def back_kernel(rows, place, own, other, probes, parts, total_in, _, weight, total, sums, block, *refs):
-    cols, put_sem, get_sem = refs
+def back_kernel(rows, place, own, other, probes, parts, total_in, _, weight, total, totals, block, *refs):
+    cols, sums, put_sem, get_sem, sums_sem = refs
     gets = fetch(place, BACK, probes, cols, get_sem)
     puts = put_rows(place, BACK, own, other, weight, rows, put_sem)
     assemble(place[CORE], own, block, rows)
@@ -142,8 +142,11 @@
     total[...] = total_in[...] + jnp.dot(
         cols[...], block[...], preferred_element_type=jnp.float32
     )
+    out = pltpu.make_async_copy(sums, totals, sums_sem)
+    out.start()
     for put in puts:
         put.wait()
+    out.wait()
 
 
 def ahead_kernel(rows, place, block, probes, total_in, _, weight, total, cols_far, cols, put_sem, get_sem):
@@ -172,14 +175,18 @@
             checksum[at : at + 1, :] = lines[z % 2][z // 2 : z // 2 + 1, :]
 
 
-def last_kernel(rows, place, own, other, cols, total_in, bias, _, weight, keys, block, put_sem):
+def last_kernel(rows, place, own, other, cols, total_in, bias, _, weight, keys, block, made, put_sem, keys_sem):
     puts = put_rows(place, FAR, own, other, weight, rows, put_sem)
     assemble(place[CORE], own, block, rows)
     assemble(1 - place[CORE], other, block, rows)
     total = total_in[...] + jnp.dot(cols[...], block[...], preferred_element_type=jnp.float32)
-    keys[...] = (total + bias[...]).astype(keys.dtype)
-    for put in puts:
+    made[...] = (total + bias[...]).astype(made.dtype)
+    for put in puts[: len(puts) // 2]:
         put.wait()
+    out = pltpu.make_async_copy(made, keys, keys_sem)
+    out.start()
+    for copy in puts[len(puts) // 2 :] + [out]:
+        copy.wait()
 
 
 VMEM = pl.BlockSpec(memory_space=pltpu.VMEM)
@@ -238,6 +245,7 @@
 def back_step(place, own, other, probes, parts, carried):
     rows, span, heads, tokens, width = sizes(own, probes)
     depth = LO * span
+    cols, put_sem, get_sem = near_scratch(tokens, depth)
     return pl.pallas_call(
         functools.partial(back_kernel, rows),
         out_shape=(
@@ -247,8 +255,14 @@
             jax.ShapeDtypeStruct((depth, heads), jnp.bfloat16),
         ),
         in_specs=[SMEM, VMEM, VMEM, HBM, VMEM, VMEM, HBM],
-        out_specs=(HBM, VMEM, VMEM, VMEM),
-        scratch_shapes=near_scratch(tokens, depth),
+        out_specs=(HBM, VMEM, HBM, VMEM),
+        scratch_shapes=[
+            cols,
+            pltpu.VMEM((NY * NC, *parts.shape[1:]), jnp.float32),
+            put_sem,
+            get_sem,
+            pltpu.SemaphoreType.DMA,
+        ],
         input_output_aliases={6: 0},
         compiler_params=LIMIT,
         cost_estimate=cost(2 * depth * heads * tokens, 2 * depth * (heads + tokens)),
@@ -299,8 +313,13 @@
             jax.ShapeDtypeStruct((tokens, heads), jnp.bfloat16),
         ),
         in_specs=[SMEM, VMEM, VMEM, VMEM, VMEM, VMEM, HBM],
-        out_specs=(HBM, VMEM),
-        scratch_shapes=[pltpu.VMEM((depth, heads), jnp.bfloat16), pltpu.SemaphoreType.DMA],
+        out_specs=(HBM, HBM),
+        scratch_shapes=[
+            pltpu.VMEM((depth, heads), jnp.bfloat16),
+            pltpu.VMEM((tokens, heads), jnp.bfloat16),
+            pltpu.SemaphoreType.DMA,
+            pltpu.SemaphoreType.DMA,
+        ],
         input_output_aliases={6: 0},
         compiler_params=SMALL,
         cost_estimate=cost(2 * depth * heads * tokens, 2 * depth * heads),

time: 95.4 us -> 95.3 us (level)
  no operation moved by 1% of the time
where the time goes in v11:
time: 95.3 us; the launch traced here: 94 us
  blocking collectives  48.7 us (51%)
  starting transfers between devices  23.8 us (25%)
  Pallas kernels  11.7 us (12%)
  waiting for transfers between devices  8.09 us (8%)
    all_gather x1, blocking collectives, body(): lax.all_gather(own_rows, AXES, axis=0, tiled=True, axis_index_groups=Z_RI...  38.5 us
    ppermute x3, starting transfers between devices, onward(): return lax.ppermute(value, AXES, ONWARD)  13.1 us
    all_to_all x1, blocking collectives, body(): lax.all_to_all(totals, AXES, split_axis=0, concat_axis=0, tiled=True, axi...  10.2 us
    ppermute x3, waiting for transfers between devices, onward(): return lax.ppermute(value, AXES, ONWARD)  7.38 us
    ppermute x3, starting transfers between devices, swap(): return lax.ppermute(value, AXES, SWAP)  5.91 us
    all_to_all x1, starting transfers between devices, body(): parts = lax.all_to_all(own, 'tp', split_axis=0, concat_axis=0, tiled=True)  4.77 us
    pallas_call x1, Pallas kernels, back_step(): pl.pallas_call(functools.partial(back_kernel, rows), out_shape=(jax.Shape...  2.65 us
    pallas_call x1, Pallas kernels, ahead_step(): pl.pallas_call(functools.partial(ahead_kernel, depth // (NZ * NC)), out_s...  2.61 us
  transfers between devices with their start and end apart: 7, of which 3 were waited for; matrix products, arithmetic and copies ran while one was open for 0% of the time, Pallas kernels for 7%

profile of v11, /device:TPU:6, one launch (start us, length us, event | category | flops | bytes accessed | tf_op | source)
XLA Modules:
  0.0 94.0 jit_solution(11480020897976039294)
XLA Ops:
  0.7 0.8 convert_bitcast_fusion
  1.5 0.1 stack.23.place
  1.6 38.5 %all_gather.3.own = bf16[1024,256]{1,0:T(8,128)(2,1)S(1)} all-gather(bf16[64,256]{1,0:T(8,128)(2,1)S(1)} %convert_bitcast_fusion), channel_id=1, replica_groups={{0,128,256,384,2,130,258,386,4,132,260,388,6,134,262,390},{1,129,257,38..., dimensions={0}, use_global_device_ids=true | all-gather | bytes 557056 | tf_op jit(solution)/shard_map/all_gather | solution.py:338
  40.1 1.9 %collective-permute-start.3 = (bf16[1024,256]{1,0:T(8,128)(2,1)S(1)}, bf16[1024,256]{1,0:T(8,128)(2,1)S(1)}, u32[]{:S(2)}, u32[]{:S(2)}) collective-permute-start(bf16[1024,256]{1,0:T(8,128)(2,1)S(1)} %all_gather.3.own), channel_id=1, source_target_pairs={{0,1},{1,0},{128,129},{129,128},{256,257},{257,256},{384,385},{385... | collective-permute-start | bytes 1572872 | tf_op jit(solution)/shard_map/ppermute | solution.py:45
  42.0 4.9 %collective-permute-start = (bf16[1024,256]{1,0:T(8,128)(2,1)S(1)}, bf16[1024,256]{1,0:T(8,128)(2,1)S(1)}, u32[]{:S(2)}, u32[]{:S(2)}) collective-permute-start(bf16[1024,256]{1,0:T(8,128)(2,1)S(1)} %all_gather.3.own), channel_id=1, source_target_pairs={{0,24},{1,9},{128,152},{129,137},{256,280},{257,265},{384,408},{38... | collective-permute-start | bytes 1572872 | tf_op jit(solution)/shard_map/ppermute | solution.py:41
  47.0 0.0 collective-permute-done.3.other
  47.0 2.7 %collective-permute-start.4 = (bf16[1024,256]{1,0:T(8,128)(2,1)S(1)}, bf16[1024,256]{1,0:T(8,128)(2,1)S(1)}, u32[]{:S(2)}, u32[]{:S(2)}) collective-permute-start(bf16[1024,256]{1,0:T(8,128)(2,1)S(1)} %collective-permute-done.3.other), channel_id=1, source_target_pairs={{0,24},{1,9},{128,152},{129,137},{256,280},{257,265},{384,408},{38... | collective-permute-start | bytes 1572872 | tf_op jit(solution)/shard_map/ppermute | solution.py:41
  49.6 0.9 shard_map.58
  50.5 4.8 %all-to-all-start = ((f32[4,8,128]{2,1,0:T(8,128)}), f32[4,8,128]{2,1,0:T(8,128)S(1)}, u32[]{:S(2)}, u32[]{:S(2)}) async-start(f32[4,8,128]{2,1,0:T(8,128)} %shard_map.58), calls=%async_computation | async-start | bytes 32768 | tf_op jit(solution)/shard_map/all_to_all | solution.py:344
  55.3 2.6 %shard_map.59 = (bf16[8192,256]{1,0:T(8,128)(2,1)}, f32[256,256]{1,0:T(8,128)S(1)}) custom-call(s32[5]{0:T(128)S(1)} %stack.23.place, bf16[1024,256]{1,0:T(8,128)(2,1)S(1)} %all_gather.3.own, bf16[1024,256]{1,0:T(8,128)(2,1)S(1)} %collective-permute-done.3.other, bf16[256,8192]{1,0:T(8,128)(2,1)} %probes.5), custom_call_target="tpu_custom_call" | custom-call | flops 268435456 | bytes 2097152 | tf_op jit(solution)/shard_map/pallas_call | solution.py:231
  57.8 0.7 all-to-all-done.parts
  58.6 0.0 collective-permute-done.own
  58.6 0.7 collective-permute-done.4.other
  59.3 2.6 %shard_map.60 = (bf16[8192,256]{1,0:T(8,128)(2,1)}, f32[256,256]{1,0:T(8,128)S(1)}, f32[8,8,128]{2,1,0:T(8,128)S(1)}, bf16[2048,256]{1,0:T(8,128)(2,1)S(1)}) custom-call(s32[5]{0:T(128)S(1)} %stack.23.place, bf16[1024,256]{1,0:T(8,128)(2,1)S(1)} %collective-permute-done.own, ...), custom_call_target="tpu_custom_call", output_to_operand_aliasing={{0}: (6, {})} | custom-call | flops 268435456 | bytes 2097152 | tf_op jit(solution)/shard_map/pallas_call | solution.py:249
  61.9 2.0 %collective-permute-start.5 = (bf16[2048,256]{1,0:T(8,128)(2,1)S(1)}, bf16[2048,256]{1,0:T(8,128)(2,1)S(1)}, u32[]{:S(2)}, u32[]{:S(2)}) collective-permute-start(bf16[2048,256]{1,0:T(8,128)(2,1)S(1)} %get-tuple-element.20), channel_id=1, source_target_pairs={{0,1},{1,0},{128,129},{129,128},{256,257},{257,256},{384,385},{385... | collective-permute-start | bytes 3145736 | tf_op jit(solution)/shard_map/ppermute | solution.py:45
  63.9 5.5 %collective-permute-start.1 = (bf16[1024,256]{1,0:T(8,128)(2,1)S(1)}, bf16[1024,256]{1,0:T(8,128)(2,1)S(1)}, u32[]{:S(2)}, u32[]{:S(2)}) collective-permute-start(bf16[1024,256]{1,0:T(8,128)(2,1)S(1)} %collective-permute-done.own), channel_id=1, source_target_pairs={{0,24},{1,9},{128,152},{129,137},{256,280},{257,265},{384,408},{38... | collective-permute-start | bytes 1572872 | tf_op jit(solution)/shard_map/ppermute | solution.py:41
  69.4 6.7 %collective-permute-done.1.own = bf16[1024,256]{1,0:T(8,128)(2,1)S(1)} collective-permute-done((bf16[1024,256]{1,0:T(8,128)(2,1)S(1)}, bf16[1024,256]{1,0:T(8,128)(2,1)S(1)}, u32[]{:S(2)}, u32[]{:S(2)}) %collective-permute-start.1) | collective-permute-done | bytes 524320 | tf_op jit(solution)/shard_map/ppermute | solution.py:41
  76.1 2.0 %collective-permute-start.2 = (bf16[1024,256]{1,0:T(8,128)(2,1)S(1)}, bf16[1024,256]{1,0:T(8,128)(2,1)S(1)}, u32[]{:S(2)}, u32[]{:S(2)}) collective-permute-start(bf16[1024,256]{1,0:T(8,128)(2,1)S(1)} %collective-permute-done.1.own), channel_id=1, source_target_pairs={{0,1},{1,0},{128,129},{129,128},{256,257},{257,256},{384,385},{385... | collective-permute-start | bytes 1572872 | tf_op jit(solution)/shard_map/ppermute | solution.py:45
  78.1 10.2 %all_to_all.10.sums = f32[8,8,128]{2,1,0:T(8,128)S(1)} all-to-all(f32[8,8,128]{2,1,0:T(8,128)S(1)} %get-tuple-element.28), channel_id=1, replica_groups={{0,1,8,9,16,17,24,25},{128,129,136,137,144,145,152,153},{256,257,264,26..., dimensions={0} | all-to-all | bytes 65536 | tf_op jit(solution)/shard_map/all_to_all | solution.py:350
  88.4 0.7 shard_map.63
  89.1 0.0 collective-permute-done.5.block
  89.1 0.0 copy-start
  89.1 2.6 %shard_map.61 = (bf16[8192,256]{1,0:T(8,128)(2,1)}, f32[256,256]{1,0:T(8,128)S(1)}, bf16[256,2048]{1,0:T(8,128)(2,1)S(1)}) custom-call(s32[5]{0:T(128)S(1)} %stack.23.place, bf16[2048,256]{1,0:T(8,128)(2,1)S(1)} %collective-permute-done.5.block, bf16[256,8192]{1,0:T(8,128)(2,1)} %probes.5, ...), custom_call_target="tpu_custom_call", output_to_operand_aliasing={{0}: (4, {})} | custom-call | flops 268435456 | bytes 3145728 | tf_op jit(solution)/shard_map/pallas_call | solution.py:275
  91.7 0.0 collective-permute-done.2.other
  91.7 0.0 copy-done
  91.7 2.3 %shard_map.62 = (bf16[8192,256]{1,0:T(8,128)(2,1)}, bf16[256,256]{1,0:T(8,128)(2,1)}) custom-call(s32[5]{0:T(128)S(1)} %stack.23.place, bf16[1024,256]{1,0:T(8,128)(2,1)S(1)} %collective-permute-done.1.own, bf16[1024,256]{1,0:T(8,128)(2,1)S(1)} %collective-permute-done.2.other, ...), custom_call_target="tpu_custom_call", output_to_operand_aliasing={{0}: (6, {})} | custom-call | flops 268435456 | bytes 1048576 | tf_op jit(solution)/shard_map/pallas_call | solution.py:309
Async XLA Ops:
  40.1 6.8 %collective-permute-start.3 = (bf16[1024,256]{1,0:T(8,128)(2,1)S(1)}, bf16[1024,256]{1,0:T(8,128)(2,1)S(1)}, u32[]{:S(2)}, u32[]{:S(2)}) collective-permute-start(bf16[1024,256]{1,0:T(8,128)(2,1)S(1)} %all_gather.3.own), channel_id=1, source_target_pairs={{0,1},{1,0},{128,129},{129,128},{256,257},{257,256},{384,385},{385... | collective-permute-start | bytes 1572872 | tf_op jit(solution)/shard_map/ppermute | solution.py:45
  42.0 16.5 %collective-permute-start = (bf16[1024,256]{1,0:T(8,128)(2,1)S(1)}, bf16[1024,256]{1,0:T(8,128)(2,1)S(1)}, u32[]{:S(2)}, u32[]{:S(2)}) collective-permute-start(bf16[1024,256]{1,0:T(8,128)(2,1)S(1)} %all_gather.3.own), channel_id=1, source_target_pairs={{0,24},{1,9},{128,152},{129,137},{256,280},{257,265},{384,408},{38... | collective-permute-start | bytes 1572872 | tf_op jit(solution)/shard_map/ppermute | solution.py:41
  47.0 12.3 %collective-permute-start.4 = (bf16[1024,256]{1,0:T(8,128)(2,1)S(1)}, bf16[1024,256]{1,0:T(8,128)(2,1)S(1)}, u32[]{:S(2)}, u32[]{:S(2)}) collective-permute-start(bf16[1024,256]{1,0:T(8,128)(2,1)S(1)} %collective-permute-done.3.other), channel_id=1, source_target_pairs={{0,24},{1,9},{128,152},{129,137},{256,280},{257,265},{384,408},{38... | collective-permute-start | bytes 1572872 | tf_op jit(solution)/shard_map/ppermute | solution.py:41
  50.5 8.1 %all-to-all-start = ((f32[4,8,128]{2,1,0:T(8,128)}), f32[4,8,128]{2,1,0:T(8,128)S(1)}, u32[]{:S(2)}, u32[]{:S(2)}) async-start(f32[4,8,128]{2,1,0:T(8,128)} %shard_map.58), calls=%async_computation | async-start | bytes 32768 | tf_op jit(solution)/shard_map/all_to_all | solution.py:344
  61.9 27.1 %collective-permute-start.5 = (bf16[2048,256]{1,0:T(8,128)(2,1)S(1)}, bf16[2048,256]{1,0:T(8,128)(2,1)S(1)}, u32[]{:S(2)}, u32[]{:S(2)}) collective-permute-start(bf16[2048,256]{1,0:T(8,128)(2,1)S(1)} %get-tuple-element.20), channel_id=1, source_target_pairs={{0,1},{1,0},{128,129},{129,128},{256,257},{257,256},{384,385},{385... | collective-permute-start | bytes 3145736 | tf_op jit(solution)/shard_map/ppermute | solution.py:45
  63.9 12.2 %collective-permute-start.1 = (bf16[1024,256]{1,0:T(8,128)(2,1)S(1)}, bf16[1024,256]{1,0:T(8,128)(2,1)S(1)}, u32[]{:S(2)}, u32[]{:S(2)}) collective-permute-start(bf16[1024,256]{1,0:T(8,128)(2,1)S(1)} %collective-permute-done.own), channel_id=1, source_target_pairs={{0,24},{1,9},{128,152},{129,137},{256,280},{257,265},{384,408},{38... | collective-permute-start | bytes 1572872 | tf_op jit(solution)/shard_map/ppermute | solution.py:41
  76.1 15.6 %collective-permute-start.2 = (bf16[1024,256]{1,0:T(8,128)(2,1)S(1)}, bf16[1024,256]{1,0:T(8,128)(2,1)S(1)}, u32[]{:S(2)}, u32[]{:S(2)}) collective-permute-start(bf16[1024,256]{1,0:T(8,128)(2,1)S(1)} %collective-permute-done.1.own), channel_id=1, source_target_pairs={{0,1},{1,0},{128,129},{129,128},{256,257},{257,256},{384,385},{385... | collective-permute-start | bytes 1572872 | tf_op jit(solution)/shard_map/ppermute | solution.py:45
  89.1 2.6 %copy-start = (f32[256]{0:T(256)S(1)}, f32[256]{0:T(256)}, u32[]{:S(2)}) copy-start(f32[256]{0:T(256)} %param.4) | copy-start | bytes 3076
